TPU v7x, 512 devices: a whole 4x4x16 slice. The times are simulated.
512 devices in a mesh: row: 8 (over x, core), col: 16 (over z), gz: 4 (over y).
Axes of the slice: x: 4, y: 4, z: 16, core: 2. Of those that a mesh axis runs over, the one named last changes fastest.
Arguments:
- density_matrix: bfloat16 [8192, 8192], P('row', 'col'), may hold values from -24 to 24
- block_pattern: int32 [128, 128], P('row', 'col'), may hold values from 0 to 1, as said below
- tile_lists: int32 [512, 16], replicated, may hold values from 0 to 127, as said below
- basis_values: bfloat16 [8, 16, 4, 1024, 384], P('row', 'col', 'gz'), may hold values from -0.09375 to 0.09375
- core_density: float32 [16, 128, 96], P('row', 'col', 'gz'), may hold values from 0.5 to 4
- orbitals: float32 [8192, 128], P(('col', 'gz')), may hold values from -6 to 6
Outputs:
- hamiltonian: float32 [8192, 8192], P('row', ('col', 'gz'))
- applied: float32 [8192, 128], P(('row', 'col', 'gz'))
Inputs may be any that keep to these rules, and one draw needn't show every extreme that they name: `block_pattern`: Symmetric, with ones on the diagonal. `tile_lists`: each row is increasing and holds exactly 1 block ids from every run of 8 ids that starts at a multiple of 8.
All inputs are finite; a program needn't handle non-finite values.
Results may differ from a plain program's by a relative error of at most 0.00048.
Values may be sent and summed in bfloat16 or wider, within the bound.
No kernel may reach another device: no remote copies, remote signals or barrier semaphores. Data moves between devices by JAX's collectives and lax.ppermute only.
A program may use at most 64 MiB of HBM per device.

v0:
```python
import jax
import jax.numpy as jnp
from jax import lax
from jax.sharding import PartitionSpec as P

pbe_kappa = 0.804
pbe_mu = 0.2195149727645171
exch_const = 0.75 * (3.0 / 3.141592653589793) ** (1.0 / 3.0)
grad_scale = 4.0 * (3.0 * 3.141592653589793**2) ** (2.0 / 3.0)
density_floor = 0.2
spacing = 0.125


def with_halo(cells, sides, width):
    for axis, dim in sides:
        count = lax.axis_size(axis)
        head = lax.slice_in_dim(cells, 0, width, axis=dim)
        tail = lax.slice_in_dim(cells, cells.shape[dim] - width, cells.shape[dim], axis=dim)
        cells = jnp.concatenate(
            [
                lax.ppermute(tail, axis, [(i, (i + 1) % count) for i in range(count)]),
                cells,
                lax.ppermute(head, axis, [((i + 1) % count, i) for i in range(count)]),
            ],
            axis=dim,
        )
    return cells


def split_up(array, dim, devices):
    lengths = array.shape
    parts = array.reshape(*lengths[:dim], devices, lengths[dim] // devices, *lengths[dim + 1 :])
    return jnp.moveaxis(parts, dim, 0)


def sum_at_owner(array, axis, dim):
    devices = lax.axis_size(axis)
    parts = lax.all_to_all(split_up(array, dim, devices), axis, 0, 0, tiled=True)
    return jnp.sum(parts, axis=0)


def energy(density, grad_square):
    scaled = grad_square / (grad_scale * density ** (8.0 / 3.0))
    enhance = 1.0 + pbe_kappa - pbe_kappa / (1.0 + pbe_mu * scaled / pbe_kappa)
    return -exch_const * density ** (4.0 / 3.0) * enhance


def total_energy(density, grad_square):
    return jnp.sum(energy(density, grad_square))


def centered(grid_values, direction):
    higher = [slice(1, -1), slice(1, -1), slice(1, -1)]
    lesser = [slice(1, -1), slice(1, -1), slice(1, -1)]
    higher[direction] = slice(2, None)
    lesser[direction] = slice(None, -2)
    return (grid_values[tuple(higher)] - grid_values[tuple(lesser)]) / (2.0 * spacing)


def potential_deep(density):
    padded = with_halo(density, (("row", 0), ("col", 1), ("gz", 2)), 2)
    gradients = [centered(padded, direction) for direction in range(3)]
    grad_square = (
        gradients[0] * gradients[0] + gradients[1] * gradients[1] + gradients[2] * gradients[2]
    )
    inner = padded[1:-1, 1:-1, 1:-1]
    first, second = jax.grad(total_energy, argnums=(0, 1))(inner, grad_square)
    divergence = centered(2.0 * second * gradients[0], 0)
    divergence = divergence + centered(2.0 * second * gradients[1], 1)
    divergence = divergence + centered(2.0 * second * gradients[2], 2)
    return first[1:-1, 1:-1, 1:-1] - divergence


def shards(density_matrix, block_pattern, tile_lists, basis_values, core_density, orbitals):
    row_count = lax.axis_size("row")
    column_count = lax.axis_size("col")
    depth_count = lax.axis_size("gz")
    row_index = lax.axis_index("row")
    column_index = lax.axis_index("col")
    depth_index = lax.axis_index("gz")
    row_blocks, column_blocks = block_pattern.shape
    block_size = density_matrix.shape[0] // row_blocks
    listed = tile_lists.shape[1]
    per_row = listed // row_count
    per_column = listed // column_count
    width = listed * block_size
    block_area = block_size * block_size
    slab_lists = tile_lists.reshape(row_count, column_count, depth_count, listed)
    slab_lists = lax.dynamic_index_in_dim(slab_lists, depth_index, axis=2, keepdims=False)
    mine_rows = (
        lax.dynamic_slice_in_dim(slab_lists, row_index * per_row, per_row, 2)
        - row_index * row_blocks
    )
    mine_cols = (
        lax.dynamic_slice_in_dim(slab_lists, column_index * per_column, per_column, 2)
        - column_index * column_blocks
    )
    block_ids = (mine_rows[:, :, :, None] * column_blocks + mine_cols[:, :, None, :]).reshape(-1)
    pattern_flat = block_pattern.reshape(-1)
    stored = density_matrix.reshape(row_blocks, block_size, column_blocks, block_size)
    stored = stored.transpose(0, 2, 1, 3).reshape(row_blocks * column_blocks, block_area)
    stored = stored * pattern_flat.astype(jnp.bfloat16)[:, None]
    outgoing = jnp.take(stored, block_ids, axis=0).reshape(
        row_count, column_count, per_row * per_column, block_area
    )
    flat_out = outgoing.reshape(row_count * column_count, per_row * per_column, block_area)
    incoming = lax.all_to_all(flat_out, ("row", "col"), split_axis=0, concat_axis=0, tiled=True)
    tile_matrix = incoming.reshape(
        row_count, column_count, per_row, per_column, block_size, block_size
    )
    tile_matrix = tile_matrix.transpose(0, 2, 4, 1, 3, 5).reshape(width, width)
    phi_tile = basis_values.reshape(width, -1)
    product = jnp.dot(tile_matrix, phi_tile, preferred_element_type=jnp.float32)
    rho_tile = jnp.sum(phi_tile * product, axis=0).reshape(core_density.shape)
    density = jnp.maximum(rho_tile + core_density, density_floor)
    field = potential_deep(density)
    weighted = (phi_tile * field.reshape(1, -1)).astype(jnp.bfloat16)
    local_ham = lax.dot_general(
        weighted, phi_tile, (((1,), (1,)), ((), ())), preferred_element_type=jnp.float32
    )
    returning = local_ham.reshape(
        row_count, per_row, block_size, column_count, per_column, block_size
    )
    returning = returning.transpose(0, 3, 1, 4, 2, 5).reshape(
        row_count, column_count, per_row * per_column, block_area
    )
    flat_back = returning.reshape(row_count * column_count, per_row * per_column, block_area)
    arrived = lax.all_to_all(flat_back, ("row", "col"), split_axis=0, concat_axis=0, tiled=True)
    owned = jnp.zeros((row_blocks * column_blocks, block_area), jnp.float32)
    owned = owned.at[block_ids].add(arrived.reshape(-1, block_area))
    owned = owned * pattern_flat.astype(jnp.float32)[:, None]
    dense = owned.reshape(row_blocks, column_blocks, block_size, block_size)
    dense = dense.transpose(0, 2, 1, 3).reshape(row_blocks * block_size, column_blocks * block_size)
    share = sum_at_owner(dense, "gz", 1)
    terms = jnp.dot(
        share, orbitals, precision=lax.Precision.HIGHEST, preferred_element_type=jnp.float32
    )
    applied = sum_at_owner(terms, ("col", "gz"), 0)
    return (share, applied)


def solution(mesh):
    placed = (
        P("row", "col"),
        P("row", "col"),
        P(),
        P("row", "col", "gz", None, None),
        P("row", "col", "gz"),
        P(("col", "gz"), None),
    )
    return jax.shard_map(
        shards,
        mesh=mesh,
        in_specs=placed,
        out_specs=(P("row", ("col", "gz")), P(("row", "col", "gz"), None)),
        check_vma=False,
    )
```

profile of v0, /device:TPU:8, one launch (start us, length us, event | category | flops | bytes accessed | tf_op | source)
XLA Modules:
  0.0 511.9 jit_solution(12653079396379790335)
XLA Ops:
  4.1 2.5 subtract_reduce_fusion
  7.2 3.9 reshape.138
  11.1 2.2 copy.68
  13.3 1.7 reshape.139
  15.1 1.8 gather_fusion
  17.0 2.7 gather.7
  19.6 3.7 broadcast_select_fusion
  23.3 116.7 %all_to_all.20 = bf16[128,2,4096]{2,1,0:T(2,128)(2,1)S(1)} all-to-all(bf16[128,2,4096]{2,1,0:T(2,128)(2,1)S(1)} %broadcast_select_fusion), channel_id=1, replica_groups=mesh['row'=8,'col'=16,'gz'=4] {'row','col'}, dimensions={0} | all-to-all | bytes 4194304 | tf_op jit(solution)/shard_map/all_to_all | solution.py:107
  141.3 5.5 %reshape.140 = bf16[8,16,2,1,64,64]{5,4,1,0,2,3:T(8,128)(2,1)} reshape(bf16[128,2,4096]{2,0,1:T(8,128)(2,1)S(1)} %copy.54) | data formatting | bytes 4194304 | tf_op jit(solution)/shard_map/reshape | solution.py:108
  146.8 7.7 %copy.55 = bf16[8,2,64,16,1,64]{5,3,2,1,0,4:T(8,128)(2,1)} copy(bf16[8,2,64,16,1,64]{5,2,3,0,1,4:T(8,128)(2,1)} %bitcast.50) | data formatting | bytes 4194304 | tf_op jit(solution)/shard_map/transpose | solution.py:111
  154.5 5.5 %reshape.141 = bf16[1024,1024]{1,0:T(8,128)(2,1)S(1)} reshape(bf16[8,2,64,16,1,64]{5,3,2,1,0,4:T(8,128)(2,1)} %copy.55) | data formatting | bytes 4194304 | tf_op jit(solution)/shard_map/reshape | solution.py:111
  162.9 2.9 collective-permute-done
  165.8 4.9 collective-permute-start.2
  170.7 2.2 collective-permute-start.3
  172.9 5.6 %collective-permute-done.3 = f32[6,2,24]{2,1,0:T(2,128)S(1)} collective-permute-done((f32[6,2,24]{2,1,0:T(2,128)S(1)}, f32[6,2,24]{2,1,0:T(2,128)S(1)}, u32[]{:S(2)}, u32[]{:S(2)}) %collective-permute-start.3) | collective-permute-done | bytes 1184 | tf_op jit(solution)/shard_map/ppermute | solution.py:23
  178.6 3.5 collective-permute-start.4
  182.1 2.4 collective-permute-start.5
  184.6 3.5 collective-permute-done.5
  188.8 2.4 convolution_bitcast_fusion
  191.2 4.1 copy.65
  195.3 8.5 %reshape.165 = f32[128,2,4096]{2,1,0:T(2,128)} reshape(f32[8,16,2,1,64,64]{5,4,2,1,0,3:T(8,128)} %copy.65) | data formatting | bytes 8388608 | tf_op jit(solution)/shard_map/reshape;reshape | solution.py:127
  203.7 17.4 %all-to-all-start.1 = ((f32[128,2,4096]{2,1,0:T(2,128)}), f32[128,2,4096]{2,1,0:T(2,128)}, u32[]{:S(2)}, u32[]{:S(2)}) async-start(f32[128,2,4096]{2,1,0:T(2,128)} %reshape.165), calls=%async_computation.1 | async-start | bytes 8388608 | tf_op jit(solution)/shard_map/all_to_all | solution.py:128
  221.3 184.1 %all-to-all-done.1 = f32[128,2,4096]{2,1,0:T(2,128)} async-done(((f32[128,2,4096]{2,1,0:T(2,128)}), f32[128,2,4096]{2,1,0:T(2,128)}, u32[]{:S(2)}, u32[]{:S(2)}) %all-to-all-start.1) | async-done | bytes 4194336 | tf_op jit(solution)/shard_map/all_to_all | solution.py:128
  405.5 6.1 %reshape.158 = f32[256,4096]{1,0:T(8,128)} reshape(f32[128,2,4096]{2,1,0:T(2,128)} %all-to-all-done.1) | data formatting | bytes 8388608 | tf_op jit(solution)/shard_map/reshape | solution.py:130
  411.5 8.9 %scatter_custom_fusion = f32[128,4096]{1,0:T(8,128)} fusion(s32[256]{0:T(256)S(1)} %bitcast.61, f32[256,4096]{1,0:T(8,128)} %reshape.158, f32[]{:T(128)} %constant.99.clone.1), kind=kCustom, calls=%fused_computation.8 | custom fusion | flops 1048576 | bytes 2097664 | tf_op jit(solution)/shard_map/scatter-add | solution.py:130
  420.5 1.9 broadcast_multiply_fusion
  422.3 3.0 reshape.145
  425.3 5.6 %copy.59 = f32[16,64,8,64]{1,0,3,2:T(8,128)} copy(f32[16,64,8,64]{3,1,2,0:T(8,128)} %bitcast.51) | data formatting | bytes 4194304 | tf_op jit(solution)/shard_map/transpose | solution.py:133
  431.0 3.5 reshape_reshape.8
  434.5 29.6 %all_to_all.21 = f32[4,1024,128]{1,2,0:T(8,128)} all-to-all(f32[4,1024,128]{1,2,0:T(8,128)S(1)} %bitcast.52), channel_id=1, replica_groups=mesh['row'=8,'col'=16,'gz'=4] {'gz'}, dimensions={0} | all-to-all | bytes 4194304 | tf_op jit(solution)/shard_map/all_to_all | solution.py:38
  464.1 1.8 reduce_sum.28
  466.7 44.4 %all_to_all.22 = f32[64,16,128]{2,1,0:T(8,128)S(1)} all-to-all(f32[64,16,128]{2,1,0:T(8,128)S(1)} %fusion.3), channel_id=1, replica_groups=mesh['row'=8,'col'=16,'gz'=4] {'col','gz'}, dimensions={0} | all-to-all | bytes 1048576 | tf_op jit(solution)/shard_map/all_to_all | solution.py:38
  (47 shorter events, 10.7 us)
Async XLA Ops:
  0.6 465.5 %copy-start = (f32[128,128]{1,0:T(8,128)S(1)}, f32[128,128]{1,0:T(8,128)}, u32[]{:S(2)}) copy-start(f32[128,128]{1,0:T(8,128)} %param.11) | copy-start | bytes 196612
  154.5 5.6 %copy-start.1 = (bf16[1,1,1,1024,384]{4,3,2,1,0:T(8,128)(2,1)S(1)}, bf16[1,1,1,1024,384]{4,3,2,1,0:T(8,128)(2,1)}, u32[]{:S(2)}) copy-start(bf16[1,1,1,1024,384]{4,3,2,1,0:T(8,128)(2,1)} %param.9) | copy-start | bytes 2359300
  160.1 1.4 copy-start.3
  161.5 1.4 collective-permute-start.1
  161.5 4.3 collective-permute-start
  165.8 7.1 %collective-permute-start.2 = (f32[6,2,24]{2,1,0:T(2,128)S(1)}, f32[6,2,24]{2,1,0:T(2,128)S(1)}, u32[]{:S(2)}, u32[]{:S(2)}) collective-permute-start(f32[6,2,24]{2,1,0:T(2,128)S(1)} %get-tuple-element.26), channel_id=1, source_target_pairs={{0,4},{4,8},{8,12},{12,16},{16,20},{20,24},{24,28},{28,32},{32,36}... | collective-permute-start | bytes 3464 | tf_op jit(solution)/shard_map/ppermute | solution.py:21
  170.7 7.8 %collective-permute-start.3 = (f32[6,2,24]{2,1,0:T(2,128)S(1)}, f32[6,2,24]{2,1,0:T(2,128)S(1)}, u32[]{:S(2)}, u32[]{:S(2)}) collective-permute-start(f32[6,2,24]{2,1,0:T(2,128)S(1)} %get-tuple-element.27), channel_id=1, source_target_pairs={{4,0},{8,4},{12,8},{16,12},{20,16},{24,20},{28,24},{32,28},{36,32}... | collective-permute-start | bytes 3464 | tf_op jit(solution)/shard_map/ppermute | solution.py:23
  178.6 6.0 %collective-permute-start.4 = (f32[6,12,2]{2,1,0:T(8,128)S(1)}, f32[6,12,2]{2,1,0:T(8,128)S(1)}, u32[]{:S(2)}, u32[]{:S(2)}) collective-permute-start(f32[6,12,2]{2,1,0:T(8,128)S(1)} %get-tuple-element.24), channel_id=1, source_target_pairs={{0,1},{1,2},{2,3},{3,0},{4,5},{5,6},{6,7},{7,4},{8,9},{9,10},{10,1... | collective-permute-start | bytes 1736 | tf_op jit(solution)/shard_map/ppermute | solution.py:21
  182.1 6.0 %collective-permute-start.5 = (f32[6,12,2]{2,1,0:T(8,128)S(1)}, f32[6,12,2]{2,1,0:T(8,128)S(1)}, u32[]{:S(2)}, u32[]{:S(2)}) collective-permute-start(f32[6,12,2]{2,1,0:T(8,128)S(1)} %get-tuple-element.25), channel_id=1, source_target_pairs={{1,0},{2,1},{3,2},{0,3},{5,4},{6,5},{7,6},{4,7},{9,8},{10,9},{11,1... | collective-permute-start | bytes 1736 | tf_op jit(solution)/shard_map/ppermute | solution.py:23
  203.7 201.7 %all-to-all-start.1 = ((f32[128,2,4096]{2,1,0:T(2,128)}), f32[128,2,4096]{2,1,0:T(2,128)}, u32[]{:S(2)}, u32[]{:S(2)}) async-start(f32[128,2,4096]{2,1,0:T(2,128)} %reshape.165), calls=%async_computation.1 | async-start | bytes 8388608 | tf_op jit(solution)/shard_map/all_to_all | solution.py:128
  466.1 45.6 %copy-start.2 = (f32[1024,128]{1,0:T(8,128)}, f32[1024,128]{1,0:T(8,128)S(1)}, u32[]{:S(2)}) copy-start(f32[1024,128]{1,0:T(8,128)S(1)} %copy.61) | copy-start | bytes 1572868
where the time goes:
time: 522 us; the launch traced here: 512 us
  waiting for transfers between devices  197 us (38%)
  blocking collectives  191 us (37%)
  local copies, waits for them, and re-layouts  65.9 us (13%)
  starting transfers between devices  30.8 us (6%)
  other arithmetic  22 us (4%)
    all_to_all x1, waiting for transfers between devices, shards(): lax.all_to_all(flat_back, ('row', 'col'), split_axis=0, concat_axis=0, ti...  184 us
    all_to_all x1, blocking collectives, shards(): lax.all_to_all(flat_out, ('row', 'col'), split_axis=0, concat_axis=0, til...  117 us
    all_to_all x2, blocking collectives, sum_at_owner(): lax.all_to_all(split_up(array, dim, devices), axis, 0, 0, tiled=True)  74 us
    all_to_all x1, starting transfers between devices, shards(): lax.all_to_all(flat_back, ('row', 'col'), split_axis=0, concat_axis=0, ti...  17.4 us
    another operation x2, local copies, waits for them, and re-layouts, shards(): returning.reshape(row_count * column_count, per_row * per_column, block_a...  12.5 us
  transfers between devices with their start and end apart: 7, of which 6 were waited for; matrix products, arithmetic and copies ran while one was open for 0% of the time, Pallas kernels for 0%

commit v1 on v0

v1 whole, which is shorter than its diff:
```python
import jax
import jax.numpy as jnp
from jax import lax
from jax.experimental import pallas as pl
from jax.experimental.pallas import tpu as pltpu
from jax.sharding import PartitionSpec as P


pbe_kappa = 0.804
pbe_mu = 0.2195149727645171
exch_const = 0.75 * (3.0 / 3.141592653589793) ** (1.0 / 3.0)
grad_scale = 4.0 * (3.0 * 3.141592653589793**2) ** (2.0 / 3.0)
density_floor = 0.2
spacing = 0.125

PLANE = ("row", "col")
BS = 64
PAGES = 20
SCALE_ROWS = 32


def with_halo(cells, sides, width):
    for axis, dim in sides:
        count = lax.axis_size(axis)
        head = lax.slice_in_dim(cells, 0, width, axis=dim)
        tail = lax.slice_in_dim(cells, cells.shape[dim] - width, cells.shape[dim], axis=dim)
        cells = jnp.concatenate(
            [
                lax.ppermute(tail, axis, [(i, (i + 1) % count) for i in range(count)]),
                cells,
                lax.ppermute(head, axis, [((i + 1) % count, i) for i in range(count)]),
            ],
            axis=dim,
        )
    return cells


def energy(density, grad_square):
    scaled = grad_square / (grad_scale * density ** (8.0 / 3.0))
    enhance = 1.0 + pbe_kappa - pbe_kappa / (1.0 + pbe_mu * scaled / pbe_kappa)
    return -exch_const * density ** (4.0 / 3.0) * enhance


def total_energy(density, grad_square):
    return jnp.sum(energy(density, grad_square))


def centered(grid_values, direction):
    higher = [slice(1, -1), slice(1, -1), slice(1, -1)]
    lesser = [slice(1, -1), slice(1, -1), slice(1, -1)]
    higher[direction] = slice(2, None)
    lesser[direction] = slice(None, -2)
    return (grid_values[tuple(higher)] - grid_values[tuple(lesser)]) / (2.0 * spacing)


def potential_deep(density):
    padded = with_halo(density, (("row", 0), ("col", 1), ("gz", 2)), 2)
    gradients = [centered(padded, direction) for direction in range(3)]
    grad_square = (
        gradients[0] * gradients[0] + gradients[1] * gradients[1] + gradients[2] * gradients[2]
    )
    inner = padded[1:-1, 1:-1, 1:-1]
    first, second = jax.grad(total_energy, argnums=(0, 1))(inner, grad_square)
    divergence = centered(2.0 * second * gradients[0], 0)
    divergence = divergence + centered(2.0 * second * gradients[1], 1)
    divergence = divergence + centered(2.0 * second * gradients[2], 2)
    return first[1:-1, 1:-1, 1:-1] - divergence


def listed_pair(ids_ref, lists_ref, t):
    row, col, depth = ids_ref[0], ids_ref[1], ids_ref[2]
    tile = t * 4 + depth
    a0 = lists_ref[2 * row, tile] - 16 * row
    a1 = lists_ref[2 * row + 1, tile] - 16 * row
    b = lists_ref[col, tile] - 8 * col
    return a0, a1, b


def lane_pair(low, high, rows):
    lane = lax.broadcasted_iota(jnp.int32, (rows, 128), 1)
    return jnp.where(lane < BS, low, high)


def pack_kernel(ids_ref, lists_ref, pattern_ref, matrix_ref, out_ref, held):
    def turn(q, carry):
        rows = pl.ds(pl.multiple_of(q * 128, 128), 128)
        for m in range(4):
            block = matrix_ref[rows, 128 * m : 128 * m + 128].T
            for half in range(2):
                b = 2 * m + half
                keep = lane_pair(
                    pattern_ref[b, 2 * q].astype(jnp.float32),
                    pattern_ref[b, 2 * q + 1].astype(jnp.float32),
                    BS,
                ).astype(jnp.bfloat16)
                kept = block[BS * half : BS * half + BS] * keep
                held[0, b, q] = kept
                held[1, b, q] = pltpu.roll(kept, BS, 1)
        return carry

    lax.fori_loop(0, 8, turn, 0)

    def fill(t, carry):
        a0, a1, b = listed_pair(ids_ref, lists_ref, t)
        out_ref[t, :, 0:BS] = held[a0 & 1, b, a0 >> 1, :, 0:BS]
        out_ref[t, :, BS:128] = held[1 - (a1 & 1), b, a1 >> 1, :, BS:128]
        return carry

    lax.fori_loop(0, 128, fill, 0, unroll=4)


def density_kernel(blocks_ref, phi_ref, unit_ref, orbitals_ref, out_ref):
    phi = phi_ref[...]

    def part(n, total):
        rows = pl.ds(pl.multiple_of(n * 128, 128), 128)
        left = jnp.concatenate([blocks_ref[r, rows, :] for r in range(8)], axis=1)
        product = jnp.dot(left, phi, preferred_element_type=jnp.float32)
        return total + jnp.sum(phi_ref[rows, :].astype(jnp.float32) * product, axis=0, keepdims=True)

    out_ref[...] = lax.fori_loop(0, 8, part, jnp.zeros((1, 384), jnp.float32))


def ham_kernel(scale_ref, phi_ref, field_ref, out_ref):
    phi = phi_ref[...]

    def part(r, carry):
        rows = phi_ref[pl.ds(pl.multiple_of(r * 128, 128), 128), :].astype(jnp.float32)
        weighted = (rows * field_ref[...]).astype(jnp.bfloat16)
        block = lax.dot_general(phi, weighted, (((1,), (1,)), ((), ())), preferred_element_type=jnp.float32)
        out_ref[r] = block * scale_ref[0]
        return carry

    lax.fori_loop(0, 8, part, 0)


def coded(page):
    largest = jnp.max(jnp.abs(page), axis=0, keepdims=True)
    power = jnp.floor(jnp.log2(jnp.maximum(largest, 1e-30))) + 1.0
    power = jnp.clip(power, -90.0, 90.0)
    levels = jnp.clip(jnp.round(page * jnp.exp2(15.0 - power)), -32767.0, 32767.0)
    return levels.astype(jnp.int32).astype(jnp.int16), power


def owner_kernel(
    ids_ref, lists_ref, pattern_ref, scale_ref, blocks_ref, orbitals_ref, out_ref, sums, turned, terms, powers
):
    sums[...] = jnp.zeros_like(sums)

    def add(t, carry):
        a0, a1, b = listed_pair(ids_ref, lists_ref, t)
        block = blocks_ref[t]
        sums[a0 & 1, b, a0 >> 1, :, 0:BS] += block[:, 0:BS]
        sums[1 - (a1 & 1), b, a1 >> 1, :, BS:128] += block[:, BS:128]
        return carry

    lax.fori_loop(0, 128, add, 0, unroll=4)
    powers[...] = jnp.zeros_like(powers)

    def finish(q, carry):
        for b in range(8):
            keep = lane_pair(
                pattern_ref[b, 2 * q].astype(jnp.float32), pattern_ref[b, 2 * q + 1].astype(jnp.float32), BS
            )
            page = (sums[0, b, q] + pltpu.roll(sums[1, b, q], BS, 1)) * (keep * scale_ref[0])
            from_here = lax.rem(ids_ref[2] - b // 2 + 4, 4)
            start = pl.multiple_of(128 * from_here + BS * (b % 2), BS)
            turned[pl.ds(start, BS), :] = page
            levels, power = coded(page)
            place = (b % 2) * 8 + q
            out_ref[b // 2, pl.ds(pl.multiple_of(place * BS, BS), BS), :] = levels
            powers[b // 2, pl.ds(place, 1), :] = power
        part = lax.dot_general(
            turned[...],
            orbitals_ref[...].reshape(512, 128),
            (((0,), (0,)), ((), ())),
            precision=lax.Precision.HIGHEST,
            preferred_element_type=jnp.float32,
        )
        for half in range(2):
            for g in range(4):
                start = BS * half + 16 * g
                rows = pl.ds(pl.multiple_of((2 * q + half) * 16, 16), 16)
                terms[g, rows, :] = part[start : start + 16]
        return carry

    lax.fori_loop(0, 8, finish, 0)
    for g in range(4):
        for n in range(4):
            levels, power = coded(terms[g, BS * n : BS * n + BS, :])
            out_ref[g, (16 + n) * BS : (17 + n) * BS, :] = levels
            powers[g, 16 + n : 17 + n, :] = power
        out_ref[g, PAGES * BS : PAGES * BS + SCALE_ROWS, :] = (
            powers[g].astype(jnp.int32).astype(jnp.int16)
        )


def term_kernel(coded_ref, out_ref):
    steps = [
        jnp.exp2(coded_ref[g, PAGES * BS : PAGES * BS + SCALE_ROWS, :].astype(jnp.float32) - 15.0)
        for g in range(4)
    ]
    for n in range(4):
        total = jnp.zeros((BS, 128), jnp.float32)
        for g in range(4):
            levels = coded_ref[g, (16 + n) * BS : (17 + n) * BS, :].astype(jnp.float32)
            total = total + levels * steps[g][16 + n : 17 + n]
        out_ref[BS * n : BS * n + BS, :] = total


def share_kernel(coded_ref, out_ref):
    steps = [
        jnp.exp2(coded_ref[g, PAGES * BS : PAGES * BS + SCALE_ROWS, :].astype(jnp.float32) - 15.0)
        for g in range(4)
    ]
    for q in range(8):
        halves = []
        for half in range(2):
            place = half * 8 + q
            total = jnp.zeros((BS, 128), jnp.float32)
            for g in range(4):
                levels = coded_ref[g, place * BS : place * BS + BS, :].astype(jnp.float32)
                total = total + levels * steps[g][place : place + 1]
            halves.append(total)
        out_ref[128 * q : 128 * q + 128, :] = jnp.concatenate(halves, axis=0).T


smem = pl.BlockSpec(memory_space=pltpu.SMEM)
vmem = pl.BlockSpec(memory_space=pltpu.VMEM)
anywhere = pl.BlockSpec(memory_space=pl.ANY)


def exchange(array, axes):
    return lax.all_to_all(array, axes, 0, 0, tiled=True)


def shards(density_matrix, block_pattern, tile_lists, basis_values, core_density, orbitals):
    ids = jnp.stack([lax.axis_index("row"), lax.axis_index("col"), lax.axis_index("gz")]).astype(jnp.int32)
    lists = tile_lists.T
    pattern = block_pattern.T
    phi = basis_values.reshape(1024, 384)

    outgoing = pl.pallas_call(
        pack_kernel,
        out_shape=jax.ShapeDtypeStruct((128, BS, 128), jnp.bfloat16),
        in_specs=[smem, smem, smem, vmem],
        out_specs=vmem,
        scratch_shapes=[pltpu.VMEM((2, 8, 8, BS, 128), jnp.bfloat16)],
        name="pack",
    )(ids, lists, pattern, density_matrix)
    incoming = exchange(outgoing, PLANE)

    largest = jnp.full((8, 128), jnp.max(jnp.abs(phi)).astype(jnp.float32))
    for axis in PLANE:
        count = lax.axis_size(axis)
        step = 1
        while step < count:
            other = lax.ppermute(largest, axis, [(i, i ^ step) for i in range(count)])
            largest = jnp.maximum(largest, other)
            step *= 2
    columns = [orbitals]
    for step in range(1, 4):
        columns.append(lax.ppermute(orbitals, "gz", [(i, (i + step) % 4) for i in range(4)]))
    all_orbitals = jnp.stack(columns)
    unit = jnp.square(jnp.maximum(largest, 1e-15))[0, 0:1]

    rho = pl.pallas_call(
        density_kernel,
        out_shape=jax.ShapeDtypeStruct((1, 384), jnp.float32),
        in_specs=[vmem, vmem, anywhere, anywhere],
        out_specs=vmem,
        name="density",
    )(incoming.reshape(8, 1024, 128), phi, unit, all_orbitals)
    density = jnp.maximum(rho.reshape(core_density.shape) + core_density, density_floor)
    field = potential_deep(density)

    local_ham = pl.pallas_call(
        ham_kernel,
        out_shape=jax.ShapeDtypeStruct((8, 1024, 128), jnp.float32),
        in_specs=[smem, vmem, vmem],
        out_specs=vmem,
        name="ham",
    )(1.0 / unit, phi, field.reshape(1, -1))
    returning = local_ham.astype(jnp.float16).reshape(128, BS, 128)
    arrived = exchange(returning, PLANE).astype(jnp.float32)

    levels = pl.pallas_call(
        owner_kernel,
        out_shape=jax.ShapeDtypeStruct((4, PAGES * BS + SCALE_ROWS, 128), jnp.int16),
        in_specs=[smem, smem, smem, smem, vmem, vmem],
        out_specs=vmem,
        scratch_shapes=[
            pltpu.VMEM((2, 8, 8, BS, 128), jnp.float32),
            pltpu.VMEM((512, 128), jnp.float32),
            pltpu.VMEM((4, 256, 128), jnp.float32),
            pltpu.VMEM((4, SCALE_ROWS, 128), jnp.float32),
        ],
        name="owner",
    )(ids, lists, pattern, unit, arrived, all_orbitals)
    levels = exchange(levels, "gz")
    terms = pl.pallas_call(
        term_kernel,
        out_shape=jax.ShapeDtypeStruct((256, 128), jnp.float32),
        in_specs=[vmem],
        out_specs=vmem,
        name="terms",
    )(levels)
    applied = jnp.sum(exchange(terms.reshape(16, 16, 128), "col"), axis=0)
    share = pl.pallas_call(
        share_kernel,
        out_shape=jax.ShapeDtypeStruct((1024, 128), jnp.float32),
        in_specs=[vmem],
        out_specs=vmem,
        name="share",
    )(levels)
    return (share, applied)


def solution(mesh):
    placed = (
        P("row", "col"),
        P("row", "col"),
        P(),
        P("row", "col", "gz", None, None),
        P("row", "col", "gz"),
        P(("col", "gz"), None),
    )
    return jax.shard_map(
        shards,
        mesh=mesh,
        in_specs=placed,
        out_specs=(P("row", ("col", "gz")), P(("row", "col", "gz"), None)),
        check_vma=False,
    )
```

time: 522 us -> 368 us (0.70)
  the two profiles are of different devices: /device:TPU:8 before, /device:TPU:32 now
where the time goes in v1:
time: 368 us; the launch traced here: 367 us
  blocking collectives  130 us (35%)
  waiting for transfers between devices  96.8 us (26%)
  starting transfers between devices  91.9 us (25%)
  Pallas kernels  33.6 us (9%)
  other arithmetic  8.91 us (2%)
    all_to_all x2, blocking collectives, exchange(): return lax.all_to_all(array, axes, 0, 0, tiled=True)  130 us
    ppermute x7, waiting for transfers between devices, shards(): other = lax.ppermute(largest, axis, [(i, i ^ step) for i in range(count)])  75.6 us
    ppermute x7, starting transfers between devices, shards(): other = lax.ppermute(largest, axis, [(i, i ^ step) for i in range(count)])  41.1 us
    all_to_all x2, starting transfers between devices, exchange(): return lax.all_to_all(array, axes, 0, 0, tiled=True)  26.5 us
    all_to_all x2, waiting for transfers between devices, exchange(): return lax.all_to_all(array, axes, 0, 0, tiled=True)  11 us
    pallas_call x1, Pallas kernels, shards(): pl.pallas_call(owner_kernel, out_shape=jax.ShapeDtypeStruct((4, PAGES * B...  11 us
    ppermute x3, starting transfers between devices, shards(): lax.ppermute(orbitals, 'gz', [(i, (i + step) % 4) for i in range(4)])  10.9 us
    ppermute x3, starting transfers between devices, with_halo(): lax.ppermute(head, axis, [((i + 1) % count, i) for i in range(count)])  8.72 us
  transfers between devices with their start and end apart: 18, of which 12 were waited for; matrix products, arithmetic and copies ran while one was open for 1% of the time, Pallas kernels for 1%

profile of v1, /device:TPU:32, one launch (start us, length us, event | category | flops | bytes accessed | tf_op | source)
XLA Modules:
  0.0 366.7 jit_solution(3106932657330924789)
XLA Ops:
  1.3 6.5 %pack.1 = bf16[128,64,128]{2,1,0:T(8,128)(2,1)} custom-call(s32[3]{0:T(128)} %pad_add_fusion.ids_ref, s32[16,512]{1,0:T(8,128)} %bitcast.20, s32[8,16]{1,0:T(8,128)} %bitcast.26, bf16[1024,512]{1,0:T(8,128)(2,1)} %matrix_ref.1), custom_call_target="tpu_custom_call" | custom-call | tf_op jit(solution)/shard_map/pack/pallas_call | solution.py:243
  7.8 19.1 %all-to-all-start = ((bf16[128,64,128]{2,1,0:T(8,128)(2,1)}), bf16[128,64,128]{2,1,0:T(8,128)(2,1)S(1)}, u32[]{:S(2)}, u32[]{:S(2)}) async-start(bf16[128,64,128]{2,1,0:T(8,128)(2,1)} %pack.1), calls=%async_computation | async-start | bytes 4194304 | tf_op jit(solution)/shard_map/all_to_all | solution.py:234
  28.3 2.0 collective-permute-start
  31.4 3.5 collective-permute-start.1
  34.9 2.0 collective-permute-done.1
  36.9 5.3 %collective-permute-start.2 = (f32[8,128]{1,0:T(8,128)S(1)}, f32[8,128]{1,0:T(8,128)S(1)}, u32[]{:S(2)}, u32[]{:S(2)}) collective-permute-start(f32[8,128]{1,0:T(8,128)S(1)} %fusion.21), channel_id=1, source_target_pairs={{0,256},{64,320},{128,384},{192,448},{256,0},{320,64},{384,128},{4... | collective-permute-start | bytes 12296 | tf_op jit(solution)/shard_map/ppermute | solution.py:258
  42.2 1.7 collective-permute-done.2
  43.9 2.8 collective-permute-start.3
  46.7 68.3 %collective-permute-done.3 = f32[8,128]{1,0:T(8,128)S(1)} collective-permute-done((f32[8,128]{1,0:T(8,128)S(1)}, f32[8,128]{1,0:T(8,128)S(1)}, u32[]{:S(2)}, u32[]{:S(2)}) %collective-permute-start.3) | collective-permute-done | bytes 4128 | tf_op jit(solution)/shard_map/ppermute | solution.py:258
  115.0 6.1 %collective-permute-start.4 = (f32[8,128]{1,0:T(8,128)S(1)}, f32[8,128]{1,0:T(8,128)S(1)}, u32[]{:S(2)}, u32[]{:S(2)}) collective-permute-start(f32[8,128]{1,0:T(8,128)S(1)} %max.36), channel_id=1, source_target_pairs={{0,8},{4,12},{8,0},{12,4},{16,24},{20,28},{24,16},{28,20},{32,40},... | collective-permute-start | bytes 12296 | tf_op jit(solution)/shard_map/ppermute | solution.py:258
  122.7 8.6 %collective-permute-start.5 = (f32[8,128]{1,0:T(8,128)S(1)}, f32[8,128]{1,0:T(8,128)S(1)}, u32[]{:S(2)}, u32[]{:S(2)}) collective-permute-start(f32[8,128]{1,0:T(8,128)S(1)} %max.37), channel_id=1, source_target_pairs={{0,16},{4,20},{8,24},{12,28},{16,0},{20,4},{24,8},{28,12},{32,48},... | collective-permute-start | bytes 12296 | tf_op jit(solution)/shard_map/ppermute | solution.py:258
  132.9 12.8 %collective-permute-start.6 = (f32[8,128]{1,0:T(8,128)S(1)}, f32[8,128]{1,0:T(8,128)S(1)}, u32[]{:S(2)}, u32[]{:S(2)}) collective-permute-start(f32[8,128]{1,0:T(8,128)S(1)} %max.38), channel_id=1, source_target_pairs={{0,32},{4,36},{8,40},{12,44},{16,48},{20,52},{24,56},{28,60},{32,0... | collective-permute-start | bytes 12296 | tf_op jit(solution)/shard_map/ppermute | solution.py:258
  145.7 3.5 collective-permute-start.7
  149.2 3.6 collective-permute-start.9
  152.8 3.9 %collective-permute-start.8 = (f32[128,128]{1,0:T(8,128)S(1)}, f32[128,128]{1,0:T(8,128)S(1)}, u32[]{:S(2)}, u32[]{:S(2)}) collective-permute-start(f32[128,128]{1,0:T(8,128)S(1)} %copy-done.2), channel_id=1, source_target_pairs={{0,2},{1,3},{2,0},{3,1},{4,6},{5,7},{6,4},{7,5},{8,10},{9,11},{10,... | collective-permute-start | bytes 196616 | tf_op jit(solution)/shard_map/ppermute | solution.py:263
  157.2 3.2 collective-permute-done.8
  162.5 5.4 %density.1 = f32[1,384]{1,0:T(1,128)} custom-call(bf16[8,1024,128]{2,1,0:T(8,128)(2,1)} %bitcast.16, bf16[1024,384]{1,0:T(8,128)(2,1)} %bitcast.17, f32[1]{0:T(128)} %bitcast.6.unit_ref.scale_ref, f32[4,128,128]{2,1,0:T(8,128)} %pad_maximum_fusion.orbitals_ref), custom_call_target="tpu_custom_call" | custom-call | tf_op jit(solution)/shard_map/density/pallas_call | solution.py:267
  170.1 3.4 collective-permute-done.10
  173.5 1.9 collective-permute-start.12
  175.4 3.9 %collective-permute-start.13 = (f32[6,2,24]{2,1,0:T(2,128)S(1)}, f32[6,2,24]{2,1,0:T(2,128)S(1)}, u32[]{:S(2)}, u32[]{:S(2)}) collective-permute-start(f32[6,2,24]{2,1,0:T(2,128)S(1)} %get-tuple-element.19), channel_id=1, source_target_pairs={{4,0},{8,4},{12,8},{16,12},{20,16},{24,20},{28,24},{32,28},{36,32}... | collective-permute-start | bytes 3464 | tf_op jit(solution)/shard_map/ppermute | solution.py:31
  181.1 2.3 collective-permute-start.14
  183.3 4.8 %collective-permute-start.15 = (f32[6,12,2]{2,1,0:T(8,128)S(1)}, f32[6,12,2]{2,1,0:T(8,128)S(1)}, u32[]{:S(2)}, u32[]{:S(2)}) collective-permute-start(f32[6,12,2]{2,1,0:T(8,128)S(1)} %get-tuple-element.17), channel_id=1, source_target_pairs={{1,0},{2,1},{3,2},{0,3},{5,4},{6,5},{7,6},{4,7},{9,8},{10,9},{11,1... | collective-permute-start | bytes 1736 | tf_op jit(solution)/shard_map/ppermute | solution.py:31
  191.0 6.3 %ham.1 = f32[8,1024,128]{2,1,0:T(8,128)} custom-call(f32[1]{0:T(128)S(6)} %div.38.scale_ref, bf16[1024,384]{1,0:T(8,128)(2,1)} %bitcast.18, f32[1,384]{1,0:T(1,128)} %reshape.25.field_ref), custom_call_target="tpu_custom_call" | custom-call | tf_op jit(solution)/shard_map/ham/pallas_call | solution.py:277
  197.3 2.5 convert_element_type.10
  199.8 106.5 %all_to_all.20 = f16[128,64,128]{2,1,0:T(8,128)(2,1)S(1)} all-to-all(f16[128,64,128]{2,1,0:T(8,128)(2,1)S(1)} %bitcast.15), channel_id=1, replica_groups=mesh['row'=8,'col'=16,'gz'=4] {'row','col'}, dimensions={0} | all-to-all | bytes 4194304 | tf_op jit(solution)/shard_map/all_to_all | solution.py:234
  306.3 2.4 convert_element_type.11.blocks_ref
  308.7 11.0 %owner.1 = s16[4,1312,128]{2,1,0:T(8,128)(2,1)} custom-call(s32[3]{0:T(128)} %pad_add_fusion.ids_ref, s32[16,512]{1,0:T(8,128)} %bitcast.21, s32[8,16]{1,0:T(8,128)} %bitcast.27, f32[1]{0:T(128)} %bitcast.6.unit_ref.scale_ref, f32[128,64,128]{2,1,0:T(8,128)} %convert_element_type.11.blocks_ref, f32[4,128,128]{2,1,0:T(8,128)} %pad_maximum_fusion.orbitals_ref), custom_call_target="tpu_custom_call" | custom-call | tf_op jit(solution)/shard_map/owner/pallas_call | solution.py:287
  319.7 23.6 %all_to_all.21.coded_ref = s16[4,1312,128]{2,1,0:T(8,128)(2,1)} all-to-all(s16[4,1312,128]{2,1,0:T(8,128)(2,1)} %owner.1), channel_id=1, replica_groups=mesh['row'=8,'col'=16,'gz'=4] {'gz'}, dimensions={0} | all-to-all | bytes 2686976 | tf_op jit(solution)/shard_map/all_to_all | solution.py:234
  343.2 2.0 terms.1
  345.3 7.4 %all-to-all-start.3 = ((f32[16,16,128]{2,1,0:T(8,128)}), f32[16,16,128]{2,1,0:T(8,128)S(1)}, u32[]{:S(2)}, u32[]{:S(2)}) async-start(f32[16,16,128]{2,1,0:T(8,128)} %bitcast.19), calls=%async_computation.3 | async-start | bytes 262144 | tf_op jit(solution)/shard_map/all_to_all | solution.py:234
  352.7 2.5 share.1
  355.1 11.0 %all-to-all-done.3 = f32[16,16,128]{2,1,0:T(8,128)S(1)} async-done(((f32[16,16,128]{2,1,0:T(8,128)}), f32[16,16,128]{2,1,0:T(8,128)S(1)}, u32[]{:S(2)}, u32[]{:S(2)}) %all-to-all-start.3) | async-done | bytes 131104 | tf_op jit(solution)/shard_map/all_to_all | solution.py:234
  (46 shorter events, 14.9 us)
Async XLA Ops:
  7.8 19.1 %copy-start.1 = (bf16[1,1,1,1024,384]{4,3,2,1,0:T(8,128)(2,1)S(1)}, bf16[1,1,1,1024,384]{4,3,2,1,0:T(8,128)(2,1)}, u32[]{:S(2)}) copy-start(bf16[1,1,1,1024,384]{4,3,2,1,0:T(8,128)(2,1)} %param.9) | copy-start | bytes 2359300
  7.8 137.9 %copy-start.2 = (f32[128,128]{1,0:T(8,128)S(1)}, f32[128,128]{1,0:T(8,128)}, u32[]{:S(2)}) copy-start(f32[128,128]{1,0:T(8,128)} %param.11) | copy-start | bytes 196612
  7.8 153.4 %all-to-all-start = ((bf16[128,64,128]{2,1,0:T(8,128)(2,1)}), bf16[128,64,128]{2,1,0:T(8,128)(2,1)S(1)}, u32[]{:S(2)}, u32[]{:S(2)}) async-start(bf16[128,64,128]{2,1,0:T(8,128)(2,1)} %pack.1), calls=%async_computation | async-start | bytes 4194304 | tf_op jit(solution)/shard_map/all_to_all | solution.py:234
  27.0 141.7 %copy-start.3 = (f32[2,8,24]{2,1,0:T(8,128)S(1)}, f32[2,8,24]{2,1,0:T(8,128)}, u32[]{:S(2)}) copy-start(f32[2,8,24]{2,1,0:T(8,128)} %param.10) | copy-start | bytes 4612
  28.3 3.1 collective-permute-start
  31.4 5.5 %collective-permute-start.1 = (f32[8,128]{1,0:T(8,128)S(1)}, f32[8,128]{1,0:T(8,128)S(1)}, u32[]{:S(2)}, u32[]{:S(2)}) collective-permute-start(f32[8,128]{1,0:T(8,128)S(1)} %broadcast_maximum_fusion), channel_id=1, source_target_pairs={{0,128},{64,192},{128,0},{192,64},{256,384},{320,448},{384,256},{4... | collective-permute-start | bytes 12296 | tf_op jit(solution)/shard_map/ppermute | solution.py:258
  36.9 7.0 %collective-permute-start.2 = (f32[8,128]{1,0:T(8,128)S(1)}, f32[8,128]{1,0:T(8,128)S(1)}, u32[]{:S(2)}, u32[]{:S(2)}) collective-permute-start(f32[8,128]{1,0:T(8,128)S(1)} %fusion.21), channel_id=1, source_target_pairs={{0,256},{64,320},{128,384},{192,448},{256,0},{320,64},{384,128},{4... | collective-permute-start | bytes 12296 | tf_op jit(solution)/shard_map/ppermute | solution.py:258
  43.9 71.1 %collective-permute-start.3 = (f32[8,128]{1,0:T(8,128)S(1)}, f32[8,128]{1,0:T(8,128)S(1)}, u32[]{:S(2)}, u32[]{:S(2)}) collective-permute-start(f32[8,128]{1,0:T(8,128)S(1)} %max.35), channel_id=1, source_target_pairs={{0,4},{4,0},{8,12},{12,8},{16,20},{20,16},{24,28},{28,24},{32,36},... | collective-permute-start | bytes 12296 | tf_op jit(solution)/shard_map/ppermute | solution.py:258
  115.0 7.7 %collective-permute-start.4 = (f32[8,128]{1,0:T(8,128)S(1)}, f32[8,128]{1,0:T(8,128)S(1)}, u32[]{:S(2)}, u32[]{:S(2)}) collective-permute-start(f32[8,128]{1,0:T(8,128)S(1)} %max.36), channel_id=1, source_target_pairs={{0,8},{4,12},{8,0},{12,4},{16,24},{20,28},{24,16},{28,20},{32,40},... | collective-permute-start | bytes 12296 | tf_op jit(solution)/shard_map/ppermute | solution.py:258
  122.7 10.2 %collective-permute-start.5 = (f32[8,128]{1,0:T(8,128)S(1)}, f32[8,128]{1,0:T(8,128)S(1)}, u32[]{:S(2)}, u32[]{:S(2)}) collective-permute-start(f32[8,128]{1,0:T(8,128)S(1)} %max.37), channel_id=1, source_target_pairs={{0,16},{4,20},{8,24},{12,28},{16,0},{20,4},{24,8},{28,12},{32,48},... | collective-permute-start | bytes 12296 | tf_op jit(solution)/shard_map/ppermute | solution.py:258
  132.9 23.8 %collective-permute-start.6 = (f32[8,128]{1,0:T(8,128)S(1)}, f32[8,128]{1,0:T(8,128)S(1)}, u32[]{:S(2)}, u32[]{:S(2)}) collective-permute-start(f32[8,128]{1,0:T(8,128)S(1)} %max.38), channel_id=1, source_target_pairs={{0,32},{4,36},{8,40},{12,44},{16,48},{20,52},{24,56},{28,60},{32,0... | collective-permute-start | bytes 12296 | tf_op jit(solution)/shard_map/ppermute | solution.py:258
  145.7 11.5 %collective-permute-start.7 = (f32[128,128]{1,0:T(8,128)S(1)}, f32[128,128]{1,0:T(8,128)S(1)}, u32[]{:S(2)}, u32[]{:S(2)}) collective-permute-start(f32[128,128]{1,0:T(8,128)S(1)} %copy-done.2), channel_id=1, source_target_pairs={{0,1},{1,2},{2,3},{3,0},{4,5},{5,6},{6,7},{7,4},{8,9},{9,10},{10,1... | collective-permute-start | bytes 196616 | tf_op jit(solution)/shard_map/ppermute | solution.py:263
  149.2 8.0 %collective-permute-start.9 = (f32[128,128]{1,0:T(8,128)S(1)}, f32[128,128]{1,0:T(8,128)S(1)}, u32[]{:S(2)}, u32[]{:S(2)}) collective-permute-start(f32[128,128]{1,0:T(8,128)S(1)} %copy-done.2), channel_id=1, source_target_pairs={{0,3},{1,0},{2,1},{3,2},{4,7},{5,4},{6,5},{7,6},{8,11},{9,8},{10,9... | collective-permute-start | bytes 196616 | tf_op jit(solution)/shard_map/ppermute | solution.py:263
  152.8 7.7 %collective-permute-start.8 = (f32[128,128]{1,0:T(8,128)S(1)}, f32[128,128]{1,0:T(8,128)S(1)}, u32[]{:S(2)}, u32[]{:S(2)}) collective-permute-start(f32[128,128]{1,0:T(8,128)S(1)} %copy-done.2), channel_id=1, source_target_pairs={{0,2},{1,3},{2,0},{3,1},{4,6},{5,7},{6,4},{7,5},{8,10},{9,11},{10,... | collective-permute-start | bytes 196616 | tf_op jit(solution)/shard_map/ppermute | solution.py:263
  161.2 1.3 copy-start
  168.7 1.4 collective-permute-start.11
  168.7 4.8 %collective-permute-start.10 = (f32[2,8,24]{2,1,0:T(8,128)S(1)}, f32[2,8,24]{2,1,0:T(8,128)S(1)}, u32[]{:S(2)}, u32[]{:S(2)}) collective-permute-start(f32[2,8,24]{2,1,0:T(8,128)S(1)} %add_maximum_fusion), channel_id=1, source_target_pairs={{0,64},{64,128},{128,192},{192,256},{256,320},{320,384},{384,448},... | collective-permute-start | bytes 4616 | tf_op jit(solution)/shard_map/ppermute | solution.py:29
  173.5 5.9 %collective-permute-start.12 = (f32[6,2,24]{2,1,0:T(2,128)S(1)}, f32[6,2,24]{2,1,0:T(2,128)S(1)}, u32[]{:S(2)}, u32[]{:S(2)}) collective-permute-start(f32[6,2,24]{2,1,0:T(2,128)S(1)} %get-tuple-element.18), channel_id=1, source_target_pairs={{0,4},{4,8},{8,12},{12,16},{16,20},{20,24},{24,28},{28,32},{32,36}... | collective-permute-start | bytes 3464 | tf_op jit(solution)/shard_map/ppermute | solution.py:29
  175.4 5.5 %collective-permute-start.13 = (f32[6,2,24]{2,1,0:T(2,128)S(1)}, f32[6,2,24]{2,1,0:T(2,128)S(1)}, u32[]{:S(2)}, u32[]{:S(2)}) collective-permute-start(f32[6,2,24]{2,1,0:T(2,128)S(1)} %get-tuple-element.19), channel_id=1, source_target_pairs={{4,0},{8,4},{12,8},{16,12},{20,16},{24,20},{28,24},{32,28},{36,32}... | collective-permute-start | bytes 3464 | tf_op jit(solution)/shard_map/ppermute | solution.py:31
  181.1 7.7 %collective-permute-start.14 = (f32[6,12,2]{2,1,0:T(8,128)S(1)}, f32[6,12,2]{2,1,0:T(8,128)S(1)}, u32[]{:S(2)}, u32[]{:S(2)}) collective-permute-start(f32[6,12,2]{2,1,0:T(8,128)S(1)} %get-tuple-element.16), channel_id=1, source_target_pairs={{0,1},{1,2},{2,3},{3,0},{4,5},{5,6},{6,7},{7,4},{8,9},{9,10},{10,1... | collective-permute-start | bytes 1736 | tf_op jit(solution)/shard_map/ppermute | solution.py:29
  183.3 6.5 %collective-permute-start.15 = (f32[6,12,2]{2,1,0:T(8,128)S(1)}, f32[6,12,2]{2,1,0:T(8,128)S(1)}, u32[]{:S(2)}, u32[]{:S(2)}) collective-permute-start(f32[6,12,2]{2,1,0:T(8,128)S(1)} %get-tuple-element.17), channel_id=1, source_target_pairs={{1,0},{2,1},{3,2},{0,3},{5,4},{6,5},{7,6},{4,7},{9,8},{10,9},{11,1... | collective-permute-start | bytes 1736 | tf_op jit(solution)/shard_map/ppermute | solution.py:31
  345.3 20.8 %all-to-all-start.3 = ((f32[16,16,128]{2,1,0:T(8,128)}), f32[16,16,128]{2,1,0:T(8,128)S(1)}, u32[]{:S(2)}, u32[]{:S(2)}) async-start(f32[16,16,128]{2,1,0:T(8,128)} %bitcast.19), calls=%async_computation.3 | async-start | bytes 262144 | tf_op jit(solution)/shard_map/all_to_all | solution.py:234

commit v2 on v1

--- a/solution.py
+++ b/solution.py
@@ -13,10 +13,12 @@
 density_floor = 0.2
 spacing = 0.125
 
+
 PLANE = ("row", "col")
 BS = 64
-PAGES = 20
-SCALE_ROWS = 32
+MIB = 1024 * 1024
+PAGES = 16
+SCALES = 16
 
 
 def with_halo(cells, sides, width):
@@ -143,7 +145,20 @@
 
 
 def owner_kernel(
-    ids_ref, lists_ref, pattern_ref, scale_ref, blocks_ref, orbitals_ref, out_ref, sums, turned, terms, powers
+    ids_ref,
+    lists_ref,
+    pattern_ref,
+    scale_ref,
+    blocks_ref,
+    orbitals_ref,
+    terms_ref,
+    out0_ref,
+    out1_ref,
+    out2_ref,
+    out3_ref,
+    sums,
+    turned,
+    powers,
 ):
     sums[...] = jnp.zeros_like(sums)
 
@@ -155,21 +170,24 @@
         return carry
 
     lax.fori_loop(0, 128, add, 0, unroll=4)
-    powers[...] = jnp.zeros_like(powers)
+    unit = scale_ref[0]
+    outs = (out0_ref, out1_ref, out2_ref, out3_ref)
 
     def finish(q, carry):
-        for b in range(8):
-            keep = lane_pair(
-                pattern_ref[b, 2 * q].astype(jnp.float32), pattern_ref[b, 2 * q + 1].astype(jnp.float32), BS
-            )
-            page = (sums[0, b, q] + pltpu.roll(sums[1, b, q], BS, 1)) * (keep * scale_ref[0])
-            from_here = lax.rem(ids_ref[2] - b // 2 + 4, 4)
-            start = pl.multiple_of(128 * from_here + BS * (b % 2), BS)
-            turned[pl.ds(start, BS), :] = page
-            levels, power = coded(page)
-            place = (b % 2) * 8 + q
-            out_ref[b // 2, pl.ds(pl.multiple_of(place * BS, BS), BS), :] = levels
-            powers[b // 2, pl.ds(place, 1), :] = power
+        for n, out in enumerate(outs):
+            peer = lax.rem(ids_ref[2] + n, 4)
+            for half in range(2):
+                b = 2 * peer + half
+                keep = lane_pair(
+                    pattern_ref[b, 2 * q].astype(jnp.float32), pattern_ref[b, 2 * q + 1].astype(jnp.float32), BS
+                )
+                page = (sums[0, b, q] + pltpu.roll(sums[1, b, q], BS, 1)) * (keep * unit)
+                place = 2 * n + half
+                turned[BS * place : BS * place + BS, :] = page
+                levels, power = coded(page)
+                place = half * 8 + q
+                out[pl.ds(pl.multiple_of(place * BS, BS), BS), :] = levels
+                powers[n, pl.ds(place, 1), :] = power
         part = lax.dot_general(
             turned[...],
             orbitals_ref[...].reshape(512, 128),
@@ -178,49 +196,37 @@
             preferred_element_type=jnp.float32,
         )
         for half in range(2):
-            for g in range(4):
-                start = BS * half + 16 * g
-                rows = pl.ds(pl.multiple_of((2 * q + half) * 16, 16), 16)
-                terms[g, rows, :] = part[start : start + 16]
+            levels, power = coded(part[BS * half : BS * half + BS])
+            terms_ref[2 * q + half, 0:BS, :] = levels
+            terms_ref[2 * q + half, BS : BS + 8, :] = (
+                jnp.broadcast_to(power, (8, 128)).astype(jnp.int32).astype(jnp.int16)
+            )
         return carry
 
     lax.fori_loop(0, 8, finish, 0)
-    for g in range(4):
-        for n in range(4):
-            levels, power = coded(terms[g, BS * n : BS * n + BS, :])
-            out_ref[g, (16 + n) * BS : (17 + n) * BS, :] = levels
-            powers[g, 16 + n : 17 + n, :] = power
-        out_ref[g, PAGES * BS : PAGES * BS + SCALE_ROWS, :] = (
-            powers[g].astype(jnp.int32).astype(jnp.int16)
-        )
+    for n, out in enumerate(outs):
+        out[PAGES * BS : PAGES * BS + SCALES, :] = powers[n].astype(jnp.int32).astype(jnp.int16)
 
 
 def term_kernel(coded_ref, out_ref):
-    steps = [
-        jnp.exp2(coded_ref[g, PAGES * BS : PAGES * BS + SCALE_ROWS, :].astype(jnp.float32) - 15.0)
-        for g in range(4)
-    ]
-    for n in range(4):
-        total = jnp.zeros((BS, 128), jnp.float32)
-        for g in range(4):
-            levels = coded_ref[g, (16 + n) * BS : (17 + n) * BS, :].astype(jnp.float32)
-            total = total + levels * steps[g][16 + n : 17 + n]
-        out_ref[BS * n : BS * n + BS, :] = total
-
-
-def share_kernel(coded_ref, out_ref):
-    steps = [
-        jnp.exp2(coded_ref[g, PAGES * BS : PAGES * BS + SCALE_ROWS, :].astype(jnp.float32) - 15.0)
-        for g in range(4)
-    ]
+    total = jnp.zeros((BS, 128), jnp.float32)
+    for c in range(16):
+        step = jnp.exp2(coded_ref[c, BS : BS + 8, :].astype(jnp.float32)[0:1] - 15.0)
+        total = total + coded_ref[c, 0:BS, :].astype(jnp.float32) * step
+    out_ref[...] = total
+
+
+def share_kernel(coded0_ref, coded1_ref, coded2_ref, coded3_ref, out_ref):
+    parts = (coded0_ref, coded1_ref, coded2_ref, coded3_ref)
+    steps = [jnp.exp2(part[PAGES * BS : PAGES * BS + SCALES, :].astype(jnp.float32) - 15.0) for part in parts]
     for q in range(8):
         halves = []
         for half in range(2):
             place = half * 8 + q
             total = jnp.zeros((BS, 128), jnp.float32)
-            for g in range(4):
-                levels = coded_ref[g, place * BS : place * BS + BS, :].astype(jnp.float32)
-                total = total + levels * steps[g][place : place + 1]
+            for part, step in zip(parts, steps):
+                levels = part[place * BS : place * BS + BS, :].astype(jnp.float32)
+                total = total + levels * step[place : place + 1]
             halves.append(total)
         out_ref[128 * q : 128 * q + 128, :] = jnp.concatenate(halves, axis=0).T
 
@@ -251,16 +257,17 @@
     incoming = exchange(outgoing, PLANE)
 
     largest = jnp.full((8, 128), jnp.max(jnp.abs(phi)).astype(jnp.float32))
-    for axis in PLANE:
-        count = lax.axis_size(axis)
-        step = 1
-        while step < count:
-            other = lax.ppermute(largest, axis, [(i, i ^ step) for i in range(count)])
-            largest = jnp.maximum(largest, other)
-            step *= 2
+    for step in (1, 2, 4):
+        other = lax.ppermute(largest, "row", [(i, i ^ step) for i in range(8)])
+        largest = jnp.maximum(largest, other)
+    others = []
+    for step in range(1, 16):
+        others.append(lax.ppermute(largest, "col", [(i, i ^ step) for i in range(16)]))
+    for other in others:
+        largest = jnp.maximum(largest, other)
     columns = [orbitals]
     for step in range(1, 4):
-        columns.append(lax.ppermute(orbitals, "gz", [(i, (i + step) % 4) for i in range(4)]))
+        columns.append(lax.ppermute(orbitals, "gz", [(i, (i - step) % 4) for i in range(4)]))
     all_orbitals = jnp.stack(columns)
     unit = jnp.square(jnp.maximum(largest, 1e-15))[0, 0:1]
 
@@ -269,6 +276,7 @@
         out_shape=jax.ShapeDtypeStruct((1, 384), jnp.float32),
         in_specs=[vmem, vmem, anywhere, anywhere],
         out_specs=vmem,
+        compiler_params=pltpu.CompilerParams(vmem_limit_bytes=12 * MIB),
         name="density",
     )(incoming.reshape(8, 1024, 128), phi, unit, all_orbitals)
     density = jnp.maximum(rho.reshape(core_density.shape) + core_density, density_floor)
@@ -279,40 +287,46 @@
         out_shape=jax.ShapeDtypeStruct((8, 1024, 128), jnp.float32),
         in_specs=[smem, vmem, vmem],
         out_specs=vmem,
+        compiler_params=pltpu.CompilerParams(vmem_limit_bytes=16 * MIB),
         name="ham",
     )(1.0 / unit, phi, field.reshape(1, -1))
     returning = local_ham.astype(jnp.float16).reshape(128, BS, 128)
     arrived = exchange(returning, PLANE).astype(jnp.float32)
 
-    levels = pl.pallas_call(
+    page_shape = jax.ShapeDtypeStruct((PAGES * BS + SCALES, 128), jnp.int16)
+    terms, *pages = pl.pallas_call(
         owner_kernel,
-        out_shape=jax.ShapeDtypeStruct((4, PAGES * BS + SCALE_ROWS, 128), jnp.int16),
+        out_shape=[jax.ShapeDtypeStruct((16, BS + 8, 128), jnp.int16)] + [page_shape] * 4,
         in_specs=[smem, smem, smem, smem, vmem, vmem],
-        out_specs=vmem,
+        out_specs=[vmem] * 5,
         scratch_shapes=[
             pltpu.VMEM((2, 8, 8, BS, 128), jnp.float32),
             pltpu.VMEM((512, 128), jnp.float32),
-            pltpu.VMEM((4, 256, 128), jnp.float32),
-            pltpu.VMEM((4, SCALE_ROWS, 128), jnp.float32),
+            pltpu.VMEM((4, SCALES, 128), jnp.float32),
         ],
+        compiler_params=pltpu.CompilerParams(vmem_limit_bytes=24 * MIB),
         name="owner",
     )(ids, lists, pattern, unit, arrived, all_orbitals)
-    levels = exchange(levels, "gz")
-    terms = pl.pallas_call(
-        term_kernel,
-        out_shape=jax.ShapeDtypeStruct((256, 128), jnp.float32),
-        in_specs=[vmem],
-        out_specs=vmem,
-        name="terms",
-    )(levels)
-    applied = jnp.sum(exchange(terms.reshape(16, 16, 128), "col"), axis=0)
+    terms = exchange(terms, "col")
+    for step in range(1, 4):
+        pages[step] = lax.ppermute(pages[step], "gz", [(i, (i + step) % 4) for i in range(4)])
     share = pl.pallas_call(
         share_kernel,
         out_shape=jax.ShapeDtypeStruct((1024, 128), jnp.float32),
+        in_specs=[vmem] * 4,
+        out_specs=vmem,
+        compiler_params=pltpu.CompilerParams(vmem_limit_bytes=8 * MIB),
+        name="share",
+    )(*pages)
+    sums = pl.pallas_call(
+        term_kernel,
+        out_shape=jax.ShapeDtypeStruct((BS, 128), jnp.float32),
         in_specs=[vmem],
         out_specs=vmem,
-        name="share",
-    )(levels)
+        compiler_params=pltpu.CompilerParams(vmem_limit_bytes=4 * MIB),
+        name="sums",
+    )(terms)
+    applied = jnp.sum(exchange(sums.reshape(4, 16, 128), "gz"), axis=0)
     return (share, applied)
 
 

time: 368 us -> 377 us (1.024)
  starting transfers between devices: 91.9 us -> 164 us
  waiting for transfers between devices: 96.8 us -> 71.4 us
  blocking collectives: 130 us -> 109 us
  Pallas kernels: 33.6 us -> 24 us
  other arithmetic: 8.91 us -> 3.34 us
    ppermute x10 -> x24, starting transfers between devices: 52 us -> 119 us  [the longest x15 85.1 us: shards(): lax.ppermute(largest, 'col', [(i, i ^ step) for i in range(16)])]
    ppermute x10 -> x24, waiting for transfers between devices: 78.8 us -> 52.5 us  [the longest x15 45.4 us: shards(): lax.ppermute(largest, 'col', [(i, i ^ step) for i in range(16)])]
    all_to_all x2 -> x1, blocking collectives: 130 us -> 109 us  [exchange(): return lax.all_to_all(array, axes, 0, 0, tiled=True)]
    all_to_all x2 -> x3, starting transfers between devices: 26.5 us -> 31.7 us  [exchange(): return lax.all_to_all(array, axes, 0, 0, tiled=True)]
    all_to_all x2 -> x3, waiting for transfers between devices: 11 us -> 11.3 us  [exchange(): return lax.all_to_all(array, axes, 0, 0, tiled=True)]
  transfers between devices with their start and end apart: 18 -> 33, of which waited for: 12 -> 12; matrix products, arithmetic and copies ran while one was open for 1% -> 1% of each run, Pallas kernels for 1% -> 0%
where the time goes in v2:
time: 377 us; the launch traced here: 376 us
  starting transfers between devices  164 us (44%)
  blocking collectives  109 us (29%)
  waiting for transfers between devices  71.4 us (19%)
  Pallas kernels  24 us (6%)
    all_to_all x1, blocking collectives, exchange(): return lax.all_to_all(array, axes, 0, 0, tiled=True)  109 us
    ppermute x15, starting transfers between devices, shards(): lax.ppermute(largest, 'col', [(i, i ^ step) for i in range(16)])  85.1 us
    ppermute x15, waiting for transfers between devices, shards(): lax.ppermute(largest, 'col', [(i, i ^ step) for i in range(16)])  45.4 us
    all_to_all x3, starting transfers between devices, exchange(): return lax.all_to_all(array, axes, 0, 0, tiled=True)  31.7 us
    ppermute x3, starting transfers between devices, shards(): lax.ppermute(pages[step], 'gz', [(i, (i + step) % 4) for i in range(4)])  12.1 us
    all_to_all x3, waiting for transfers between devices, exchange(): return lax.all_to_all(array, axes, 0, 0, tiled=True)  11.3 us
    ppermute x3, starting transfers between devices, shards(): lax.ppermute(orbitals, 'gz', [(i, (i - step) % 4) for i in range(4)])  10.9 us
    ppermute x3, starting transfers between devices, shards(): other = lax.ppermute(largest, 'row', [(i, i ^ step) for i in range(8)])  10.8 us
  transfers between devices with their start and end apart: 33, of which 12 were waited for; matrix products, arithmetic and copies ran while one was open for 1% of the time, Pallas kernels for 0%

profile of v2, /device:TPU:32, one launch (start us, length us, event | category | flops | bytes accessed | tf_op | source)
XLA Modules:
  0.0 376.0 jit_solution(3120160115351595210)
XLA Ops:
  1.3 6.5 %pack.1 = bf16[128,64,128]{2,1,0:T(8,128)(2,1)} custom-call(s32[3]{0:T(128)} %pad_add_fusion.ids_ref, s32[16,512]{1,0:T(8,128)} %bitcast.18, s32[8,16]{1,0:T(8,128)} %bitcast.20, bf16[1024,512]{1,0:T(8,128)(2,1)} %matrix_ref.1), custom_call_target="tpu_custom_call" | custom-call | tf_op jit(solution)/shard_map/pack/pallas_call | solution.py:249
  7.8 19.1 %all-to-all-start = ((bf16[128,64,128]{2,1,0:T(8,128)(2,1)}), bf16[128,64,128]{2,1,0:T(8,128)(2,1)S(1)}, u32[]{:S(2)}, u32[]{:S(2)}) async-start(bf16[128,64,128]{2,1,0:T(8,128)(2,1)} %pack.1), calls=%async_computation | async-start | bytes 4194304 | tf_op jit(solution)/shard_map/all_to_all | solution.py:240
  31.4 3.5 collective-permute-start.1
  36.9 5.3 %collective-permute-start.2 = (f32[8,128]{1,0:T(8,128)S(1)}, f32[8,128]{1,0:T(8,128)S(1)}, u32[]{:S(2)}, u32[]{:S(2)}) collective-permute-start(f32[8,128]{1,0:T(8,128)S(1)} %fusion.21), channel_id=1, source_target_pairs={{0,256},{64,320},{128,384},{192,448},{256,0},{320,64},{384,128},{4... | collective-permute-start | bytes 12296 | tf_op jit(solution)/shard_map/ppermute | solution.py:261
  44.0 5.4 %collective-permute-start.17 = (f32[8,128]{1,0:T(8,128)S(1)}, f32[8,128]{1,0:T(8,128)S(1)}, u32[]{:S(2)}, u32[]{:S(2)}) collective-permute-start(f32[8,128]{1,0:T(8,128)S(1)} %max.68), channel_id=1, source_target_pairs={{0,60},{4,56},{8,52},{12,48},{16,44},{20,40},{24,36},{28,32},{32,2... | collective-permute-start | bytes 12296 | tf_op jit(solution)/shard_map/ppermute | solution.py:265
  51.3 10.5 %collective-permute-start.15 = (f32[8,128]{1,0:T(8,128)S(1)}, f32[8,128]{1,0:T(8,128)S(1)}, u32[]{:S(2)}, u32[]{:S(2)}) collective-permute-start(f32[8,128]{1,0:T(8,128)S(1)} %max.68), channel_id=1, source_target_pairs={{0,52},{4,48},{8,60},{12,56},{16,36},{20,32},{24,44},{28,40},{32,2... | collective-permute-start | bytes 12296 | tf_op jit(solution)/shard_map/ppermute | solution.py:265
  61.9 2.8 collective-permute-start.14
  64.7 10.8 %collective-permute-start.13 = (f32[8,128]{1,0:T(8,128)S(1)}, f32[8,128]{1,0:T(8,128)S(1)}, u32[]{:S(2)}, u32[]{:S(2)}) collective-permute-start(f32[8,128]{1,0:T(8,128)S(1)} %max.68), channel_id=1, source_target_pairs={{0,44},{4,40},{8,36},{12,32},{16,60},{20,56},{24,52},{28,48},{32,1... | collective-permute-start | bytes 12296 | tf_op jit(solution)/shard_map/ppermute | solution.py:265
  75.5 45.4 %collective-permute-done.17 = f32[8,128]{1,0:T(8,128)S(1)} collective-permute-done((f32[8,128]{1,0:T(8,128)S(1)}, f32[8,128]{1,0:T(8,128)S(1)}, u32[]{:S(2)}, u32[]{:S(2)}) %collective-permute-start.17) | collective-permute-done | bytes 4128 | tf_op jit(solution)/shard_map/ppermute | solution.py:265
  120.9 9.1 %collective-permute-start.12 = (f32[8,128]{1,0:T(8,128)S(1)}, f32[8,128]{1,0:T(8,128)S(1)}, u32[]{:S(2)}, u32[]{:S(2)}) collective-permute-start(f32[8,128]{1,0:T(8,128)S(1)} %max.68), channel_id=1, source_target_pairs={{0,40},{4,44},{8,32},{12,36},{16,56},{20,60},{24,48},{28,52},{32,8... | collective-permute-start | bytes 12296 | tf_op jit(solution)/shard_map/ppermute | solution.py:265
  130.0 3.6 collective-permute-start.11
  133.7 10.4 %collective-permute-start.10 = (f32[8,128]{1,0:T(8,128)S(1)}, f32[8,128]{1,0:T(8,128)S(1)}, u32[]{:S(2)}, u32[]{:S(2)}) collective-permute-start(f32[8,128]{1,0:T(8,128)S(1)} %max.68), channel_id=1, source_target_pairs={{0,32},{4,36},{8,40},{12,44},{16,48},{20,52},{24,56},{28,60},{32,0... | collective-permute-start | bytes 12296 | tf_op jit(solution)/shard_map/ppermute | solution.py:265
  146.2 10.0 %collective-permute-start.8 = (f32[8,128]{1,0:T(8,128)S(1)}, f32[8,128]{1,0:T(8,128)S(1)}, u32[]{:S(2)}, u32[]{:S(2)}) collective-permute-start(f32[8,128]{1,0:T(8,128)S(1)} %max.68), channel_id=1, source_target_pairs={{0,24},{4,28},{8,16},{12,20},{16,8},{20,12},{24,0},{28,4},{32,56},... | collective-permute-start | bytes 12296 | tf_op jit(solution)/shard_map/ppermute | solution.py:265
  158.1 7.3 %collective-permute-start.6 = (f32[8,128]{1,0:T(8,128)S(1)}, f32[8,128]{1,0:T(8,128)S(1)}, u32[]{:S(2)}, u32[]{:S(2)}) collective-permute-start(f32[8,128]{1,0:T(8,128)S(1)} %max.68), channel_id=1, source_target_pairs={{0,16},{4,20},{8,24},{12,28},{16,0},{20,4},{24,8},{28,12},{32,48},... | collective-permute-start | bytes 12296 | tf_op jit(solution)/shard_map/ppermute | solution.py:265
  167.4 5.4 %collective-permute-start.4 = (f32[8,128]{1,0:T(8,128)S(1)}, f32[8,128]{1,0:T(8,128)S(1)}, u32[]{:S(2)}, u32[]{:S(2)}) collective-permute-start(f32[8,128]{1,0:T(8,128)S(1)} %max.68), channel_id=1, source_target_pairs={{0,8},{4,12},{8,0},{12,4},{16,24},{20,28},{24,16},{28,20},{32,40},... | collective-permute-start | bytes 12296 | tf_op jit(solution)/shard_map/ppermute | solution.py:265
  174.7 4.9 %collective-permute-start.18 = (f32[128,128]{1,0:T(8,128)S(1)}, f32[128,128]{1,0:T(8,128)S(1)}, u32[]{:S(2)}, u32[]{:S(2)}) collective-permute-start(f32[128,128]{1,0:T(8,128)S(1)} %copy-done.4), channel_id=1, source_target_pairs={{0,3},{1,0},{2,1},{3,2},{4,7},{5,4},{6,5},{7,6},{8,11},{9,8},{10,9... | collective-permute-start | bytes 196616 | tf_op jit(solution)/shard_map/ppermute | solution.py:270
  181.6 4.1 %collective-permute-start.19 = (f32[128,128]{1,0:T(8,128)S(1)}, f32[128,128]{1,0:T(8,128)S(1)}, u32[]{:S(2)}, u32[]{:S(2)}) collective-permute-start(f32[128,128]{1,0:T(8,128)S(1)} %copy-done.4), channel_id=1, source_target_pairs={{0,2},{1,3},{2,0},{3,1},{4,6},{5,7},{6,4},{7,5},{8,10},{9,11},{10,... | collective-permute-start | bytes 196616 | tf_op jit(solution)/shard_map/ppermute | solution.py:270
  189.3 3.1 density.1
  194.0 3.5 collective-permute-done.21
  199.9 3.4 collective-permute-start.24
  205.6 2.5 collective-permute-start.25
  208.1 4.6 %collective-permute-start.26 = (f32[6,12,2]{2,1,0:T(8,128)S(1)}, f32[6,12,2]{2,1,0:T(8,128)S(1)}, u32[]{:S(2)}, u32[]{:S(2)}) collective-permute-start(f32[6,12,2]{2,1,0:T(8,128)S(1)} %get-tuple-element.27), channel_id=1, source_target_pairs={{1,0},{2,1},{3,2},{0,3},{5,4},{6,5},{7,6},{4,7},{9,8},{10,9},{11,1... | collective-permute-start | bytes 1736 | tf_op jit(solution)/shard_map/ppermute | solution.py:33
  215.0 3.2 ham.1
  218.4 108.9 %all_to_all.20 = f16[128,64,128]{2,1,0:T(8,128)(2,1)S(1)} all-to-all(f16[128,64,128]{2,1,0:T(8,128)(2,1)S(1)} %bitcast.22), channel_id=1, replica_groups=mesh['row'=8,'col'=16,'gz'=4] {'row','col'}, dimensions={0} | all-to-all | bytes 4194304 | tf_op jit(solution)/shard_map/all_to_all | solution.py:240
  328.1 9.4 %owner.1 = (s16[16,72,128]{2,1,0:T(8,128)(2,1)}, s16[1040,128]{1,0:T(8,128)(2,1)S(1)}, s16[1040,128]{1,0:T(8,128)(2,1)S(1)}, s16[1040,128]{1,0:T(8,128)(2,1)S(1)}, s16[1040,128]{1,0:T(8,128)(2,1)S(1)}) custom-call(s32[3]{0:T(128)S(1)} %copy-done.3, s32[16,512]{1,0:T(8,128)S(1)} %bitcast.19, s32[8,16]{1,0:T(8,128)S(1)} %bitcast.21, ...), custom_call_target="tpu_custom_call" | custom-call | tf_op jit(solution)/shard_map/owner/pallas_call | solution.py:297
  337.5 7.5 %all-to-all-start.2 = ((s16[16,72,128]{2,1,0:T(8,128)(2,1)}), s16[16,72,128]{2,1,0:T(8,128)(2,1)S(1)}, u32[]{:S(2)}, u32[]{:S(2)}) async-start(s16[16,72,128]{2,1,0:T(8,128)(2,1)} %get-tuple-element.11), calls=%async_computation.2 | async-start | bytes 589824 | tf_op jit(solution)/shard_map/all_to_all | solution.py:240
  345.0 3.7 collective-permute-start.27
  348.7 5.2 %collective-permute-start.28 = (s16[1040,128]{1,0:T(8,128)(2,1)S(1)}, s16[1040,128]{1,0:T(8,128)(2,1)S(1)}, u32[]{:S(2)}, u32[]{:S(2)}) collective-permute-start(s16[1040,128]{1,0:T(8,128)(2,1)S(1)} %get-tuple-element.9), channel_id=1, source_target_pairs={{0,2},{1,3},{2,0},{3,1},{4,6},{5,7},{6,4},{7,5},{8,10},{9,11},{10,... | collective-permute-start | bytes 798728 | tf_op jit(solution)/shard_map/ppermute | solution.py:312
  353.9 3.3 collective-permute-start.29
  357.2 7.0 %all-to-all-done.2.coded_ref = s16[16,72,128]{2,1,0:T(8,128)(2,1)S(1)} async-done(((s16[16,72,128]{2,1,0:T(8,128)(2,1)}), s16[16,72,128]{2,1,0:T(8,128)(2,1)S(1)}, u32[]{:S(2)}, u32[]{:S(2)}) %all-to-all-start.2) | async-done | bytes 294944 | tf_op jit(solution)/shard_map/all_to_all | solution.py:240
  364.9 5.1 %all-to-all-start.3 = ((f32[4,16,128]{2,1,0:T(8,128)}), f32[4,16,128]{2,1,0:T(8,128)S(1)}, u32[]{:S(2)}, u32[]{:S(2)}) async-start(f32[4,16,128]{2,1,0:T(8,128)} %bitcast.13), calls=%async_computation.3 | async-start | bytes 65536 | tf_op jit(solution)/shard_map/all_to_all | solution.py:240
  371.1 4.3 %all-to-all-done.3 = f32[4,16,128]{2,1,0:T(8,128)S(1)} async-done(((f32[4,16,128]{2,1,0:T(8,128)}), f32[4,16,128]{2,1,0:T(8,128)S(1)}, u32[]{:S(2)}, u32[]{:S(2)}) %all-to-all-start.3) | async-done | bytes 32800 | tf_op jit(solution)/shard_map/all_to_all | solution.py:240
  (76 shorter events, 34.7 us)
Async XLA Ops:
  7.8 181.5 %all-to-all-start = ((bf16[128,64,128]{2,1,0:T(8,128)(2,1)}), bf16[128,64,128]{2,1,0:T(8,128)(2,1)S(1)}, u32[]{:S(2)}, u32[]{:S(2)}) async-start(bf16[128,64,128]{2,1,0:T(8,128)(2,1)} %pack.1), calls=%async_computation | async-start | bytes 4194304 | tf_op jit(solution)/shard_map/all_to_all | solution.py:240
  28.4 3.1 collective-permute-start
  31.4 5.5 %collective-permute-start.1 = (f32[8,128]{1,0:T(8,128)S(1)}, f32[8,128]{1,0:T(8,128)S(1)}, u32[]{:S(2)}, u32[]{:S(2)}) collective-permute-start(f32[8,128]{1,0:T(8,128)S(1)} %broadcast_maximum_fusion), channel_id=1, source_target_pairs={{0,128},{64,192},{128,0},{192,64},{256,384},{320,448},{384,256},{4... | collective-permute-start | bytes 12296 | tf_op jit(solution)/shard_map/ppermute | solution.py:261
  36.9 7.0 %collective-permute-start.2 = (f32[8,128]{1,0:T(8,128)S(1)}, f32[8,128]{1,0:T(8,128)S(1)}, u32[]{:S(2)}, u32[]{:S(2)}) collective-permute-start(f32[8,128]{1,0:T(8,128)S(1)} %fusion.21), channel_id=1, source_target_pairs={{0,256},{64,320},{128,384},{192,448},{256,0},{320,64},{384,128},{4... | collective-permute-start | bytes 12296 | tf_op jit(solution)/shard_map/ppermute | solution.py:261
  44.0 77.0 %collective-permute-start.17 = (f32[8,128]{1,0:T(8,128)S(1)}, f32[8,128]{1,0:T(8,128)S(1)}, u32[]{:S(2)}, u32[]{:S(2)}) collective-permute-start(f32[8,128]{1,0:T(8,128)S(1)} %max.68), channel_id=1, source_target_pairs={{0,60},{4,56},{8,52},{12,48},{16,44},{20,40},{24,36},{28,32},{32,2... | collective-permute-start | bytes 12296 | tf_op jit(solution)/shard_map/ppermute | solution.py:265
  49.4 80.6 %collective-permute-start.16 = (f32[8,128]{1,0:T(8,128)S(1)}, f32[8,128]{1,0:T(8,128)S(1)}, u32[]{:S(2)}, u32[]{:S(2)}) collective-permute-start(f32[8,128]{1,0:T(8,128)S(1)} %max.68), channel_id=1, source_target_pairs={{0,56},{4,60},{8,48},{12,52},{16,40},{20,44},{24,32},{28,36},{32,2... | collective-permute-start | bytes 12296 | tf_op jit(solution)/shard_map/ppermute | solution.py:265
  51.3 82.3 %collective-permute-start.15 = (f32[8,128]{1,0:T(8,128)S(1)}, f32[8,128]{1,0:T(8,128)S(1)}, u32[]{:S(2)}, u32[]{:S(2)}) collective-permute-start(f32[8,128]{1,0:T(8,128)S(1)} %max.68), channel_id=1, source_target_pairs={{0,52},{4,48},{8,60},{12,56},{16,36},{20,32},{24,44},{28,40},{32,2... | collective-permute-start | bytes 12296 | tf_op jit(solution)/shard_map/ppermute | solution.py:265
  61.9 82.2 %collective-permute-start.14 = (f32[8,128]{1,0:T(8,128)S(1)}, f32[8,128]{1,0:T(8,128)S(1)}, u32[]{:S(2)}, u32[]{:S(2)}) collective-permute-start(f32[8,128]{1,0:T(8,128)S(1)} %max.68), channel_id=1, source_target_pairs={{0,48},{4,52},{8,56},{12,60},{16,32},{20,36},{24,40},{28,44},{32,1... | collective-permute-start | bytes 12296 | tf_op jit(solution)/shard_map/ppermute | solution.py:265
  64.7 81.4 %collective-permute-start.13 = (f32[8,128]{1,0:T(8,128)S(1)}, f32[8,128]{1,0:T(8,128)S(1)}, u32[]{:S(2)}, u32[]{:S(2)}) collective-permute-start(f32[8,128]{1,0:T(8,128)S(1)} %max.68), channel_id=1, source_target_pairs={{0,44},{4,40},{8,36},{12,32},{16,60},{20,56},{24,52},{28,48},{32,1... | collective-permute-start | bytes 12296 | tf_op jit(solution)/shard_map/ppermute | solution.py:265
  120.9 35.3 %collective-permute-start.12 = (f32[8,128]{1,0:T(8,128)S(1)}, f32[8,128]{1,0:T(8,128)S(1)}, u32[]{:S(2)}, u32[]{:S(2)}) collective-permute-start(f32[8,128]{1,0:T(8,128)S(1)} %max.68), channel_id=1, source_target_pairs={{0,40},{4,44},{8,32},{12,36},{16,56},{20,60},{24,48},{28,52},{32,8... | collective-permute-start | bytes 12296 | tf_op jit(solution)/shard_map/ppermute | solution.py:265
  130.0 28.1 %collective-permute-start.11 = (f32[8,128]{1,0:T(8,128)S(1)}, f32[8,128]{1,0:T(8,128)S(1)}, u32[]{:S(2)}, u32[]{:S(2)}) collective-permute-start(f32[8,128]{1,0:T(8,128)S(1)} %max.68), channel_id=1, source_target_pairs={{0,36},{4,32},{8,44},{12,40},{16,52},{20,48},{24,60},{28,56},{32,4... | collective-permute-start | bytes 12296 | tf_op jit(solution)/shard_map/ppermute | solution.py:265
  133.7 31.8 %collective-permute-start.10 = (f32[8,128]{1,0:T(8,128)S(1)}, f32[8,128]{1,0:T(8,128)S(1)}, u32[]{:S(2)}, u32[]{:S(2)}) collective-permute-start(f32[8,128]{1,0:T(8,128)S(1)} %max.68), channel_id=1, source_target_pairs={{0,32},{4,36},{8,40},{12,44},{16,48},{20,52},{24,56},{28,60},{32,0... | collective-permute-start | bytes 12296 | tf_op jit(solution)/shard_map/ppermute | solution.py:265
  144.0 23.3 %collective-permute-start.9 = (f32[8,128]{1,0:T(8,128)S(1)}, f32[8,128]{1,0:T(8,128)S(1)}, u32[]{:S(2)}, u32[]{:S(2)}) collective-permute-start(f32[8,128]{1,0:T(8,128)S(1)} %max.68), channel_id=1, source_target_pairs={{0,28},{4,24},{8,20},{12,16},{16,12},{20,8},{24,4},{28,0},{32,60},... | collective-permute-start | bytes 12296 | tf_op jit(solution)/shard_map/ppermute | solution.py:265
  146.2 26.6 %collective-permute-start.8 = (f32[8,128]{1,0:T(8,128)S(1)}, f32[8,128]{1,0:T(8,128)S(1)}, u32[]{:S(2)}, u32[]{:S(2)}) collective-permute-start(f32[8,128]{1,0:T(8,128)S(1)} %max.68), channel_id=1, source_target_pairs={{0,24},{4,28},{8,16},{12,20},{16,8},{20,12},{24,0},{28,4},{32,56},... | collective-permute-start | bytes 12296 | tf_op jit(solution)/shard_map/ppermute | solution.py:265
  156.2 18.5 %collective-permute-start.7 = (f32[8,128]{1,0:T(8,128)S(1)}, f32[8,128]{1,0:T(8,128)S(1)}, u32[]{:S(2)}, u32[]{:S(2)}) collective-permute-start(f32[8,128]{1,0:T(8,128)S(1)} %max.68), channel_id=1, source_target_pairs={{0,20},{4,16},{8,28},{12,24},{16,4},{20,0},{24,12},{28,8},{32,52},... | collective-permute-start | bytes 12296 | tf_op jit(solution)/shard_map/ppermute | solution.py:265
  158.1 21.5 %collective-permute-start.6 = (f32[8,128]{1,0:T(8,128)S(1)}, f32[8,128]{1,0:T(8,128)S(1)}, u32[]{:S(2)}, u32[]{:S(2)}) collective-permute-start(f32[8,128]{1,0:T(8,128)S(1)} %max.68), channel_id=1, source_target_pairs={{0,16},{4,20},{8,24},{12,28},{16,0},{20,4},{24,8},{28,12},{32,48},... | collective-permute-start | bytes 12296 | tf_op jit(solution)/shard_map/ppermute | solution.py:265
  165.4 16.2 %collective-permute-start.5 = (f32[8,128]{1,0:T(8,128)S(1)}, f32[8,128]{1,0:T(8,128)S(1)}, u32[]{:S(2)}, u32[]{:S(2)}) collective-permute-start(f32[8,128]{1,0:T(8,128)S(1)} %max.68), channel_id=1, source_target_pairs={{0,12},{4,8},{8,4},{12,0},{16,28},{20,24},{24,20},{28,16},{32,44},... | collective-permute-start | bytes 12296 | tf_op jit(solution)/shard_map/ppermute | solution.py:265
  167.4 18.4 %collective-permute-start.4 = (f32[8,128]{1,0:T(8,128)S(1)}, f32[8,128]{1,0:T(8,128)S(1)}, u32[]{:S(2)}, u32[]{:S(2)}) collective-permute-start(f32[8,128]{1,0:T(8,128)S(1)} %max.68), channel_id=1, source_target_pairs={{0,8},{4,12},{8,0},{12,4},{16,24},{20,28},{24,16},{28,20},{32,40},... | collective-permute-start | bytes 12296 | tf_op jit(solution)/shard_map/ppermute | solution.py:265
  172.8 13.0 %collective-permute-start.3 = (f32[8,128]{1,0:T(8,128)S(1)}, f32[8,128]{1,0:T(8,128)S(1)}, u32[]{:S(2)}, u32[]{:S(2)}) collective-permute-start(f32[8,128]{1,0:T(8,128)S(1)} %max.68), channel_id=1, source_target_pairs={{0,4},{4,0},{8,12},{12,8},{16,20},{20,16},{24,28},{28,24},{32,36},... | collective-permute-start | bytes 12296 | tf_op jit(solution)/shard_map/ppermute | solution.py:265
  174.7 11.6 %collective-permute-start.18 = (f32[128,128]{1,0:T(8,128)S(1)}, f32[128,128]{1,0:T(8,128)S(1)}, u32[]{:S(2)}, u32[]{:S(2)}) collective-permute-start(f32[128,128]{1,0:T(8,128)S(1)} %copy-done.4), channel_id=1, source_target_pairs={{0,3},{1,0},{2,1},{3,2},{4,7},{5,4},{6,5},{7,6},{8,11},{9,8},{10,9... | collective-permute-start | bytes 196616 | tf_op jit(solution)/shard_map/ppermute | solution.py:270
  179.7 7.4 %collective-permute-start.20 = (f32[128,128]{1,0:T(8,128)S(1)}, f32[128,128]{1,0:T(8,128)S(1)}, u32[]{:S(2)}, u32[]{:S(2)}) collective-permute-start(f32[128,128]{1,0:T(8,128)S(1)} %copy-done.4), channel_id=1, source_target_pairs={{0,1},{1,2},{2,3},{3,0},{4,5},{5,6},{6,7},{7,4},{8,9},{9,10},{10,1... | collective-permute-start | bytes 196616 | tf_op jit(solution)/shard_map/ppermute | solution.py:270
  181.6 7.7 %collective-permute-start.19 = (f32[128,128]{1,0:T(8,128)S(1)}, f32[128,128]{1,0:T(8,128)S(1)}, u32[]{:S(2)}, u32[]{:S(2)}) collective-permute-start(f32[128,128]{1,0:T(8,128)S(1)} %copy-done.4), channel_id=1, source_target_pairs={{0,2},{1,3},{2,0},{3,1},{4,6},{5,7},{6,4},{7,5},{8,10},{9,11},{10,... | collective-permute-start | bytes 196616 | tf_op jit(solution)/shard_map/ppermute | solution.py:270
  192.6 4.9 %collective-permute-start.21 = (f32[2,8,24]{2,1,0:T(8,128)S(1)}, f32[2,8,24]{2,1,0:T(8,128)S(1)}, u32[]{:S(2)}, u32[]{:S(2)}) collective-permute-start(f32[2,8,24]{2,1,0:T(8,128)S(1)} %add_maximum_fusion), channel_id=1, source_target_pairs={{0,64},{64,128},{128,192},{192,256},{256,320},{320,384},{384,448},... | collective-permute-start | bytes 4616 | tf_op jit(solution)/shard_map/ppermute | solution.py:31
  197.5 5.9 %collective-permute-start.23 = (f32[6,2,24]{2,1,0:T(2,128)S(1)}, f32[6,2,24]{2,1,0:T(2,128)S(1)}, u32[]{:S(2)}, u32[]{:S(2)}) collective-permute-start(f32[6,2,24]{2,1,0:T(2,128)S(1)} %get-tuple-element.28), channel_id=1, source_target_pairs={{0,4},{4,8},{8,12},{12,16},{16,20},{20,24},{24,28},{28,32},{32,36}... | collective-permute-start | bytes 3464 | tf_op jit(solution)/shard_map/ppermute | solution.py:31
  199.9 5.5 %collective-permute-start.24 = (f32[6,2,24]{2,1,0:T(2,128)S(1)}, f32[6,2,24]{2,1,0:T(2,128)S(1)}, u32[]{:S(2)}, u32[]{:S(2)}) collective-permute-start(f32[6,2,24]{2,1,0:T(2,128)S(1)} %get-tuple-element.29), channel_id=1, source_target_pairs={{4,0},{8,4},{12,8},{16,12},{20,16},{24,20},{28,24},{32,28},{36,32}... | collective-permute-start | bytes 3464 | tf_op jit(solution)/shard_map/ppermute | solution.py:33
  205.6 7.8 %collective-permute-start.25 = (f32[6,12,2]{2,1,0:T(8,128)S(1)}, f32[6,12,2]{2,1,0:T(8,128)S(1)}, u32[]{:S(2)}, u32[]{:S(2)}) collective-permute-start(f32[6,12,2]{2,1,0:T(8,128)S(1)} %get-tuple-element.26), channel_id=1, source_target_pairs={{0,1},{1,2},{2,3},{3,0},{4,5},{5,6},{6,7},{7,4},{8,9},{9,10},{10,1... | collective-permute-start | bytes 1736 | tf_op jit(solution)/shard_map/ppermute | solution.py:31
  208.1 6.3 %collective-permute-start.26 = (f32[6,12,2]{2,1,0:T(8,128)S(1)}, f32[6,12,2]{2,1,0:T(8,128)S(1)}, u32[]{:S(2)}, u32[]{:S(2)}) collective-permute-start(f32[6,12,2]{2,1,0:T(8,128)S(1)} %get-tuple-element.27), channel_id=1, source_target_pairs={{1,0},{2,1},{3,2},{0,3},{5,4},{6,5},{7,6},{4,7},{9,8},{10,9},{11,1... | collective-permute-start | bytes 1736 | tf_op jit(solution)/shard_map/ppermute | solution.py:33
  337.5 26.7 %all-to-all-start.2 = ((s16[16,72,128]{2,1,0:T(8,128)(2,1)}), s16[16,72,128]{2,1,0:T(8,128)(2,1)S(1)}, u32[]{:S(2)}, u32[]{:S(2)}) async-start(s16[16,72,128]{2,1,0:T(8,128)(2,1)} %get-tuple-element.11), calls=%async_computation.2 | async-start | bytes 589824 | tf_op jit(solution)/shard_map/all_to_all | solution.py:240
  345.0 24.9 %collective-permute-start.27 = (s16[1040,128]{1,0:T(8,128)(2,1)S(1)}, s16[1040,128]{1,0:T(8,128)(2,1)S(1)}, u32[]{:S(2)}, u32[]{:S(2)}) collective-permute-start(s16[1040,128]{1,0:T(8,128)(2,1)S(1)} %get-tuple-element.8), channel_id=1, source_target_pairs={{0,1},{1,2},{2,3},{3,0},{4,5},{5,6},{6,7},{7,4},{8,9},{9,10},{10,1... | collective-permute-start | bytes 798728 | tf_op jit(solution)/shard_map/ppermute | solution.py:312
  348.7 21.3 %collective-permute-start.28 = (s16[1040,128]{1,0:T(8,128)(2,1)S(1)}, s16[1040,128]{1,0:T(8,128)(2,1)S(1)}, u32[]{:S(2)}, u32[]{:S(2)}) collective-permute-start(s16[1040,128]{1,0:T(8,128)(2,1)S(1)} %get-tuple-element.9), channel_id=1, source_target_pairs={{0,2},{1,3},{2,0},{3,1},{4,6},{5,7},{6,4},{7,5},{8,10},{9,11},{10,... | collective-permute-start | bytes 798728 | tf_op jit(solution)/shard_map/ppermute | solution.py:312
  353.9 16.1 %collective-permute-start.29 = (s16[1040,128]{1,0:T(8,128)(2,1)S(1)}, s16[1040,128]{1,0:T(8,128)(2,1)S(1)}, u32[]{:S(2)}, u32[]{:S(2)}) collective-permute-start(s16[1040,128]{1,0:T(8,128)(2,1)S(1)} %get-tuple-element.10), channel_id=1, source_target_pairs={{0,3},{1,0},{2,1},{3,2},{4,7},{5,4},{6,5},{7,6},{8,11},{9,8},{10,9... | collective-permute-start | bytes 798728 | tf_op jit(solution)/shard_map/ppermute | solution.py:312
  364.9 10.5 %all-to-all-start.3 = ((f32[4,16,128]{2,1,0:T(8,128)}), f32[4,16,128]{2,1,0:T(8,128)S(1)}, u32[]{:S(2)}, u32[]{:S(2)}) async-start(f32[4,16,128]{2,1,0:T(8,128)} %bitcast.13), calls=%async_computation.3 | async-start | bytes 65536 | tf_op jit(solution)/shard_map/all_to_all | solution.py:240
  (7 other events, 354.5 us)

commit v3 on v2

--- a/solution.py
+++ b/solution.py
@@ -111,7 +111,7 @@
     lax.fori_loop(0, 128, fill, 0, unroll=4)
 
 
-def density_kernel(blocks_ref, phi_ref, unit_ref, orbitals_ref, out_ref):
+def density_kernel(blocks_ref, phi_ref, unit_ref, out_ref):
     phi = phi_ref[...]
 
     def part(n, total):
@@ -159,18 +159,18 @@
     sums,
     turned,
     powers,
+    products,
 ):
     sums[...] = jnp.zeros_like(sums)
 
     def add(t, carry):
         a0, a1, b = listed_pair(ids_ref, lists_ref, t)
-        block = blocks_ref[t]
+        block = blocks_ref[t] * scale_ref[8 * (((t & 15) ^ ids_ref[1]) >> 2)]
         sums[a0 & 1, b, a0 >> 1, :, 0:BS] += block[:, 0:BS]
         sums[1 - (a1 & 1), b, a1 >> 1, :, BS:128] += block[:, BS:128]
         return carry
 
     lax.fori_loop(0, 128, add, 0, unroll=4)
-    unit = scale_ref[0]
     outs = (out0_ref, out1_ref, out2_ref, out3_ref)
 
     def finish(q, carry):
@@ -181,7 +181,7 @@
                 keep = lane_pair(
                     pattern_ref[b, 2 * q].astype(jnp.float32), pattern_ref[b, 2 * q + 1].astype(jnp.float32), BS
                 )
-                page = (sums[0, b, q] + pltpu.roll(sums[1, b, q], BS, 1)) * (keep * unit)
+                page = (sums[0, b, q] + pltpu.roll(sums[1, b, q], BS, 1)) * keep
                 place = 2 * n + half
                 turned[BS * place : BS * place + BS, :] = page
                 levels, power = coded(page)
@@ -196,24 +196,36 @@
             preferred_element_type=jnp.float32,
         )
         for half in range(2):
-            levels, power = coded(part[BS * half : BS * half + BS])
-            terms_ref[2 * q + half, 0:BS, :] = levels
-            terms_ref[2 * q + half, BS : BS + 8, :] = (
-                jnp.broadcast_to(power, (8, 128)).astype(jnp.int32).astype(jnp.int16)
-            )
+            for g in range(4):
+                start = BS * half + 16 * g
+                rows = pl.ds(pl.multiple_of((2 * q + half) * 16, 16), 16)
+                products[g, rows, :] = part[start : start + 16]
         return carry
 
     lax.fori_loop(0, 8, finish, 0)
+    for g in range(4):
+        product_powers = []
+        for n in range(4):
+            levels, power = coded(products[g, BS * n : BS * n + BS, :])
+            terms_ref[g, BS * n : BS * n + BS, :] = levels
+            product_powers.append(power)
+        terms_ref[g, 4 * BS : 4 * BS + 8, :] = (
+            jnp.concatenate(product_powers * 2, axis=0).astype(jnp.int32).astype(jnp.int16)
+        )
     for n, out in enumerate(outs):
         out[PAGES * BS : PAGES * BS + SCALES, :] = powers[n].astype(jnp.int32).astype(jnp.int16)
 
 
 def term_kernel(coded_ref, out_ref):
-    total = jnp.zeros((BS, 128), jnp.float32)
-    for c in range(16):
-        step = jnp.exp2(coded_ref[c, BS : BS + 8, :].astype(jnp.float32)[0:1] - 15.0)
-        total = total + coded_ref[c, 0:BS, :].astype(jnp.float32) * step
-    out_ref[...] = total
+    steps = [
+        jnp.exp2(coded_ref[g, 4 * BS : 4 * BS + 8, :].astype(jnp.float32) - 15.0) for g in range(4)
+    ]
+    for n in range(4):
+        total = jnp.zeros((BS, 128), jnp.float32)
+        for g in range(4):
+            levels = coded_ref[g, BS * n : BS * n + BS, :].astype(jnp.float32)
+            total = total + levels * steps[g][n : n + 1]
+        out_ref[BS * n : BS * n + BS, :] = total
 
 
 def share_kernel(coded0_ref, coded1_ref, coded2_ref, coded3_ref, out_ref):
@@ -261,24 +273,21 @@
         other = lax.ppermute(largest, "row", [(i, i ^ step) for i in range(8)])
         largest = jnp.maximum(largest, other)
     others = []
-    for step in range(1, 16):
+    for step in (1, 2, 3):
         others.append(lax.ppermute(largest, "col", [(i, i ^ step) for i in range(16)]))
     for other in others:
         largest = jnp.maximum(largest, other)
-    columns = [orbitals]
-    for step in range(1, 4):
-        columns.append(lax.ppermute(orbitals, "gz", [(i, (i - step) % 4) for i in range(4)]))
-    all_orbitals = jnp.stack(columns)
-    unit = jnp.square(jnp.maximum(largest, 1e-15))[0, 0:1]
+    largest = jnp.maximum(largest, 1e-15)
+    unit = jnp.square(largest)[0, 0:1]
 
     rho = pl.pallas_call(
         density_kernel,
         out_shape=jax.ShapeDtypeStruct((1, 384), jnp.float32),
-        in_specs=[vmem, vmem, anywhere, anywhere],
+        in_specs=[vmem, vmem, anywhere],
         out_specs=vmem,
         compiler_params=pltpu.CompilerParams(vmem_limit_bytes=12 * MIB),
         name="density",
-    )(incoming.reshape(8, 1024, 128), phi, unit, all_orbitals)
+    )(incoming.reshape(8, 1024, 128), phi, unit)
     density = jnp.maximum(rho.reshape(core_density.shape) + core_density, density_floor)
     field = potential_deep(density)
 
@@ -292,24 +301,42 @@
     )(1.0 / unit, phi, field.reshape(1, -1))
     returning = local_ham.astype(jnp.float16).reshape(128, BS, 128)
     arrived = exchange(returning, PLANE).astype(jnp.float32)
+    peaks = [largest]
+    for step in (4, 8, 12):
+        peaks.append(lax.ppermute(largest, "col", [(i, i ^ step) for i in range(16)]))
+    columns = [orbitals]
+    for step in range(1, 4):
+        columns.append(lax.ppermute(orbitals, "gz", [(i, (i - step) % 4) for i in range(4)]))
+    units = jnp.square(jnp.concatenate(peaks, axis=0)[:, 0])
+    all_orbitals = jnp.stack(columns)
 
     page_shape = jax.ShapeDtypeStruct((PAGES * BS + SCALES, 128), jnp.int16)
     terms, *pages = pl.pallas_call(
         owner_kernel,
-        out_shape=[jax.ShapeDtypeStruct((16, BS + 8, 128), jnp.int16)] + [page_shape] * 4,
+        out_shape=[jax.ShapeDtypeStruct((4, 4 * BS + 8, 128), jnp.int16)] + [page_shape] * 4,
         in_specs=[smem, smem, smem, smem, vmem, vmem],
         out_specs=[vmem] * 5,
         scratch_shapes=[
             pltpu.VMEM((2, 8, 8, BS, 128), jnp.float32),
             pltpu.VMEM((512, 128), jnp.float32),
             pltpu.VMEM((4, SCALES, 128), jnp.float32),
+            pltpu.VMEM((4, 256, 128), jnp.float32),
         ],
         compiler_params=pltpu.CompilerParams(vmem_limit_bytes=24 * MIB),
         name="owner",
-    )(ids, lists, pattern, unit, arrived, all_orbitals)
-    terms = exchange(terms, "col")
+    )(ids, lists, pattern, units, arrived, all_orbitals)
+    terms = exchange(terms, "gz")
     for step in range(1, 4):
         pages[step] = lax.ppermute(pages[step], "gz", [(i, (i + step) % 4) for i in range(4)])
+    sums = pl.pallas_call(
+        term_kernel,
+        out_shape=jax.ShapeDtypeStruct((256, 128), jnp.float32),
+        in_specs=[vmem],
+        out_specs=vmem,
+        compiler_params=pltpu.CompilerParams(vmem_limit_bytes=4 * MIB),
+        name="sums",
+    )(terms)
+    applied = jnp.sum(exchange(sums.reshape(16, 16, 128), "col"), axis=0)
     share = pl.pallas_call(
         share_kernel,
         out_shape=jax.ShapeDtypeStruct((1024, 128), jnp.float32),
@@ -318,15 +345,6 @@
         compiler_params=pltpu.CompilerParams(vmem_limit_bytes=8 * MIB),
         name="share",
     )(*pages)
-    sums = pl.pallas_call(
-        term_kernel,
-        out_shape=jax.ShapeDtypeStruct((BS, 128), jnp.float32),
-        in_specs=[vmem],
-        out_specs=vmem,
-        compiler_params=pltpu.CompilerParams(vmem_limit_bytes=4 * MIB),
-        name="sums",
-    )(terms)
-    applied = jnp.sum(exchange(sums.reshape(4, 16, 128), "gz"), axis=0)
     return (share, applied)
 
 

time: 377 us -> 323 us (0.86)
  the two profiles are of different devices: /device:TPU:32 before, /device:TPU:6 now
where the time goes in v3:
time: 323 us; the launch traced here: 322 us
  waiting for transfers between devices  161 us (50%)
  starting transfers between devices  120 us (37%)
  Pallas kernels  22.7 us (7%)
  blocking collectives  9.11 us (3%)
  other arithmetic  4.74 us (1%)
    ppermute x6, waiting for transfers between devices, shards(): lax.ppermute(largest, 'col', [(i, i ^ step) for i in range(16)])  132 us
    all_to_all x3, starting transfers between devices, exchange(): return lax.all_to_all(array, axes, 0, 0, tiled=True)  40.3 us
    ppermute x6, starting transfers between devices, shards(): lax.ppermute(largest, 'col', [(i, i ^ step) for i in range(16)])  38.1 us
    ppermute x3, starting transfers between devices, shards(): lax.ppermute(pages[step], 'gz', [(i, (i + step) % 4) for i in range(4)])  9.51 us
    ppermute x3, waiting for transfers between devices, with_halo(): lax.ppermute(tail, axis, [(i, (i + 1) % count) for i in range(count)])  9.42 us
    all_to_all x1, blocking collectives, exchange(): return lax.all_to_all(array, axes, 0, 0, tiled=True)  9.11 us
    ppermute x3, starting transfers between devices, shards(): lax.ppermute(orbitals, 'gz', [(i, (i - step) % 4) for i in range(4)])  8.97 us
    pallas_call x1, Pallas kernels, shards(): pl.pallas_call(owner_kernel, out_shape=[jax.ShapeDtypeStruct((4, 4 * BS +...  8.07 us
  transfers between devices with their start and end apart: 24, of which 15 were waited for; matrix products, arithmetic and copies ran while one was open for 1% of the time, Pallas kernels for 0%

profile of v3, /device:TPU:6, one launch (start us, length us, event | category | flops | bytes accessed | tf_op | source)
XLA Modules:
  0.0 321.6 jit_solution(1361314121096940736)
XLA Ops:
  1.3 6.5 %pack.1 = bf16[128,64,128]{2,1,0:T(8,128)(2,1)} custom-call(s32[3]{0:T(128)} %pad_add_fusion.ids_ref, s32[16,512]{1,0:T(8,128)} %bitcast.18, s32[8,16]{1,0:T(8,128)} %bitcast.20, bf16[1024,512]{1,0:T(8,128)(2,1)} %matrix_ref.1), custom_call_target="tpu_custom_call" | custom-call | tf_op jit(solution)/shard_map/pack/pallas_call | solution.py:261
  7.8 20.0 %all-to-all-start = ((bf16[128,64,128]{2,1,0:T(8,128)(2,1)}), bf16[128,64,128]{2,1,0:T(8,128)(2,1)S(1)}, u32[]{:S(2)}, u32[]{:S(2)}) async-start(bf16[128,64,128]{2,1,0:T(8,128)(2,1)} %pack.1), calls=%async_computation | async-start | bytes 4194304 | tf_op jit(solution)/shard_map/all_to_all | solution.py:252
  32.2 2.5 collective-permute-start.1
  34.8 2.9 collective-permute-done.1
  37.7 2.9 collective-permute-start.2
  40.7 4.1 %collective-permute-done.2 = f32[8,128]{1,0:T(8,128)S(1)} collective-permute-done((f32[8,128]{1,0:T(8,128)S(1)}, f32[8,128]{1,0:T(8,128)S(1)}, u32[]{:S(2)}, u32[]{:S(2)}) %collective-permute-start.2) | collective-permute-done | bytes 4128 | tf_op jit(solution)/shard_map/ppermute | solution.py:273
  44.8 5.2 %collective-permute-start.5 = (f32[8,128]{1,0:T(8,128)S(1)}, f32[8,128]{1,0:T(8,128)S(1)}, u32[]{:S(2)}, u32[]{:S(2)}) collective-permute-start(f32[8,128]{1,0:T(8,128)S(1)} %max.32), channel_id=1, source_target_pairs={{0,12},{4,8},{8,4},{12,0},{16,28},{20,24},{24,20},{28,16},{32,44},... | collective-permute-start | bytes 12296 | tf_op jit(solution)/shard_map/ppermute | solution.py:277
  51.9 3.0 collective-permute-start.3
  54.9 61.1 %collective-permute-done.5 = f32[8,128]{1,0:T(8,128)S(1)} collective-permute-done((f32[8,128]{1,0:T(8,128)S(1)}, f32[8,128]{1,0:T(8,128)S(1)}, u32[]{:S(2)}, u32[]{:S(2)}) %collective-permute-start.5) | collective-permute-done | bytes 4128 | tf_op jit(solution)/shard_map/ppermute | solution.py:277
  116.0 2.5 collective-permute-done.4
  119.1 4.5 %all-to-all-done = bf16[128,64,128]{2,1,0:T(8,128)(2,1)S(1)} async-done(((bf16[128,64,128]{2,1,0:T(8,128)(2,1)}), bf16[128,64,128]{2,1,0:T(8,128)(2,1)S(1)}, u32[]{:S(2)}, u32[]{:S(2)}) %all-to-all-start) | async-done | bytes 2097184 | tf_op jit(solution)/shard_map/all_to_all | solution.py:252
  123.7 3.1 density.1
  130.1 2.9 collective-permute-start.12
  133.0 4.9 %collective-permute-start.11 = (f32[6,2,24]{2,1,0:T(2,128)S(1)}, f32[6,2,24]{2,1,0:T(2,128)S(1)}, u32[]{:S(2)}, u32[]{:S(2)}) collective-permute-start(f32[6,2,24]{2,1,0:T(2,128)S(1)} %get-tuple-element.30), channel_id=1, source_target_pairs={{0,4},{4,8},{8,12},{12,16},{16,20},{20,24},{24,28},{28,32},{32,36}... | collective-permute-start | bytes 3464 | tf_op jit(solution)/shard_map/ppermute | solution.py:31
  137.9 3.1 collective-permute-done.11
  141.1 4.9 %collective-permute-start.14 = (f32[6,12,2]{2,1,0:T(8,128)S(1)}, f32[6,12,2]{2,1,0:T(8,128)S(1)}, u32[]{:S(2)}, u32[]{:S(2)}) collective-permute-start(f32[6,12,2]{2,1,0:T(8,128)S(1)} %get-tuple-element.29), channel_id=1, source_target_pairs={{1,0},{2,1},{3,2},{0,3},{5,4},{6,5},{7,6},{4,7},{9,8},{10,9},{11,1... | collective-permute-start | bytes 1736 | tf_op jit(solution)/shard_map/ppermute | solution.py:33
  148.6 4.6 %collective-permute-done.13 = f32[6,12,2]{2,1,0:T(8,128)S(1)} collective-permute-done((f32[6,12,2]{2,1,0:T(8,128)S(1)}, f32[6,12,2]{2,1,0:T(8,128)S(1)}, u32[]{:S(2)}, u32[]{:S(2)}) %collective-permute-start.13) | collective-permute-done | bytes 608 | tf_op jit(solution)/shard_map/ppermute | solution.py:31
  153.8 3.1 ham.1
  158.6 13.0 %all-to-all-start.1 = ((f16[128,64,128]{2,1,0:T(8,128)(2,1)}), f16[128,64,128]{2,1,0:T(8,128)(2,1)S(1)}, u32[]{:S(2)}, u32[]{:S(2)}) async-start(f16[128,64,128]{2,1,0:T(8,128)(2,1)} %bitcast.22), calls=%async_computation.1 | async-start | bytes 4194304 | tf_op jit(solution)/shard_map/all_to_all | solution.py:252
  173.5 3.0 collective-permute-start.16
  176.6 4.0 %collective-permute-start.15 = (f32[128,128]{1,0:T(8,128)S(1)}, f32[128,128]{1,0:T(8,128)S(1)}, u32[]{:S(2)}, u32[]{:S(2)}) collective-permute-start(f32[128,128]{1,0:T(8,128)S(1)} %copy-done.4), channel_id=1, source_target_pairs={{0,3},{1,0},{2,1},{3,2},{4,7},{5,4},{6,5},{7,6},{8,11},{9,8},{10,9... | collective-permute-start | bytes 196616 | tf_op jit(solution)/shard_map/ppermute | solution.py:309
  180.6 7.4 %collective-permute-start.8 = (f32[8,128]{1,0:T(8,128)S(1)}, f32[8,128]{1,0:T(8,128)S(1)}, u32[]{:S(2)}, u32[]{:S(2)}) collective-permute-start(f32[8,128]{1,0:T(8,128)S(1)} %get-tuple-element.18), channel_id=1, source_target_pairs={{0,48},{4,52},{8,56},{12,60},{16,32},{20,36},{24,40},{28,44},{32,1... | collective-permute-start | bytes 12296 | tf_op jit(solution)/shard_map/ppermute | solution.py:306
  188.0 7.2 %collective-permute-start.7 = (f32[8,128]{1,0:T(8,128)S(1)}, f32[8,128]{1,0:T(8,128)S(1)}, u32[]{:S(2)}, u32[]{:S(2)}) collective-permute-start(f32[8,128]{1,0:T(8,128)S(1)} %get-tuple-element.18), channel_id=1, source_target_pairs={{0,32},{4,36},{8,40},{12,44},{16,48},{20,52},{24,56},{28,60},{32,0... | collective-permute-start | bytes 12296 | tf_op jit(solution)/shard_map/ppermute | solution.py:306
  195.2 66.7 %collective-permute-done.8 = f32[8,128]{1,0:T(8,128)S(1)} collective-permute-done((f32[8,128]{1,0:T(8,128)S(1)}, f32[8,128]{1,0:T(8,128)S(1)}, u32[]{:S(2)}, u32[]{:S(2)}) %collective-permute-start.8) | collective-permute-done | bytes 4128 | tf_op jit(solution)/shard_map/ppermute | solution.py:306
  261.9 13.4 %collective-permute-start.6 = (f32[8,128]{1,0:T(8,128)S(1)}, f32[8,128]{1,0:T(8,128)S(1)}, u32[]{:S(2)}, u32[]{:S(2)}) collective-permute-start(f32[8,128]{1,0:T(8,128)S(1)} %get-tuple-element.18), channel_id=1, source_target_pairs={{0,16},{4,20},{8,24},{12,28},{16,0},{20,4},{24,8},{28,12},{32,48},... | collective-permute-start | bytes 12296 | tf_op jit(solution)/shard_map/ppermute | solution.py:306
  277.8 8.1 %owner.1 = (s16[4,264,128]{2,1,0:T(8,128)(2,1)S(1)}, s16[1040,128]{1,0:T(8,128)(2,1)S(1)}, s16[1040,128]{1,0:T(8,128)(2,1)S(1)}, s16[1040,128]{1,0:T(8,128)(2,1)S(1)}, s16[1040,128]{1,0:T(8,128)(2,1)S(1)}) custom-call(s32[3]{0:T(128)S(1)} %copy-done.3, s32[16,512]{1,0:T(8,128)S(1)} %bitcast.19, s32[8,16]{1,0:T(8,128)S(1)} %bitcast.21, ...), custom_call_target="tpu_custom_call" | custom-call | tf_op jit(solution)/shard_map/owner/pallas_call | solution.py:314
  285.9 9.1 %all_to_all.20.coded_ref = s16[4,264,128]{2,1,0:T(8,128)(2,1)S(1)} all-to-all(s16[4,264,128]{2,1,0:T(8,128)(2,1)S(1)} %get-tuple-element.11), channel_id=1, replica_groups=mesh['row'=8,'col'=16,'gz'=4] {'gz'}, dimensions={0} | all-to-all | bytes 540672 | tf_op jit(solution)/shard_map/all_to_all | solution.py:252
  295.7 7.3 %all-to-all-start.3 = ((f32[16,16,128]{2,1,0:T(8,128)}), f32[16,16,128]{2,1,0:T(8,128)S(1)}, u32[]{:S(2)}, u32[]{:S(2)}) async-start(f32[16,16,128]{2,1,0:T(8,128)} %bitcast.13), calls=%async_computation.3 | async-start | bytes 262144 | tf_op jit(solution)/shard_map/all_to_all | solution.py:252
  305.5 4.0 %collective-permute-start.19 = (s16[1040,128]{1,0:T(8,128)(2,1)S(1)}, s16[1040,128]{1,0:T(8,128)(2,1)S(1)}, u32[]{:S(2)}, u32[]{:S(2)}) collective-permute-start(s16[1040,128]{1,0:T(8,128)(2,1)S(1)} %get-tuple-element.9), channel_id=1, source_target_pairs={{0,2},{1,3},{2,0},{3,1},{4,6},{5,7},{6,4},{7,5},{8,10},{9,11},{10,... | collective-permute-start | bytes 798728 | tf_op jit(solution)/shard_map/ppermute | solution.py:330
  309.5 3.1 collective-permute-start.20
  312.5 4.8 %collective-permute-done.18.coded1_ref = s16[1040,128]{1,0:T(8,128)(2,1)S(1)} collective-permute-done((s16[1040,128]{1,0:T(8,128)(2,1)S(1)}, s16[1040,128]{1,0:T(8,128)(2,1)S(1)}, u32[]{:S(2)}, u32[]{:S(2)}) %collective-permute-start.18) | collective-permute-done | bytes 266272 | tf_op jit(solution)/shard_map/ppermute | solution.py:330
  317.3 2.5 collective-permute-done.20.coded3_ref
  (59 shorter events, 23.7 us)
Async XLA Ops:
  7.8 20.0 %copy-start = (bf16[1,1,1,1024,384]{4,3,2,1,0:T(8,128)(2,1)S(1)}, bf16[1,1,1,1024,384]{4,3,2,1,0:T(8,128)(2,1)}, u32[]{:S(2)}) copy-start(bf16[1,1,1,1024,384]{4,3,2,1,0:T(8,128)(2,1)} %param.9) | copy-start | bytes 2359300
  7.8 115.9 %all-to-all-start = ((bf16[128,64,128]{2,1,0:T(8,128)(2,1)}), bf16[128,64,128]{2,1,0:T(8,128)(2,1)S(1)}, u32[]{:S(2)}, u32[]{:S(2)}) async-start(bf16[128,64,128]{2,1,0:T(8,128)(2,1)} %pack.1), calls=%async_computation | async-start | bytes 4194304 | tf_op jit(solution)/shard_map/all_to_all | solution.py:252
  27.8 99.1 %copy-start.5 = (f32[2,8,24]{2,1,0:T(8,128)S(1)}, f32[2,8,24]{2,1,0:T(8,128)}, u32[]{:S(2)}) copy-start(f32[2,8,24]{2,1,0:T(8,128)} %param.10) | copy-start | bytes 4612
  29.2 3.1 collective-permute-start
  32.2 5.5 %collective-permute-start.1 = (f32[8,128]{1,0:T(8,128)S(1)}, f32[8,128]{1,0:T(8,128)S(1)}, u32[]{:S(2)}, u32[]{:S(2)}) collective-permute-start(f32[8,128]{1,0:T(8,128)S(1)} %broadcast_maximum_fusion), channel_id=1, source_target_pairs={{0,128},{64,192},{128,0},{192,64},{256,384},{320,448},{384,256},{4... | collective-permute-start | bytes 12296 | tf_op jit(solution)/shard_map/ppermute | solution.py:273
  37.7 7.0 %collective-permute-start.2 = (f32[8,128]{1,0:T(8,128)S(1)}, f32[8,128]{1,0:T(8,128)S(1)}, u32[]{:S(2)}, u32[]{:S(2)}) collective-permute-start(f32[8,128]{1,0:T(8,128)S(1)} %fusion.24), channel_id=1, source_target_pairs={{0,256},{64,320},{128,384},{192,448},{256,0},{320,64},{384,128},{4... | collective-permute-start | bytes 12296 | tf_op jit(solution)/shard_map/ppermute | solution.py:273
  44.8 71.2 %collective-permute-start.5 = (f32[8,128]{1,0:T(8,128)S(1)}, f32[8,128]{1,0:T(8,128)S(1)}, u32[]{:S(2)}, u32[]{:S(2)}) collective-permute-start(f32[8,128]{1,0:T(8,128)S(1)} %max.32), channel_id=1, source_target_pairs={{0,12},{4,8},{8,4},{12,0},{16,28},{20,24},{24,20},{28,16},{32,44},... | collective-permute-start | bytes 12296 | tf_op jit(solution)/shard_map/ppermute | solution.py:277
  50.0 68.5 %collective-permute-start.4 = (f32[8,128]{1,0:T(8,128)S(1)}, f32[8,128]{1,0:T(8,128)S(1)}, u32[]{:S(2)}, u32[]{:S(2)}) collective-permute-start(f32[8,128]{1,0:T(8,128)S(1)} %max.32), channel_id=1, source_target_pairs={{0,8},{4,12},{8,0},{12,4},{16,24},{20,28},{24,16},{28,20},{32,40},... | collective-permute-start | bytes 12296 | tf_op jit(solution)/shard_map/ppermute | solution.py:277
  51.9 66.7 %collective-permute-start.3 = (f32[8,128]{1,0:T(8,128)S(1)}, f32[8,128]{1,0:T(8,128)S(1)}, u32[]{:S(2)}, u32[]{:S(2)}) collective-permute-start(f32[8,128]{1,0:T(8,128)S(1)} %max.32), channel_id=1, source_target_pairs={{0,4},{4,0},{8,12},{12,8},{16,20},{20,16},{24,28},{28,24},{32,36},... | collective-permute-start | bytes 12296 | tf_op jit(solution)/shard_map/ppermute | solution.py:277
  126.9 1.4 collective-permute-start.10
  127.0 3.1 collective-permute-start.9
  130.1 7.8 %collective-permute-start.12 = (f32[6,2,24]{2,1,0:T(2,128)S(1)}, f32[6,2,24]{2,1,0:T(2,128)S(1)}, u32[]{:S(2)}, u32[]{:S(2)}) collective-permute-start(f32[6,2,24]{2,1,0:T(2,128)S(1)} %get-tuple-element.31), channel_id=1, source_target_pairs={{4,0},{8,4},{12,8},{16,12},{20,16},{24,20},{28,24},{32,28},{36,32}... | collective-permute-start | bytes 3464 | tf_op jit(solution)/shard_map/ppermute | solution.py:33
  133.0 8.0 %collective-permute-start.11 = (f32[6,2,24]{2,1,0:T(2,128)S(1)}, f32[6,2,24]{2,1,0:T(2,128)S(1)}, u32[]{:S(2)}, u32[]{:S(2)}) collective-permute-start(f32[6,2,24]{2,1,0:T(2,128)S(1)} %get-tuple-element.30), channel_id=1, source_target_pairs={{0,4},{4,8},{8,12},{12,16},{16,20},{20,24},{24,28},{28,32},{32,36}... | collective-permute-start | bytes 3464 | tf_op jit(solution)/shard_map/ppermute | solution.py:31
  141.1 7.5 %collective-permute-start.14 = (f32[6,12,2]{2,1,0:T(8,128)S(1)}, f32[6,12,2]{2,1,0:T(8,128)S(1)}, u32[]{:S(2)}, u32[]{:S(2)}) collective-permute-start(f32[6,12,2]{2,1,0:T(8,128)S(1)} %get-tuple-element.29), channel_id=1, source_target_pairs={{1,0},{2,1},{3,2},{0,3},{5,4},{6,5},{7,6},{4,7},{9,8},{10,9},{11,1... | collective-permute-start | bytes 1736 | tf_op jit(solution)/shard_map/ppermute | solution.py:33
  146.0 7.2 %collective-permute-start.13 = (f32[6,12,2]{2,1,0:T(8,128)S(1)}, f32[6,12,2]{2,1,0:T(8,128)S(1)}, u32[]{:S(2)}, u32[]{:S(2)}) collective-permute-start(f32[6,12,2]{2,1,0:T(8,128)S(1)} %get-tuple-element.28), channel_id=1, source_target_pairs={{0,1},{1,2},{2,3},{3,0},{4,5},{5,6},{6,7},{7,4},{8,9},{9,10},{10,1... | collective-permute-start | bytes 1736 | tf_op jit(solution)/shard_map/ppermute | solution.py:31
  158.6 13.0 %copy-start.4 = (f32[128,128]{1,0:T(8,128)S(1)}, f32[128,128]{1,0:T(8,128)}, u32[]{:S(2)}) copy-start(f32[128,128]{1,0:T(8,128)} %param.11) | copy-start | bytes 196612
  158.6 118.5 %all-to-all-start.1 = ((f16[128,64,128]{2,1,0:T(8,128)(2,1)}), f16[128,64,128]{2,1,0:T(8,128)(2,1)S(1)}, u32[]{:S(2)}, u32[]{:S(2)}) async-start(f16[128,64,128]{2,1,0:T(8,128)(2,1)} %bitcast.22), calls=%async_computation.1 | async-start | bytes 4194304 | tf_op jit(solution)/shard_map/all_to_all | solution.py:252
  171.6 105.4 %collective-permute-start.17 = (f32[128,128]{1,0:T(8,128)S(1)}, f32[128,128]{1,0:T(8,128)S(1)}, u32[]{:S(2)}, u32[]{:S(2)}) collective-permute-start(f32[128,128]{1,0:T(8,128)S(1)} %copy-done.4), channel_id=1, source_target_pairs={{0,1},{1,2},{2,3},{3,0},{4,5},{5,6},{6,7},{7,4},{8,9},{9,10},{10,1... | collective-permute-start | bytes 196616 | tf_op jit(solution)/shard_map/ppermute | solution.py:309
  173.5 103.4 %collective-permute-start.16 = (f32[128,128]{1,0:T(8,128)S(1)}, f32[128,128]{1,0:T(8,128)S(1)}, u32[]{:S(2)}, u32[]{:S(2)}) collective-permute-start(f32[128,128]{1,0:T(8,128)S(1)} %copy-done.4), channel_id=1, source_target_pairs={{0,2},{1,3},{2,0},{3,1},{4,6},{5,7},{6,4},{7,5},{8,10},{9,11},{10,... | collective-permute-start | bytes 196616 | tf_op jit(solution)/shard_map/ppermute | solution.py:309
  176.6 100.4 %collective-permute-start.15 = (f32[128,128]{1,0:T(8,128)S(1)}, f32[128,128]{1,0:T(8,128)S(1)}, u32[]{:S(2)}, u32[]{:S(2)}) collective-permute-start(f32[128,128]{1,0:T(8,128)S(1)} %copy-done.4), channel_id=1, source_target_pairs={{0,3},{1,0},{2,1},{3,2},{4,7},{5,4},{6,5},{7,6},{8,11},{9,8},{10,9... | collective-permute-start | bytes 196616 | tf_op jit(solution)/shard_map/ppermute | solution.py:309
  180.6 81.3 %collective-permute-start.8 = (f32[8,128]{1,0:T(8,128)S(1)}, f32[8,128]{1,0:T(8,128)S(1)}, u32[]{:S(2)}, u32[]{:S(2)}) collective-permute-start(f32[8,128]{1,0:T(8,128)S(1)} %get-tuple-element.18), channel_id=1, source_target_pairs={{0,48},{4,52},{8,56},{12,60},{16,32},{20,36},{24,40},{28,44},{32,1... | collective-permute-start | bytes 12296 | tf_op jit(solution)/shard_map/ppermute | solution.py:306
  188.0 87.3 %collective-permute-start.7 = (f32[8,128]{1,0:T(8,128)S(1)}, f32[8,128]{1,0:T(8,128)S(1)}, u32[]{:S(2)}, u32[]{:S(2)}) collective-permute-start(f32[8,128]{1,0:T(8,128)S(1)} %get-tuple-element.18), channel_id=1, source_target_pairs={{0,32},{4,36},{8,40},{12,44},{16,48},{20,52},{24,56},{28,60},{32,0... | collective-permute-start | bytes 12296 | tf_op jit(solution)/shard_map/ppermute | solution.py:306
  261.9 14.9 %collective-permute-start.6 = (f32[8,128]{1,0:T(8,128)S(1)}, f32[8,128]{1,0:T(8,128)S(1)}, u32[]{:S(2)}, u32[]{:S(2)}) collective-permute-start(f32[8,128]{1,0:T(8,128)S(1)} %get-tuple-element.18), channel_id=1, source_target_pairs={{0,16},{4,20},{8,24},{12,28},{16,0},{20,4},{24,8},{28,12},{32,48},... | collective-permute-start | bytes 12296 | tf_op jit(solution)/shard_map/ppermute | solution.py:306
  277.0 0.8 copy-start.1
  277.0 0.8 copy-start.2
  277.0 0.7 copy-start.3
  295.7 25.3 %all-to-all-start.3 = ((f32[16,16,128]{2,1,0:T(8,128)}), f32[16,16,128]{2,1,0:T(8,128)S(1)}, u32[]{:S(2)}, u32[]{:S(2)}) async-start(f32[16,16,128]{2,1,0:T(8,128)} %bitcast.13), calls=%async_computation.3 | async-start | bytes 262144 | tf_op jit(solution)/shard_map/all_to_all | solution.py:252
  303.0 14.3 %collective-permute-start.18 = (s16[1040,128]{1,0:T(8,128)(2,1)S(1)}, s16[1040,128]{1,0:T(8,128)(2,1)S(1)}, u32[]{:S(2)}, u32[]{:S(2)}) collective-permute-start(s16[1040,128]{1,0:T(8,128)(2,1)S(1)} %get-tuple-element.8), channel_id=1, source_target_pairs={{0,1},{1,2},{2,3},{3,0},{4,5},{5,6},{6,7},{7,4},{8,9},{9,10},{10,1... | collective-permute-start | bytes 798728 | tf_op jit(solution)/shard_map/ppermute | solution.py:330
  305.5 11.8 %collective-permute-start.19 = (s16[1040,128]{1,0:T(8,128)(2,1)S(1)}, s16[1040,128]{1,0:T(8,128)(2,1)S(1)}, u32[]{:S(2)}, u32[]{:S(2)}) collective-permute-start(s16[1040,128]{1,0:T(8,128)(2,1)S(1)} %get-tuple-element.9), channel_id=1, source_target_pairs={{0,2},{1,3},{2,0},{3,1},{4,6},{5,7},{6,4},{7,5},{8,10},{9,11},{10,... | collective-permute-start | bytes 798728 | tf_op jit(solution)/shard_map/ppermute | solution.py:330
  309.5 10.4 %collective-permute-start.20 = (s16[1040,128]{1,0:T(8,128)(2,1)S(1)}, s16[1040,128]{1,0:T(8,128)(2,1)S(1)}, u32[]{:S(2)}, u32[]{:S(2)}) collective-permute-start(s16[1040,128]{1,0:T(8,128)(2,1)S(1)} %get-tuple-element.10), channel_id=1, source_target_pairs={{0,3},{1,0},{2,1},{3,2},{4,7},{5,4},{6,5},{7,6},{8,11},{9,8},{10,9... | collective-permute-start | bytes 798728 | tf_op jit(solution)/shard_map/ppermute | solution.py:330

commit v4 on v3

--- a/solution.py
+++ b/solution.py
@@ -19,6 +19,7 @@
 MIB = 1024 * 1024
 PAGES = 16
 SCALES = 16
+LEVELS = 32760.0
 
 
 def with_halo(cells, sides, width):
@@ -83,70 +84,75 @@
     return jnp.where(lane < BS, low, high)
 
 
-def pack_kernel(ids_ref, lists_ref, pattern_ref, matrix_ref, out_ref, held):
+def pack_kernel(ids_ref, lists_ref, pattern_ref, matrix_ref, out_ref, pages_ref, held):
     def turn(q, carry):
         rows = pl.ds(pl.multiple_of(q * 128, 128), 128)
+        first = (q < 4).astype(jnp.float32)
         for m in range(4):
             block = matrix_ref[rows, 128 * m : 128 * m + 128].T
             for half in range(2):
                 b = 2 * m + half
-                keep = lane_pair(
-                    pattern_ref[b, 2 * q].astype(jnp.float32),
-                    pattern_ref[b, 2 * q + 1].astype(jnp.float32),
-                    BS,
-                ).astype(jnp.bfloat16)
-                kept = block[BS * half : BS * half + BS] * keep
-                held[0, b, q] = kept
-                held[1, b, q] = pltpu.roll(kept, BS, 1)
+                low = pattern_ref[b, 2 * q].astype(jnp.float32)
+                high = pattern_ref[b, 2 * q + 1].astype(jnp.float32)
+                part = block[BS * half : BS * half + BS]
+                straight = lane_pair(low * first, high * (1.0 - first), BS).astype(jnp.bfloat16)
+                crossed = lane_pair(low * (1.0 - first), high * first, BS).astype(jnp.bfloat16)
+                held[b * 8 + q] = part * straight
+                held[64 + b * 8 + q] = pltpu.roll(part * crossed, BS, 1)
         return carry
 
     lax.fori_loop(0, 8, turn, 0)
 
     def fill(t, carry):
         a0, a1, b = listed_pair(ids_ref, lists_ref, t)
-        out_ref[t, :, 0:BS] = held[a0 & 1, b, a0 >> 1, :, 0:BS]
-        out_ref[t, :, BS:128] = held[1 - (a1 & 1), b, a1 >> 1, :, BS:128]
+        page0 = (a0 & 1) * 64 + b * 8 + (a0 >> 1)
+        page1 = (1 - (a1 & 1)) * 64 + b * 8 + (a1 >> 1)
+        pages_ref[t] = page0
+        pages_ref[128 + t] = page1
+        out_ref[t] = held[page0] + held[page1]
         return carry
 
     lax.fori_loop(0, 128, fill, 0, unroll=4)
 
 
 def density_kernel(blocks_ref, phi_ref, unit_ref, out_ref):
-    phi = phi_ref[...]
-
     def part(n, total):
-        rows = pl.ds(pl.multiple_of(n * 128, 128), 128)
+        rows = pl.ds(pl.multiple_of(n * 256, 256), 256)
         left = jnp.concatenate([blocks_ref[r, rows, :] for r in range(8)], axis=1)
-        product = jnp.dot(left, phi, preferred_element_type=jnp.float32)
+        product = jnp.dot(left, phi_ref[...], preferred_element_type=jnp.float32)
         return total + jnp.sum(phi_ref[rows, :].astype(jnp.float32) * product, axis=0, keepdims=True)
 
-    out_ref[...] = lax.fori_loop(0, 8, part, jnp.zeros((1, 384), jnp.float32))
+    out_ref[...] = lax.fori_loop(0, 4, part, jnp.zeros((1, 384), jnp.float32))
 
 
 def ham_kernel(scale_ref, phi_ref, field_ref, out_ref):
-    phi = phi_ref[...]
-
     def part(r, carry):
-        rows = phi_ref[pl.ds(pl.multiple_of(r * 128, 128), 128), :].astype(jnp.float32)
+        rows = phi_ref[pl.ds(pl.multiple_of(r * 256, 256), 256), :].astype(jnp.float32)
         weighted = (rows * field_ref[...]).astype(jnp.bfloat16)
-        block = lax.dot_general(phi, weighted, (((1,), (1,)), ((), ())), preferred_element_type=jnp.float32)
-        out_ref[r] = block * scale_ref[0]
-        return carry
-
-    lax.fori_loop(0, 8, part, 0)
+        block = lax.dot_general(
+            phi_ref[...], weighted, (((1,), (1,)), ((), ())), preferred_element_type=jnp.float32
+        )
+        out_ref[2 * r] = block[:, 0:128] * scale_ref[0]
+        out_ref[2 * r + 1] = block[:, 128:256] * scale_ref[0]
+        return carry
+
+    lax.fori_loop(0, 4, part, 0)
 
 
 def coded(page):
     largest = jnp.max(jnp.abs(page), axis=0, keepdims=True)
-    power = jnp.floor(jnp.log2(jnp.maximum(largest, 1e-30))) + 1.0
-    power = jnp.clip(power, -90.0, 90.0)
-    levels = jnp.clip(jnp.round(page * jnp.exp2(15.0 - power)), -32767.0, 32767.0)
+    power = jnp.floor(jnp.log2(jnp.clip(largest, 1e-27, 1e27))) + 1.0
+    levels = jnp.round(page * (jnp.exp2(-power) * LEVELS))
     return levels.astype(jnp.int32).astype(jnp.int16), power
+
+
+def step_of(power):
+    return jnp.exp2(power.astype(jnp.float32)) * (1.0 / LEVELS)
 
 
 def owner_kernel(
     ids_ref,
-    lists_ref,
+    pages_ref,
     pattern_ref,
     scale_ref,
     blocks_ref,
@@ -157,6 +163,7 @@
     out2_ref,
     out3_ref,
     sums,
+    factors,
     turned,
     powers,
     products,
@@ -164,37 +171,42 @@
     sums[...] = jnp.zeros_like(sums)
 
     def add(t, carry):
-        a0, a1, b = listed_pair(ids_ref, lists_ref, t)
+        page0, page1 = pages_ref[t], pages_ref[128 + t]
         block = blocks_ref[t] * scale_ref[8 * (((t & 15) ^ ids_ref[1]) >> 2)]
-        sums[a0 & 1, b, a0 >> 1, :, 0:BS] += block[:, 0:BS]
-        sums[1 - (a1 & 1), b, a1 >> 1, :, BS:128] += block[:, BS:128]
+        sums[page0] += block
+        sums[page1] += block
         return carry
 
     lax.fori_loop(0, 128, add, 0, unroll=4)
     outs = (out0_ref, out1_ref, out2_ref, out3_ref)
 
+    orbitals = orbitals_ref[...]
+    orbitals_high = orbitals.astype(jnp.bfloat16)
+    orbitals_low = (orbitals - orbitals_high.astype(jnp.float32)).astype(jnp.bfloat16)
+    factors[...] = jnp.concatenate([orbitals_high, orbitals_high, orbitals_low], axis=1)
+
     def finish(q, carry):
+        first = (q < 4).astype(jnp.float32)
         for n, out in enumerate(outs):
             peer = lax.rem(ids_ref[2] + n, 4)
             for half in range(2):
                 b = 2 * peer + half
-                keep = lane_pair(
-                    pattern_ref[b, 2 * q].astype(jnp.float32), pattern_ref[b, 2 * q + 1].astype(jnp.float32), BS
-                )
-                page = (sums[0, b, q] + pltpu.roll(sums[1, b, q], BS, 1)) * keep
+                low = pattern_ref[b, 2 * q].astype(jnp.float32)
+                high = pattern_ref[b, 2 * q + 1].astype(jnp.float32)
+                straight = lane_pair(low * first, high * (1.0 - first), BS)
+                crossed = lane_pair(high * first, low * (1.0 - first), BS)
+                page = sums[b * 8 + q] * straight + pltpu.roll(sums[64 + b * 8 + q] * crossed, BS, 1)
+                page_high = page.astype(jnp.bfloat16)
+                page_low = (page - page_high.astype(jnp.float32)).astype(jnp.bfloat16)
                 place = 2 * n + half
-                turned[BS * place : BS * place + BS, :] = page
+                turned[BS * place : BS * place + BS, :] = page_high
+                turned[512 + BS * place : 512 + BS * place + BS, :] = page_low
+                turned[1024 + BS * place : 1024 + BS * place + BS, :] = page_high
                 levels, power = coded(page)
                 place = half * 8 + q
                 out[pl.ds(pl.multiple_of(place * BS, BS), BS), :] = levels
                 powers[n, pl.ds(place, 1), :] = power
-        part = lax.dot_general(
-            turned[...],
-            orbitals_ref[...].reshape(512, 128),
-            (((0,), (0,)), ((), ())),
-            precision=lax.Precision.HIGHEST,
-            preferred_element_type=jnp.float32,
-        )
+        part = jnp.dot(factors[...], turned[...], preferred_element_type=jnp.float32).T
         for half in range(2):
             for g in range(4):
                 start = BS * half + 16 * g
@@ -218,7 +230,7 @@
 
 def term_kernel(coded_ref, out_ref):
     steps = [
-        jnp.exp2(coded_ref[g, 4 * BS : 4 * BS + 8, :].astype(jnp.float32) - 15.0) for g in range(4)
+        step_of(coded_ref[g, 4 * BS : 4 * BS + 8, :]) for g in range(4)
     ]
     for n in range(4):
         total = jnp.zeros((BS, 128), jnp.float32)
@@ -230,7 +242,7 @@
 
 def share_kernel(coded0_ref, coded1_ref, coded2_ref, coded3_ref, out_ref):
     parts = (coded0_ref, coded1_ref, coded2_ref, coded3_ref)
-    steps = [jnp.exp2(part[PAGES * BS : PAGES * BS + SCALES, :].astype(jnp.float32) - 15.0) for part in parts]
+    steps = [step_of(part[PAGES * BS : PAGES * BS + SCALES, :]) for part in parts]
     for q in range(8):
         halves = []
         for half in range(2):
@@ -258,12 +270,15 @@
     pattern = block_pattern.T
     phi = basis_values.reshape(1024, 384)
 
-    outgoing = pl.pallas_call(
+    outgoing, page_table = pl.pallas_call(
         pack_kernel,
-        out_shape=jax.ShapeDtypeStruct((128, BS, 128), jnp.bfloat16),
+        out_shape=[
+            jax.ShapeDtypeStruct((128, BS, 128), jnp.bfloat16),
+            jax.ShapeDtypeStruct((256,), jnp.int32),
+        ],
         in_specs=[smem, smem, smem, vmem],
-        out_specs=vmem,
-        scratch_shapes=[pltpu.VMEM((2, 8, 8, BS, 128), jnp.bfloat16)],
+        out_specs=[vmem, smem],
+        scratch_shapes=[pltpu.VMEM((128, BS, 128), jnp.bfloat16)],
         name="pack",
     )(ids, lists, pattern, density_matrix)
     incoming = exchange(outgoing, PLANE)
@@ -308,7 +323,7 @@
     for step in range(1, 4):
         columns.append(lax.ppermute(orbitals, "gz", [(i, (i - step) % 4) for i in range(4)]))
     units = jnp.square(jnp.concatenate(peaks, axis=0)[:, 0])
-    all_orbitals = jnp.stack(columns)
+    all_orbitals = jnp.concatenate(columns, axis=0).T
 
     page_shape = jax.ShapeDtypeStruct((PAGES * BS + SCALES, 128), jnp.int16)
     terms, *pages = pl.pallas_call(
@@ -317,14 +332,15 @@
         in_specs=[smem, smem, smem, smem, vmem, vmem],
         out_specs=[vmem] * 5,
         scratch_shapes=[
-            pltpu.VMEM((2, 8, 8, BS, 128), jnp.float32),
-            pltpu.VMEM((512, 128), jnp.float32),
+            pltpu.VMEM((128, BS, 128), jnp.float32),
+            pltpu.VMEM((128, 1536), jnp.bfloat16),
+            pltpu.VMEM((1536, 128), jnp.bfloat16),
             pltpu.VMEM((4, SCALES, 128), jnp.float32),
             pltpu.VMEM((4, 256, 128), jnp.float32),
         ],
         compiler_params=pltpu.CompilerParams(vmem_limit_bytes=24 * MIB),
         name="owner",
-    )(ids, lists, pattern, units, arrived, all_orbitals)
+    )(ids, page_table, pattern, units, arrived, all_orbitals)
     terms = exchange(terms, "gz")
     for step in range(1, 4):
         pages[step] = lax.ppermute(pages[step], "gz", [(i, (i + step) % 4) for i in range(4)])

time: 323 us -> 319 us (0.988)
  Pallas kernels: 22.7 us -> 18.9 us
where the time goes in v4:
time: 319 us; the launch traced here: 318 us
  waiting for transfers between devices  161 us (50%)
  starting transfers between devices  120 us (38%)
  Pallas kernels  18.9 us (6%)
  blocking collectives  9.11 us (3%)
  other arithmetic  4.72 us (1%)
    ppermute x6, waiting for transfers between devices, shards(): lax.ppermute(largest, 'col', [(i, i ^ step) for i in range(16)])  132 us
    all_to_all x3, starting transfers between devices, exchange(): return lax.all_to_all(array, axes, 0, 0, tiled=True)  40.4 us
    ppermute x6, starting transfers between devices, shards(): lax.ppermute(largest, 'col', [(i, i ^ step) for i in range(16)])  38.1 us
    ppermute x3, starting transfers between devices, shards(): lax.ppermute(pages[step], 'gz', [(i, (i + step) % 4) for i in range(4)])  9.51 us
    ppermute x3, waiting for transfers between devices, with_halo(): lax.ppermute(tail, axis, [(i, (i + 1) % count) for i in range(count)])  9.42 us
    all_to_all x1, blocking collectives, exchange(): return lax.all_to_all(array, axes, 0, 0, tiled=True)  9.11 us
    ppermute x3, starting transfers between devices, shards(): lax.ppermute(orbitals, 'gz', [(i, (i - step) % 4) for i in range(4)])  8.97 us
    ppermute x3, starting transfers between devices, with_halo(): lax.ppermute(head, axis, [((i + 1) % count, i) for i in range(count)])  7.87 us
  transfers between devices with their start and end apart: 24, of which 15 were waited for; matrix products, arithmetic and copies ran while one was open for 1% of the time, Pallas kernels for 0%

profile of v4, /device:TPU:6, one launch (start us, length us, event | category | flops | bytes accessed | tf_op | source)
XLA Modules:
  0.0 317.8 jit_solution(11994959533852058147)
XLA Ops:
  1.2 6.4 %pack.1 = (bf16[128,64,128]{2,1,0:T(8,128)(2,1)}, s32[256]{0:T(256)}) custom-call(s32[3]{0:T(128)} %pad_add_fusion.ids_ref, s32[16,512]{1,0:T(8,128)} %bitcast.19, s32[8,16]{1,0:T(8,128)} %bitcast.16, bf16[1024,512]{1,0:T(8,128)(2,1)} %matrix_ref.1), custom_call_target="tpu_custom_call" | custom-call | tf_op jit(solution)/shard_map/pack/pallas_call | solution.py:273
  7.6 20.0 %all-to-all-start = ((bf16[128,64,128]{2,1,0:T(8,128)(2,1)}), bf16[128,64,128]{2,1,0:T(8,128)(2,1)S(1)}, u32[]{:S(2)}, u32[]{:S(2)}) async-start(bf16[128,64,128]{2,1,0:T(8,128)(2,1)} %get-tuple-element.10), calls=%async_computation | async-start | bytes 4194304 | tf_op jit(solution)/shard_map/all_to_all | solution.py:264
  32.1 2.5 collective-permute-start.1
  34.7 2.9 collective-permute-done.1
  37.6 2.9 collective-permute-start.2
  40.6 4.1 %collective-permute-done.2 = f32[8,128]{1,0:T(8,128)S(1)} collective-permute-done((f32[8,128]{1,0:T(8,128)S(1)}, f32[8,128]{1,0:T(8,128)S(1)}, u32[]{:S(2)}, u32[]{:S(2)}) %collective-permute-start.2) | collective-permute-done | bytes 4128 | tf_op jit(solution)/shard_map/ppermute | solution.py:288
  44.6 5.2 %collective-permute-start.5 = (f32[8,128]{1,0:T(8,128)S(1)}, f32[8,128]{1,0:T(8,128)S(1)}, u32[]{:S(2)}, u32[]{:S(2)}) collective-permute-start(f32[8,128]{1,0:T(8,128)S(1)} %max.32), channel_id=1, source_target_pairs={{0,12},{4,8},{8,4},{12,0},{16,28},{20,24},{24,20},{28,16},{32,44},... | collective-permute-start | bytes 12296 | tf_op jit(solution)/shard_map/ppermute | solution.py:292
  51.8 3.0 collective-permute-start.3
  54.8 61.1 %collective-permute-done.5 = f32[8,128]{1,0:T(8,128)S(1)} collective-permute-done((f32[8,128]{1,0:T(8,128)S(1)}, f32[8,128]{1,0:T(8,128)S(1)}, u32[]{:S(2)}, u32[]{:S(2)}) %collective-permute-start.5) | collective-permute-done | bytes 4128 | tf_op jit(solution)/shard_map/ppermute | solution.py:292
  115.8 2.5 collective-permute-done.4
  119.0 4.5 %all-to-all-done = bf16[128,64,128]{2,1,0:T(8,128)(2,1)S(1)} async-done(((bf16[128,64,128]{2,1,0:T(8,128)(2,1)}), bf16[128,64,128]{2,1,0:T(8,128)(2,1)S(1)}, u32[]{:S(2)}, u32[]{:S(2)}) %all-to-all-start) | async-done | bytes 2097184 | tf_op jit(solution)/shard_map/all_to_all | solution.py:264
  123.5 2.4 density.1
  129.2 2.9 collective-permute-start.12
  132.2 4.9 %collective-permute-start.11 = (f32[6,2,24]{2,1,0:T(2,128)S(1)}, f32[6,2,24]{2,1,0:T(2,128)S(1)}, u32[]{:S(2)}, u32[]{:S(2)}) collective-permute-start(f32[6,2,24]{2,1,0:T(2,128)S(1)} %get-tuple-element.34), channel_id=1, source_target_pairs={{0,4},{4,8},{8,12},{12,16},{16,20},{20,24},{24,28},{28,32},{32,36}... | collective-permute-start | bytes 3464 | tf_op jit(solution)/shard_map/ppermute | solution.py:32
  137.0 3.1 collective-permute-done.11
  140.3 4.9 %collective-permute-start.14 = (f32[6,12,2]{2,1,0:T(8,128)S(1)}, f32[6,12,2]{2,1,0:T(8,128)S(1)}, u32[]{:S(2)}, u32[]{:S(2)}) collective-permute-start(f32[6,12,2]{2,1,0:T(8,128)S(1)} %get-tuple-element.33), channel_id=1, source_target_pairs={{1,0},{2,1},{3,2},{0,3},{5,4},{6,5},{7,6},{4,7},{9,8},{10,9},{11,1... | collective-permute-start | bytes 1736 | tf_op jit(solution)/shard_map/ppermute | solution.py:34
  147.8 4.6 %collective-permute-done.13 = f32[6,12,2]{2,1,0:T(8,128)S(1)} collective-permute-done((f32[6,12,2]{2,1,0:T(8,128)S(1)}, f32[6,12,2]{2,1,0:T(8,128)S(1)}, u32[]{:S(2)}, u32[]{:S(2)}) %collective-permute-start.13) | collective-permute-done | bytes 608 | tf_op jit(solution)/shard_map/ppermute | solution.py:32
  156.5 13.0 %all-to-all-start.1 = ((f16[128,64,128]{2,1,0:T(8,128)(2,1)}), f16[128,64,128]{2,1,0:T(8,128)(2,1)S(1)}, u32[]{:S(2)}, u32[]{:S(2)}) async-start(f16[128,64,128]{2,1,0:T(8,128)(2,1)} %bitcast.18), calls=%async_computation.1 | async-start | bytes 4194304 | tf_op jit(solution)/shard_map/all_to_all | solution.py:264
  171.5 3.0 collective-permute-start.16
  174.6 4.0 %collective-permute-start.15 = (f32[128,128]{0,1:T(8,128)S(1)}, f32[128,128]{0,1:T(8,128)S(1)}, u32[]{:S(2)}, u32[]{:S(2)}) collective-permute-start(f32[128,128]{0,1:T(8,128)S(1)} %copy.19), channel_id=1, source_target_pairs={{0,3},{1,0},{2,1},{3,2},{4,7},{5,4},{6,5},{7,6},{8,11},{9,8},{10,9... | collective-permute-start | bytes 196616 | tf_op jit(solution)/shard_map/ppermute | solution.py:324
  178.6 7.4 %collective-permute-start.8 = (f32[8,128]{1,0:T(8,128)S(1)}, f32[8,128]{1,0:T(8,128)S(1)}, u32[]{:S(2)}, u32[]{:S(2)}) collective-permute-start(f32[8,128]{1,0:T(8,128)S(1)} %get-tuple-element.22), channel_id=1, source_target_pairs={{0,48},{4,52},{8,56},{12,60},{16,32},{20,36},{24,40},{28,44},{32,1... | collective-permute-start | bytes 12296 | tf_op jit(solution)/shard_map/ppermute | solution.py:321
  186.0 7.2 %collective-permute-start.7 = (f32[8,128]{1,0:T(8,128)S(1)}, f32[8,128]{1,0:T(8,128)S(1)}, u32[]{:S(2)}, u32[]{:S(2)}) collective-permute-start(f32[8,128]{1,0:T(8,128)S(1)} %get-tuple-element.22), channel_id=1, source_target_pairs={{0,32},{4,36},{8,40},{12,44},{16,48},{20,52},{24,56},{28,60},{32,0... | collective-permute-start | bytes 12296 | tf_op jit(solution)/shard_map/ppermute | solution.py:321
  193.2 66.6 %collective-permute-done.8 = f32[8,128]{1,0:T(8,128)S(1)} collective-permute-done((f32[8,128]{1,0:T(8,128)S(1)}, f32[8,128]{1,0:T(8,128)S(1)}, u32[]{:S(2)}, u32[]{:S(2)}) %collective-permute-start.8) | collective-permute-done | bytes 4128 | tf_op jit(solution)/shard_map/ppermute | solution.py:321
  259.8 13.4 %collective-permute-start.6 = (f32[8,128]{1,0:T(8,128)S(1)}, f32[8,128]{1,0:T(8,128)S(1)}, u32[]{:S(2)}, u32[]{:S(2)}) collective-permute-start(f32[8,128]{1,0:T(8,128)S(1)} %get-tuple-element.22), channel_id=1, source_target_pairs={{0,16},{4,20},{8,24},{12,28},{16,0},{20,4},{24,8},{28,12},{32,48},... | collective-permute-start | bytes 12296 | tf_op jit(solution)/shard_map/ppermute | solution.py:321
  275.6 6.4 %owner.1 = (s16[4,264,128]{2,1,0:T(8,128)(2,1)S(1)}, s16[1040,128]{1,0:T(8,128)(2,1)S(1)}, s16[1040,128]{1,0:T(8,128)(2,1)S(1)}, s16[1040,128]{1,0:T(8,128)(2,1)S(1)}, s16[1040,128]{1,0:T(8,128)(2,1)S(1)}) custom-call(s32[3]{0:T(128)S(1)} %copy-done.2, s32[256]{0:T(256)S(1)} %copy-done.3, s32[8,16]{1,0:T(8,128)S(1)} %bitcast.17, f32[32]{0:T(128)S(1)} %fusion.5.scale_ref, ...), custom_call_target="tpu_custom_call" | custom-call | tf_op jit(solution)/shard_map/owner/pallas_call | solution.py:329
  282.0 9.1 %all_to_all.20.coded_ref = s16[4,264,128]{2,1,0:T(8,128)(2,1)S(1)} all-to-all(s16[4,264,128]{2,1,0:T(8,128)(2,1)S(1)} %get-tuple-element.15), channel_id=1, replica_groups=mesh['row'=8,'col'=16,'gz'=4] {'gz'}, dimensions={0} | all-to-all | bytes 540672 | tf_op jit(solution)/shard_map/all_to_all | solution.py:264
  291.9 7.3 %all-to-all-start.3 = ((f32[16,16,128]{2,1,0:T(8,128)}), f32[16,16,128]{2,1,0:T(8,128)S(1)}, u32[]{:S(2)}, u32[]{:S(2)}) async-start(f32[16,16,128]{2,1,0:T(8,128)} %bitcast.10), calls=%async_computation.3 | async-start | bytes 262144 | tf_op jit(solution)/shard_map/all_to_all | solution.py:264
  299.2 2.5 collective-permute-start.18
  301.7 4.0 %collective-permute-start.19 = (s16[1040,128]{1,0:T(8,128)(2,1)S(1)}, s16[1040,128]{1,0:T(8,128)(2,1)S(1)}, u32[]{:S(2)}, u32[]{:S(2)}) collective-permute-start(s16[1040,128]{1,0:T(8,128)(2,1)S(1)} %get-tuple-element.13), channel_id=1, source_target_pairs={{0,2},{1,3},{2,0},{3,1},{4,6},{5,7},{6,4},{7,5},{8,10},{9,11},{10,... | collective-permute-start | bytes 798728 | tf_op jit(solution)/shard_map/ppermute | solution.py:346
  305.7 3.1 collective-permute-start.20
  308.7 4.8 %collective-permute-done.18.coded1_ref = s16[1040,128]{1,0:T(8,128)(2,1)S(1)} collective-permute-done((s16[1040,128]{1,0:T(8,128)(2,1)S(1)}, s16[1040,128]{1,0:T(8,128)(2,1)S(1)}, u32[]{:S(2)}, u32[]{:S(2)}) %collective-permute-start.18) | collective-permute-done | bytes 266272 | tf_op jit(solution)/shard_map/ppermute | solution.py:346
  313.5 2.5 collective-permute-done.20.coded3_ref
  (60 shorter events, 23.1 us)
Async XLA Ops:
  7.6 20.1 %copy-start = (bf16[1,1,1,1024,384]{4,3,2,1,0:T(8,128)(2,1)S(1)}, bf16[1,1,1,1024,384]{4,3,2,1,0:T(8,128)(2,1)}, u32[]{:S(2)}) copy-start(bf16[1,1,1,1024,384]{4,3,2,1,0:T(8,128)(2,1)} %param.9) | copy-start | bytes 2359300
  7.6 115.9 %all-to-all-start = ((bf16[128,64,128]{2,1,0:T(8,128)(2,1)}), bf16[128,64,128]{2,1,0:T(8,128)(2,1)S(1)}, u32[]{:S(2)}, u32[]{:S(2)}) async-start(bf16[128,64,128]{2,1,0:T(8,128)(2,1)} %get-tuple-element.10), calls=%async_computation | async-start | bytes 4194304 | tf_op jit(solution)/shard_map/all_to_all | solution.py:264
  27.7 98.4 %copy-start.5 = (f32[2,8,24]{2,1,0:T(8,128)S(1)}, f32[2,8,24]{2,1,0:T(8,128)}, u32[]{:S(2)}) copy-start(f32[2,8,24]{2,1,0:T(8,128)} %param.10) | copy-start | bytes 4612
  29.1 3.1 collective-permute-start
  32.1 5.5 %collective-permute-start.1 = (f32[8,128]{1,0:T(8,128)S(1)}, f32[8,128]{1,0:T(8,128)S(1)}, u32[]{:S(2)}, u32[]{:S(2)}) collective-permute-start(f32[8,128]{1,0:T(8,128)S(1)} %broadcast_maximum_fusion), channel_id=1, source_target_pairs={{0,128},{64,192},{128,0},{192,64},{256,384},{320,448},{384,256},{4... | collective-permute-start | bytes 12296 | tf_op jit(solution)/shard_map/ppermute | solution.py:288
  37.6 7.0 %collective-permute-start.2 = (f32[8,128]{1,0:T(8,128)S(1)}, f32[8,128]{1,0:T(8,128)S(1)}, u32[]{:S(2)}, u32[]{:S(2)}) collective-permute-start(f32[8,128]{1,0:T(8,128)S(1)} %fusion.24), channel_id=1, source_target_pairs={{0,256},{64,320},{128,384},{192,448},{256,0},{320,64},{384,128},{4... | collective-permute-start | bytes 12296 | tf_op jit(solution)/shard_map/ppermute | solution.py:288
  44.6 71.2 %collective-permute-start.5 = (f32[8,128]{1,0:T(8,128)S(1)}, f32[8,128]{1,0:T(8,128)S(1)}, u32[]{:S(2)}, u32[]{:S(2)}) collective-permute-start(f32[8,128]{1,0:T(8,128)S(1)} %max.32), channel_id=1, source_target_pairs={{0,12},{4,8},{8,4},{12,0},{16,28},{20,24},{24,20},{28,16},{32,44},... | collective-permute-start | bytes 12296 | tf_op jit(solution)/shard_map/ppermute | solution.py:292
  49.9 68.5 %collective-permute-start.4 = (f32[8,128]{1,0:T(8,128)S(1)}, f32[8,128]{1,0:T(8,128)S(1)}, u32[]{:S(2)}, u32[]{:S(2)}) collective-permute-start(f32[8,128]{1,0:T(8,128)S(1)} %max.32), channel_id=1, source_target_pairs={{0,8},{4,12},{8,0},{12,4},{16,24},{20,28},{24,16},{28,20},{32,40},... | collective-permute-start | bytes 12296 | tf_op jit(solution)/shard_map/ppermute | solution.py:292
  51.8 66.7 %collective-permute-start.3 = (f32[8,128]{1,0:T(8,128)S(1)}, f32[8,128]{1,0:T(8,128)S(1)}, u32[]{:S(2)}, u32[]{:S(2)}) collective-permute-start(f32[8,128]{1,0:T(8,128)S(1)} %max.32), channel_id=1, source_target_pairs={{0,4},{4,0},{8,12},{12,8},{16,20},{20,16},{24,28},{28,24},{32,36},... | collective-permute-start | bytes 12296 | tf_op jit(solution)/shard_map/ppermute | solution.py:292
  126.1 1.4 collective-permute-start.10
  126.1 3.1 collective-permute-start.9
  129.2 7.8 %collective-permute-start.12 = (f32[6,2,24]{2,1,0:T(2,128)S(1)}, f32[6,2,24]{2,1,0:T(2,128)S(1)}, u32[]{:S(2)}, u32[]{:S(2)}) collective-permute-start(f32[6,2,24]{2,1,0:T(2,128)S(1)} %get-tuple-element.35), channel_id=1, source_target_pairs={{4,0},{8,4},{12,8},{16,12},{20,16},{24,20},{28,24},{32,28},{36,32}... | collective-permute-start | bytes 3464 | tf_op jit(solution)/shard_map/ppermute | solution.py:34
  132.2 8.0 %collective-permute-start.11 = (f32[6,2,24]{2,1,0:T(2,128)S(1)}, f32[6,2,24]{2,1,0:T(2,128)S(1)}, u32[]{:S(2)}, u32[]{:S(2)}) collective-permute-start(f32[6,2,24]{2,1,0:T(2,128)S(1)} %get-tuple-element.34), channel_id=1, source_target_pairs={{0,4},{4,8},{8,12},{12,16},{16,20},{20,24},{24,28},{28,32},{32,36}... | collective-permute-start | bytes 3464 | tf_op jit(solution)/shard_map/ppermute | solution.py:32
  140.3 7.5 %collective-permute-start.14 = (f32[6,12,2]{2,1,0:T(8,128)S(1)}, f32[6,12,2]{2,1,0:T(8,128)S(1)}, u32[]{:S(2)}, u32[]{:S(2)}) collective-permute-start(f32[6,12,2]{2,1,0:T(8,128)S(1)} %get-tuple-element.33), channel_id=1, source_target_pairs={{1,0},{2,1},{3,2},{0,3},{5,4},{6,5},{7,6},{4,7},{9,8},{10,9},{11,1... | collective-permute-start | bytes 1736 | tf_op jit(solution)/shard_map/ppermute | solution.py:34
  145.2 7.2 %collective-permute-start.13 = (f32[6,12,2]{2,1,0:T(8,128)S(1)}, f32[6,12,2]{2,1,0:T(8,128)S(1)}, u32[]{:S(2)}, u32[]{:S(2)}) collective-permute-start(f32[6,12,2]{2,1,0:T(8,128)S(1)} %get-tuple-element.32), channel_id=1, source_target_pairs={{0,1},{1,2},{2,3},{3,0},{4,5},{5,6},{6,7},{7,4},{8,9},{9,10},{10,1... | collective-permute-start | bytes 1736 | tf_op jit(solution)/shard_map/ppermute | solution.py:32
  156.5 13.0 %copy-start.4 = (f32[128,128]{1,0:T(8,128)S(1)}, f32[128,128]{1,0:T(8,128)}, u32[]{:S(2)}) copy-start(f32[128,128]{1,0:T(8,128)} %param.11) | copy-start | bytes 196612
  156.5 118.5 %all-to-all-start.1 = ((f16[128,64,128]{2,1,0:T(8,128)(2,1)}), f16[128,64,128]{2,1,0:T(8,128)(2,1)S(1)}, u32[]{:S(2)}, u32[]{:S(2)}) async-start(f16[128,64,128]{2,1,0:T(8,128)(2,1)} %bitcast.18), calls=%async_computation.1 | async-start | bytes 4194304 | tf_op jit(solution)/shard_map/all_to_all | solution.py:264
  169.6 105.3 %collective-permute-start.17 = (f32[128,128]{0,1:T(8,128)S(1)}, f32[128,128]{0,1:T(8,128)S(1)}, u32[]{:S(2)}, u32[]{:S(2)}) collective-permute-start(f32[128,128]{0,1:T(8,128)S(1)} %copy.19), channel_id=1, source_target_pairs={{0,1},{1,2},{2,3},{3,0},{4,5},{5,6},{6,7},{7,4},{8,9},{9,10},{10,1... | collective-permute-start | bytes 196616 | tf_op jit(solution)/shard_map/ppermute | solution.py:324
  171.5 103.4 %collective-permute-start.16 = (f32[128,128]{0,1:T(8,128)S(1)}, f32[128,128]{0,1:T(8,128)S(1)}, u32[]{:S(2)}, u32[]{:S(2)}) collective-permute-start(f32[128,128]{0,1:T(8,128)S(1)} %copy.19), channel_id=1, source_target_pairs={{0,2},{1,3},{2,0},{3,1},{4,6},{5,7},{6,4},{7,5},{8,10},{9,11},{10,... | collective-permute-start | bytes 196616 | tf_op jit(solution)/shard_map/ppermute | solution.py:324
  174.6 100.3 %collective-permute-start.15 = (f32[128,128]{0,1:T(8,128)S(1)}, f32[128,128]{0,1:T(8,128)S(1)}, u32[]{:S(2)}, u32[]{:S(2)}) collective-permute-start(f32[128,128]{0,1:T(8,128)S(1)} %copy.19), channel_id=1, source_target_pairs={{0,3},{1,0},{2,1},{3,2},{4,7},{5,4},{6,5},{7,6},{8,11},{9,8},{10,9... | collective-permute-start | bytes 196616 | tf_op jit(solution)/shard_map/ppermute | solution.py:324
  178.6 81.2 %collective-permute-start.8 = (f32[8,128]{1,0:T(8,128)S(1)}, f32[8,128]{1,0:T(8,128)S(1)}, u32[]{:S(2)}, u32[]{:S(2)}) collective-permute-start(f32[8,128]{1,0:T(8,128)S(1)} %get-tuple-element.22), channel_id=1, source_target_pairs={{0,48},{4,52},{8,56},{12,60},{16,32},{20,36},{24,40},{28,44},{32,1... | collective-permute-start | bytes 12296 | tf_op jit(solution)/shard_map/ppermute | solution.py:321
  186.0 87.2 %collective-permute-start.7 = (f32[8,128]{1,0:T(8,128)S(1)}, f32[8,128]{1,0:T(8,128)S(1)}, u32[]{:S(2)}, u32[]{:S(2)}) collective-permute-start(f32[8,128]{1,0:T(8,128)S(1)} %get-tuple-element.22), channel_id=1, source_target_pairs={{0,32},{4,36},{8,40},{12,44},{16,48},{20,52},{24,56},{28,60},{32,0... | collective-permute-start | bytes 12296 | tf_op jit(solution)/shard_map/ppermute | solution.py:321
  259.8 14.9 %collective-permute-start.6 = (f32[8,128]{1,0:T(8,128)S(1)}, f32[8,128]{1,0:T(8,128)S(1)}, u32[]{:S(2)}, u32[]{:S(2)}) collective-permute-start(f32[8,128]{1,0:T(8,128)S(1)} %get-tuple-element.22), channel_id=1, source_target_pairs={{0,16},{4,20},{8,24},{12,28},{16,0},{20,4},{24,8},{28,12},{32,48},... | collective-permute-start | bytes 12296 | tf_op jit(solution)/shard_map/ppermute | solution.py:321
  274.9 0.7 copy-start.1
  274.9 0.7 copy-start.2
  274.9 0.7 copy-start.3
  291.9 25.3 %all-to-all-start.3 = ((f32[16,16,128]{2,1,0:T(8,128)}), f32[16,16,128]{2,1,0:T(8,128)S(1)}, u32[]{:S(2)}, u32[]{:S(2)}) async-start(f32[16,16,128]{2,1,0:T(8,128)} %bitcast.10), calls=%async_computation.3 | async-start | bytes 262144 | tf_op jit(solution)/shard_map/all_to_all | solution.py:264
  299.2 14.3 %collective-permute-start.18 = (s16[1040,128]{1,0:T(8,128)(2,1)S(1)}, s16[1040,128]{1,0:T(8,128)(2,1)S(1)}, u32[]{:S(2)}, u32[]{:S(2)}) collective-permute-start(s16[1040,128]{1,0:T(8,128)(2,1)S(1)} %get-tuple-element.12), channel_id=1, source_target_pairs={{0,1},{1,2},{2,3},{3,0},{4,5},{5,6},{6,7},{7,4},{8,9},{9,10},{10,1... | collective-permute-start | bytes 798728 | tf_op jit(solution)/shard_map/ppermute | solution.py:346
  301.7 11.8 %collective-permute-start.19 = (s16[1040,128]{1,0:T(8,128)(2,1)S(1)}, s16[1040,128]{1,0:T(8,128)(2,1)S(1)}, u32[]{:S(2)}, u32[]{:S(2)}) collective-permute-start(s16[1040,128]{1,0:T(8,128)(2,1)S(1)} %get-tuple-element.13), channel_id=1, source_target_pairs={{0,2},{1,3},{2,0},{3,1},{4,6},{5,7},{6,4},{7,5},{8,10},{9,11},{10,... | collective-permute-start | bytes 798728 | tf_op jit(solution)/shard_map/ppermute | solution.py:346
  305.7 10.4 %collective-permute-start.20 = (s16[1040,128]{1,0:T(8,128)(2,1)S(1)}, s16[1040,128]{1,0:T(8,128)(2,1)S(1)}, u32[]{:S(2)}, u32[]{:S(2)}) collective-permute-start(s16[1040,128]{1,0:T(8,128)(2,1)S(1)} %get-tuple-element.14), channel_id=1, source_target_pairs={{0,3},{1,0},{2,1},{3,2},{4,7},{5,4},{6,5},{7,6},{8,11},{9,8},{10,9... | collective-permute-start | bytes 798728 | tf_op jit(solution)/shard_map/ppermute | solution.py:346

commit v5 on v4

--- a/solution.py
+++ b/solution.py
@@ -56,8 +56,8 @@
     return (grid_values[tuple(higher)] - grid_values[tuple(lesser)]) / (2.0 * spacing)
 
 
-def potential_deep(density):
-    padded = with_halo(density, (("row", 0), ("col", 1), ("gz", 2)), 2)
+def potential_deep(slab):
+    padded = with_halo(slab, (("col", 1),), 2)
     gradients = [centered(padded, direction) for direction in range(3)]
     grad_square = (
         gradients[0] * gradients[0] + gradients[1] * gradients[1] + gradients[2] * gradients[2]
@@ -115,14 +115,38 @@
     lax.fori_loop(0, 128, fill, 0, unroll=4)
 
 
-def density_kernel(blocks_ref, phi_ref, unit_ref, out_ref):
+def density_kernel(blocks_ref, phi_ref, core_ref, unit_ref, orbitals_ref, out_ref):
     def part(n, total):
         rows = pl.ds(pl.multiple_of(n * 256, 256), 256)
         left = jnp.concatenate([blocks_ref[r, rows, :] for r in range(8)], axis=1)
         product = jnp.dot(left, phi_ref[...], preferred_element_type=jnp.float32)
         return total + jnp.sum(phi_ref[rows, :].astype(jnp.float32) * product, axis=0, keepdims=True)
 
-    out_ref[...] = lax.fori_loop(0, 4, part, jnp.zeros((1, 384), jnp.float32))
+    rho = lax.fori_loop(0, 4, part, jnp.zeros((1, 384), jnp.float32))
+    density = jnp.maximum(rho + core_ref[...], density_floor)
+    out_ref[...] = jnp.broadcast_to(density[None], (32, 1, 384))
+
+
+def slab_kernel(ids_ref, tiles_ref, out_ref):
+    row, depth = ids_ref[0], ids_ref[2]
+    line = lax.broadcasted_iota(jnp.int32, (16, 384), 0) * 24
+    lane = lax.broadcasted_iota(jnp.int32, (16, 384), 1)
+    own_line = (lane >= line) & (lane < line + 24)
+    rows = []
+    for across in (7, 0, 1):
+        pieces = []
+        for along in (3, 0, 1):
+            place = lax.rem(row + across, 8) * 4 + lax.rem(depth + along, 4)
+            pieces.append(jnp.where(own_line, jnp.broadcast_to(tiles_ref[place], (16, 384)), 0.0))
+        rows.append(jnp.concatenate(pieces, axis=1))
+    left = jnp.concatenate(rows, axis=0)
+    source = lax.rem(lax.broadcasted_iota(jnp.int32, (1152, 128), 0), 24)
+    piece = lax.broadcasted_iota(jnp.int32, (1152, 128), 0) // 384
+    target = lax.broadcasted_iota(jnp.int32, (1152, 128), 1)
+    wanted = source + 2 + 24 * (piece - 1)
+    chosen = jnp.where((wanted == target) & (target < 28), 1.0, 0.0)
+    slab = jnp.dot(left, chosen, precision=lax.Precision.HIGHEST, preferred_element_type=jnp.float32)
+    out_ref[...] = slab.reshape(6, 8, 128)
 
 
 def ham_kernel(scale_ref, phi_ref, field_ref, out_ref):
@@ -172,7 +196,7 @@
 
     def add(t, carry):
         page0, page1 = pages_ref[t], pages_ref[128 + t]
-        block = blocks_ref[t] * scale_ref[8 * (((t & 15) ^ ids_ref[1]) >> 2)]
+        block = blocks_ref[t] * scale_ref[8 * ((t & 15) ^ ids_ref[1])]
         sums[page0] += block
         sums[page1] += block
         return carry
@@ -287,24 +311,30 @@
     for step in (1, 2, 4):
         other = lax.ppermute(largest, "row", [(i, i ^ step) for i in range(8)])
         largest = jnp.maximum(largest, other)
-    others = []
-    for step in (1, 2, 3):
-        others.append(lax.ppermute(largest, "col", [(i, i ^ step) for i in range(16)]))
-    for other in others:
-        largest = jnp.maximum(largest, other)
+    columns = [orbitals]
+    for step in range(1, 4):
+        columns.append(lax.ppermute(orbitals, "gz", [(i, (i - step) % 4) for i in range(4)]))
+    all_orbitals = jnp.concatenate(columns, axis=0).T
     largest = jnp.maximum(largest, 1e-15)
     unit = jnp.square(largest)[0, 0:1]
 
-    rho = pl.pallas_call(
+    densities = pl.pallas_call(
         density_kernel,
-        out_shape=jax.ShapeDtypeStruct((1, 384), jnp.float32),
-        in_specs=[vmem, vmem, anywhere],
+        out_shape=jax.ShapeDtypeStruct((32, 1, 384), jnp.float32),
+        in_specs=[vmem, vmem, vmem, anywhere, anywhere],
         out_specs=vmem,
         compiler_params=pltpu.CompilerParams(vmem_limit_bytes=12 * MIB),
         name="density",
-    )(incoming.reshape(8, 1024, 128), phi, unit)
-    density = jnp.maximum(rho.reshape(core_density.shape) + core_density, density_floor)
-    field = potential_deep(density)
+    )(incoming.reshape(8, 1024, 128), phi, core_density.reshape(1, 384), unit, all_orbitals)
+    slab = pl.pallas_call(
+        slab_kernel,
+        out_shape=jax.ShapeDtypeStruct((6, 8, 128), jnp.float32),
+        in_specs=[smem, vmem],
+        out_specs=vmem,
+        compiler_params=pltpu.CompilerParams(vmem_limit_bytes=8 * MIB),
+        name="slab",
+    )(ids, exchange(densities, ("row", "gz")))
+    field = potential_deep(slab[:, :, :28])
 
     local_ham = pl.pallas_call(
         ham_kernel,
@@ -317,13 +347,9 @@
     returning = local_ham.astype(jnp.float16).reshape(128, BS, 128)
     arrived = exchange(returning, PLANE).astype(jnp.float32)
     peaks = [largest]
-    for step in (4, 8, 12):
+    for step in range(1, 16):
         peaks.append(lax.ppermute(largest, "col", [(i, i ^ step) for i in range(16)]))
-    columns = [orbitals]
-    for step in range(1, 4):
-        columns.append(lax.ppermute(orbitals, "gz", [(i, (i - step) % 4) for i in range(4)]))
     units = jnp.square(jnp.concatenate(peaks, axis=0)[:, 0])
-    all_orbitals = jnp.concatenate(columns, axis=0).T
 
     page_shape = jax.ShapeDtypeStruct((PAGES * BS + SCALES, 128), jnp.int16)
     terms, *pages = pl.pallas_call(

time: 319 us -> 382 us (1.20)
  starting transfers between devices: 120 us -> 156 us
  blocking collectives: 9.11 us -> 21.9 us
  waiting for transfers between devices: 161 us -> 173 us
    all_to_all x3, waiting for transfers between devices: 4.52 us -> 66.2 us  [exchange(): return lax.all_to_all(array, axes, 0, 0, tiled=True)]
    ppermute x6 -> x15, starting transfers between devices: 38.1 us -> 81.2 us  [shards(): lax.ppermute(largest, 'col', [(i, i ^ step) for i in range(16)])]
    ppermute x6 -> x15, waiting for transfers between devices: 132 us -> 89.5 us  [shards(): lax.ppermute(largest, 'col', [(i, i ^ step) for i in range(16)])]
    all_to_all x1 -> x2, blocking collectives: 9.11 us -> 21.9 us  [exchange(): return lax.all_to_all(array, axes, 0, 0, tiled=True)]
    ppermute x3 -> x1, waiting for transfers between devices: 9.42 us -> 0.01 us  [with_halo(): lax.ppermute(tail, axis, [(i, (i + 1) % count) for i in range(count)])]
    ppermute x3 -> x1, starting transfers between devices: 7.87 us -> 1.92 us  [with_halo(): lax.ppermute(head, axis, [((i + 1) % count, i) for i in range(count)])]
  transfers between devices with their start and end apart: 24 -> 29, of which waited for: 15 -> 11; matrix products, arithmetic and copies ran while one was open for 1% -> 1% of each run, Pallas kernels for 0% -> 0%
where the time goes in v5:
time: 382 us; the launch traced here: 380 us
  waiting for transfers between devices  173 us (45%)
  starting transfers between devices  156 us (41%)
  blocking collectives  21.9 us (6%)
  Pallas kernels  19.5 us (5%)
  other arithmetic  4.55 us (1%)
    ppermute x15, waiting for transfers between devices, shards(): lax.ppermute(largest, 'col', [(i, i ^ step) for i in range(16)])  89.5 us
    ppermute x15, starting transfers between devices, shards(): lax.ppermute(largest, 'col', [(i, i ^ step) for i in range(16)])  81.2 us
    all_to_all x3, waiting for transfers between devices, exchange(): return lax.all_to_all(array, axes, 0, 0, tiled=True)  66.2 us
    all_to_all x3, starting transfers between devices, exchange(): return lax.all_to_all(array, axes, 0, 0, tiled=True)  38.7 us
    all_to_all x2, blocking collectives, exchange(): return lax.all_to_all(array, axes, 0, 0, tiled=True)  21.9 us
    ppermute x3, starting transfers between devices, shards(): lax.ppermute(orbitals, 'gz', [(i, (i - step) % 4) for i in range(4)])  11.6 us
    ppermute x3, starting transfers between devices, shards(): lax.ppermute(pages[step], 'gz', [(i, (i + step) % 4) for i in range(4)])  9.51 us
    ppermute x3, starting transfers between devices, shards(): other = lax.ppermute(largest, 'row', [(i, i ^ step) for i in range(8)])  7.78 us
  transfers between devices with their start and end apart: 29, of which 11 were waited for; matrix products, arithmetic and copies ran while one was open for 1% of the time, Pallas kernels for 0%

profile of v5, /device:TPU:6, one launch (start us, length us, event | category | flops | bytes accessed | tf_op | source)
XLA Modules:
  0.0 380.4 jit_solution(4627193402745591103)
XLA Ops:
  1.3 6.4 %pack.1 = (bf16[128,64,128]{2,1,0:T(8,128)(2,1)}, s32[256]{0:T(256)}) custom-call(s32[3]{0:T(128)} %pad_add_fusion.ids_ref, s32[16,512]{1,0:T(8,128)} %bitcast.25, s32[8,16]{1,0:T(8,128)} %bitcast.22, bf16[1024,512]{1,0:T(8,128)(2,1)} %matrix_ref.1), custom_call_target="tpu_custom_call" | custom-call | tf_op jit(solution)/shard_map/pack/pallas_call | solution.py:297
  7.7 20.0 %all-to-all-start = ((bf16[128,64,128]{2,1,0:T(8,128)(2,1)}), bf16[128,64,128]{2,1,0:T(8,128)(2,1)S(1)}, u32[]{:S(2)}, u32[]{:S(2)}) async-start(bf16[128,64,128]{2,1,0:T(8,128)(2,1)} %get-tuple-element.10), calls=%async_computation | async-start | bytes 4194304 | tf_op jit(solution)/shard_map/all_to_all | solution.py:288
  32.3 2.5 collective-permute-start.1
  34.8 4.1 %collective-permute-done.1 = f32[8,128]{0,1:T(8,128)S(1)} collective-permute-done((f32[8,128]{0,1:T(8,128)S(1)}, f32[8,128]{0,1:T(8,128)S(1)}, u32[]{:S(2)}, u32[]{:S(2)}) %collective-permute-start.1) | collective-permute-done | bytes 4128 | tf_op jit(solution)/shard_map/ppermute | solution.py:312
  39.0 3.1 collective-permute-start.2
  42.2 3.5 collective-permute-start.20
  45.7 4.8 %collective-permute-start.19 = (f32[128,128]{0,1:T(8,128)S(1)}, f32[128,128]{0,1:T(8,128)S(1)}, u32[]{:S(2)}, u32[]{:S(2)}) collective-permute-start(f32[128,128]{0,1:T(8,128)S(1)} %copy.11), channel_id=1, source_target_pairs={{0,2},{1,3},{2,0},{3,1},{4,6},{5,7},{6,4},{7,5},{8,10},{9,11},{10,... | collective-permute-start | bytes 196616 | tf_op jit(solution)/shard_map/ppermute | solution.py:316
  50.5 3.3 collective-permute-start.18
  56.7 66.2 %all-to-all-done = bf16[128,64,128]{2,1,0:T(8,128)(2,1)S(1)} async-done(((bf16[128,64,128]{2,1,0:T(8,128)(2,1)}), bf16[128,64,128]{2,1,0:T(8,128)(2,1)S(1)}, u32[]{:S(2)}, u32[]{:S(2)}) %all-to-all-start) | async-done | bytes 2097184 | tf_op jit(solution)/shard_map/all_to_all | solution.py:288
  124.7 12.7 %all_to_all.25.tiles_ref = f32[32,1,384]{2,1,0:T(1,128)S(1)} all-to-all(f32[32,1,384]{2,1,0:T(1,128)S(1)} %density.1), channel_id=1, replica_groups=mesh['row'=8,'col'=16,'gz'=4] {'row','gz'}, dimensions={0} | all-to-all | bytes 98304 | tf_op jit(solution)/shard_map/all_to_all | solution.py:288
  138.7 5.8 %collective-permute-start.21 = (f32[6,2,28]{2,1,0:T(2,128)S(1)}, f32[6,2,28]{2,1,0:T(2,128)S(1)}, u32[]{:S(2)}, u32[]{:S(2)}) collective-permute-start(f32[6,2,28]{2,1,0:T(2,128)S(1)} %get-tuple-element.28), channel_id=1, source_target_pairs={{0,4},{4,8},{8,12},{12,16},{16,20},{20,24},{24,28},{28,32},{32,36}... | collective-permute-start | bytes 4040 | tf_op jit(solution)/shard_map/ppermute | solution.py:32
  146.4 4.3 %collective-permute-done.22 = f32[6,2,28]{2,1,0:T(2,128)S(1)} collective-permute-done((f32[6,2,28]{2,1,0:T(2,128)S(1)}, f32[6,2,28]{2,1,0:T(2,128)S(1)}, u32[]{:S(2)}, u32[]{:S(2)}) %collective-permute-start.22) | collective-permute-done | bytes 1376 | tf_op jit(solution)/shard_map/ppermute | solution.py:34
  154.7 11.1 %all-to-all-start.2 = ((f16[128,64,128]{2,1,0:T(8,128)(2,1)}), f16[128,64,128]{2,1,0:T(8,128)(2,1)S(1)}, u32[]{:S(2)}, u32[]{:S(2)}) async-start(f16[128,64,128]{2,1,0:T(8,128)(2,1)} %bitcast.24), calls=%async_computation.2 | async-start | bytes 4194304 | tf_op jit(solution)/shard_map/all_to_all | solution.py:288
  165.8 4.7 %collective-permute-start.17 = (f32[8,128]{0,1:T(8,128)S(1)}, f32[8,128]{0,1:T(8,128)S(1)}, u32[]{:S(2)}, u32[]{:S(2)}) collective-permute-start(f32[8,128]{0,1:T(8,128)S(1)} %maximum_maximum_fusion), channel_id=1, source_target_pairs={{0,60},{4,56},{8,52},{12,48},{16,44},{20,40},{24,36},{28,32},{32,2... | collective-permute-start | bytes 12296 | tf_op jit(solution)/shard_map/ppermute | solution.py:351
  170.5 4.2 %collective-permute-start.16 = (f32[8,128]{0,1:T(8,128)S(1)}, f32[8,128]{0,1:T(8,128)S(1)}, u32[]{:S(2)}, u32[]{:S(2)}) collective-permute-start(f32[8,128]{0,1:T(8,128)S(1)} %maximum_maximum_fusion), channel_id=1, source_target_pairs={{0,56},{4,60},{8,48},{12,52},{16,40},{20,44},{24,32},{28,36},{32,2... | collective-permute-start | bytes 12296 | tf_op jit(solution)/shard_map/ppermute | solution.py:351
  174.7 10.1 %collective-permute-start.15 = (f32[8,128]{0,1:T(8,128)S(1)}, f32[8,128]{0,1:T(8,128)S(1)}, u32[]{:S(2)}, u32[]{:S(2)}) collective-permute-start(f32[8,128]{0,1:T(8,128)S(1)} %maximum_maximum_fusion), channel_id=1, source_target_pairs={{0,52},{4,48},{8,60},{12,56},{16,36},{20,32},{24,44},{28,40},{32,2... | collective-permute-start | bytes 12296 | tf_op jit(solution)/shard_map/ppermute | solution.py:351
  186.7 9.9 %collective-permute-start.13 = (f32[8,128]{0,1:T(8,128)S(1)}, f32[8,128]{0,1:T(8,128)S(1)}, u32[]{:S(2)}, u32[]{:S(2)}) collective-permute-start(f32[8,128]{0,1:T(8,128)S(1)} %maximum_maximum_fusion), channel_id=1, source_target_pairs={{0,44},{4,40},{8,36},{12,32},{16,60},{20,56},{24,52},{28,48},{32,1... | collective-permute-start | bytes 12296 | tf_op jit(solution)/shard_map/ppermute | solution.py:351
  196.6 86.6 %collective-permute-done.17 = f32[8,128]{0,1:T(8,128)S(1)} collective-permute-done((f32[8,128]{0,1:T(8,128)S(1)}, f32[8,128]{0,1:T(8,128)S(1)}, u32[]{:S(2)}, u32[]{:S(2)}) %collective-permute-start.17) | collective-permute-done | bytes 4128 | tf_op jit(solution)/shard_map/ppermute | solution.py:351
  285.2 9.1 %collective-permute-start.11 = (f32[8,128]{0,1:T(8,128)S(1)}, f32[8,128]{0,1:T(8,128)S(1)}, u32[]{:S(2)}, u32[]{:S(2)}) collective-permute-start(f32[8,128]{0,1:T(8,128)S(1)} %maximum_maximum_fusion), channel_id=1, source_target_pairs={{0,36},{4,32},{8,44},{12,40},{16,52},{20,48},{24,60},{28,56},{32,4... | collective-permute-start | bytes 12296 | tf_op jit(solution)/shard_map/ppermute | solution.py:351
  294.2 5.0 %collective-permute-start.10 = (f32[8,128]{0,1:T(8,128)S(1)}, f32[8,128]{0,1:T(8,128)S(1)}, u32[]{:S(2)}, u32[]{:S(2)}) collective-permute-start(f32[8,128]{0,1:T(8,128)S(1)} %maximum_maximum_fusion), channel_id=1, source_target_pairs={{0,32},{4,36},{8,40},{12,44},{16,48},{20,52},{24,56},{28,60},{32,0... | collective-permute-start | bytes 12296 | tf_op jit(solution)/shard_map/ppermute | solution.py:351
  299.2 9.6 %collective-permute-start.9 = (f32[8,128]{0,1:T(8,128)S(1)}, f32[8,128]{0,1:T(8,128)S(1)}, u32[]{:S(2)}, u32[]{:S(2)}) collective-permute-start(f32[8,128]{0,1:T(8,128)S(1)} %maximum_maximum_fusion), channel_id=1, source_target_pairs={{0,28},{4,24},{8,20},{12,16},{16,12},{20,8},{24,4},{28,0},{32,60},... | collective-permute-start | bytes 12296 | tf_op jit(solution)/shard_map/ppermute | solution.py:351
  310.8 6.6 %collective-permute-start.7 = (f32[8,128]{0,1:T(8,128)S(1)}, f32[8,128]{0,1:T(8,128)S(1)}, u32[]{:S(2)}, u32[]{:S(2)}) collective-permute-start(f32[8,128]{0,1:T(8,128)S(1)} %maximum_maximum_fusion), channel_id=1, source_target_pairs={{0,20},{4,16},{8,28},{12,24},{16,4},{20,0},{24,12},{28,8},{32,52},... | collective-permute-start | bytes 12296 | tf_op jit(solution)/shard_map/ppermute | solution.py:351
  317.4 3.2 collective-permute-start.6
  320.6 7.1 %collective-permute-start.5 = (f32[8,128]{0,1:T(8,128)S(1)}, f32[8,128]{0,1:T(8,128)S(1)}, u32[]{:S(2)}, u32[]{:S(2)}) collective-permute-start(f32[8,128]{0,1:T(8,128)S(1)} %maximum_maximum_fusion), channel_id=1, source_target_pairs={{0,12},{4,8},{8,4},{12,0},{16,28},{20,24},{24,20},{28,16},{32,44},... | collective-permute-start | bytes 12296 | tf_op jit(solution)/shard_map/ppermute | solution.py:351
  329.6 4.2 %collective-permute-start.3 = (f32[8,128]{0,1:T(8,128)S(1)}, f32[8,128]{0,1:T(8,128)S(1)}, u32[]{:S(2)}, u32[]{:S(2)}) collective-permute-start(f32[8,128]{0,1:T(8,128)S(1)} %maximum_maximum_fusion), channel_id=1, source_target_pairs={{0,4},{4,0},{8,12},{12,8},{16,20},{20,16},{24,28},{28,24},{32,36},... | collective-permute-start | bytes 12296 | tf_op jit(solution)/shard_map/ppermute | solution.py:351
  337.7 6.4 %owner.1 = (s16[4,264,128]{2,1,0:T(8,128)(2,1)S(1)}, s16[1040,128]{1,0:T(8,128)(2,1)S(1)}, s16[1040,128]{1,0:T(8,128)(2,1)S(1)}, s16[1040,128]{1,0:T(8,128)(2,1)S(1)}, s16[1040,128]{1,0:T(8,128)(2,1)S(1)}) custom-call(s32[3]{0:T(128)S(1)} %copy-done.2, s32[256]{0:T(256)S(1)} %copy-done.3, s32[8,16]{1,0:T(8,128)S(1)} %bitcast.23, f32[128]{0:T(128)S(1)} %fusion.18.scale_ref, ...), custom_call_target="tpu_custom_call" | custom-call | tf_op jit(solution)/shard_map/owner/pallas_call | solution.py:355
  344.2 9.1 %all_to_all.26.coded_ref = s16[4,264,128]{2,1,0:T(8,128)(2,1)S(1)} all-to-all(s16[4,264,128]{2,1,0:T(8,128)(2,1)S(1)} %get-tuple-element.15), channel_id=1, replica_groups=mesh['row'=8,'col'=16,'gz'=4] {'gz'}, dimensions={0} | all-to-all | bytes 540672 | tf_op jit(solution)/shard_map/all_to_all | solution.py:288
  354.0 7.6 %all-to-all-start.4 = ((f32[16,16,128]{2,1,0:T(8,128)}), f32[16,16,128]{2,1,0:T(8,128)S(1)}, u32[]{:S(2)}, u32[]{:S(2)}) async-start(f32[16,16,128]{2,1,0:T(8,128)} %bitcast.11), calls=%async_computation.4 | async-start | bytes 262144 | tf_op jit(solution)/shard_map/all_to_all | solution.py:288
  364.1 4.0 %collective-permute-start.24 = (s16[1040,128]{1,0:T(8,128)(2,1)S(1)}, s16[1040,128]{1,0:T(8,128)(2,1)S(1)}, u32[]{:S(2)}, u32[]{:S(2)}) collective-permute-start(s16[1040,128]{1,0:T(8,128)(2,1)S(1)} %get-tuple-element.13), channel_id=1, source_target_pairs={{0,2},{1,3},{2,0},{3,1},{4,6},{5,7},{6,4},{7,5},{8,10},{9,11},{10,... | collective-permute-start | bytes 798728 | tf_op jit(solution)/shard_map/ppermute | solution.py:372
  368.0 3.1 collective-permute-start.25
  371.1 5.1 %collective-permute-done.23.coded1_ref = s16[1040,128]{1,0:T(8,128)(2,1)S(1)} collective-permute-done((s16[1040,128]{1,0:T(8,128)(2,1)S(1)}, s16[1040,128]{1,0:T(8,128)(2,1)S(1)}, u32[]{:S(2)}, u32[]{:S(2)}) %collective-permute-start.23) | collective-permute-done | bytes 266272 | tf_op jit(solution)/shard_map/ppermute | solution.py:372
  376.2 2.5 collective-permute-done.25.coded3_ref
  (68 shorter events, 31.6 us)
Async XLA Ops:
  7.7 34.4 %copy-start.4 = (f32[128,128]{1,0:T(8,128)S(1)}, f32[128,128]{1,0:T(8,128)}, u32[]{:S(2)}) copy-start(f32[128,128]{1,0:T(8,128)} %param.11) | copy-start | bytes 196612
  7.7 46.1 %copy-start.5 = (f32[2,8,24]{2,1,0:T(8,128)S(1)}, f32[2,8,24]{2,1,0:T(8,128)}, u32[]{:S(2)}) copy-start(f32[2,8,24]{2,1,0:T(8,128)} %param.10) | copy-start | bytes 4612
  7.7 115.2 %all-to-all-start = ((bf16[128,64,128]{2,1,0:T(8,128)(2,1)}), bf16[128,64,128]{2,1,0:T(8,128)(2,1)S(1)}, u32[]{:S(2)}, u32[]{:S(2)}) async-start(bf16[128,64,128]{2,1,0:T(8,128)(2,1)} %get-tuple-element.10), calls=%async_computation | async-start | bytes 4194304 | tf_op jit(solution)/shard_map/all_to_all | solution.py:288
  29.1 3.1 collective-permute-start
  32.3 6.6 %collective-permute-start.1 = (f32[8,128]{0,1:T(8,128)S(1)}, f32[8,128]{0,1:T(8,128)S(1)}, u32[]{:S(2)}, u32[]{:S(2)}) collective-permute-start(f32[8,128]{0,1:T(8,128)S(1)} %broadcast_maximum_fusion), channel_id=1, source_target_pairs={{0,128},{64,192},{128,0},{192,64},{256,384},{320,448},{384,256},{4... | collective-permute-start | bytes 12296 | tf_op jit(solution)/shard_map/ppermute | solution.py:312
  38.9 98.5 %copy-start.2 = (s32[3]{0:T(128)S(1)}, s32[3]{0:T(128)}, u32[]{:S(2)}) copy-start(s32[3]{0:T(128)} %pad_add_fusion.ids_ref) | copy-start | bytes 40
  39.0 14.9 %collective-permute-start.2 = (f32[8,128]{0,1:T(8,128)S(1)}, f32[8,128]{0,1:T(8,128)S(1)}, u32[]{:S(2)}, u32[]{:S(2)}) collective-permute-start(f32[8,128]{0,1:T(8,128)S(1)} %fusion.21), channel_id=1, source_target_pairs={{0,256},{64,320},{128,384},{192,448},{256,0},{320,64},{384,128},{4... | collective-permute-start | bytes 12296 | tf_op jit(solution)/shard_map/ppermute | solution.py:312
  42.2 13.5 %collective-permute-start.20 = (f32[128,128]{0,1:T(8,128)S(1)}, f32[128,128]{0,1:T(8,128)S(1)}, u32[]{:S(2)}, u32[]{:S(2)}) collective-permute-start(f32[128,128]{0,1:T(8,128)S(1)} %copy.11), channel_id=1, source_target_pairs={{0,1},{1,2},{2,3},{3,0},{4,5},{5,6},{6,7},{7,4},{8,9},{9,10},{10,1... | collective-permute-start | bytes 196616 | tf_op jit(solution)/shard_map/ppermute | solution.py:316
  45.7 10.0 %collective-permute-start.19 = (f32[128,128]{0,1:T(8,128)S(1)}, f32[128,128]{0,1:T(8,128)S(1)}, u32[]{:S(2)}, u32[]{:S(2)}) collective-permute-start(f32[128,128]{0,1:T(8,128)S(1)} %copy.11), channel_id=1, source_target_pairs={{0,2},{1,3},{2,0},{3,1},{4,6},{5,7},{6,4},{7,5},{8,10},{9,11},{10,... | collective-permute-start | bytes 196616 | tf_op jit(solution)/shard_map/ppermute | solution.py:316
  50.5 6.2 %collective-permute-start.18 = (f32[128,128]{0,1:T(8,128)S(1)}, f32[128,128]{0,1:T(8,128)S(1)}, u32[]{:S(2)}, u32[]{:S(2)}) collective-permute-start(f32[128,128]{0,1:T(8,128)S(1)} %copy.11), channel_id=1, source_target_pairs={{0,3},{1,0},{2,1},{3,2},{4,7},{5,4},{6,5},{7,6},{8,11},{9,8},{10,9... | collective-permute-start | bytes 196616 | tf_op jit(solution)/shard_map/ppermute | solution.py:316
  138.7 7.8 %collective-permute-start.21 = (f32[6,2,28]{2,1,0:T(2,128)S(1)}, f32[6,2,28]{2,1,0:T(2,128)S(1)}, u32[]{:S(2)}, u32[]{:S(2)}) collective-permute-start(f32[6,2,28]{2,1,0:T(2,128)S(1)} %get-tuple-element.28), channel_id=1, source_target_pairs={{0,4},{4,8},{8,12},{12,16},{16,20},{20,24},{24,28},{28,32},{32,36}... | collective-permute-start | bytes 4040 | tf_op jit(solution)/shard_map/ppermute | solution.py:32
  144.5 6.2 %collective-permute-start.22 = (f32[6,2,28]{2,1,0:T(2,128)S(1)}, f32[6,2,28]{2,1,0:T(2,128)S(1)}, u32[]{:S(2)}, u32[]{:S(2)}) collective-permute-start(f32[6,2,28]{2,1,0:T(2,128)S(1)} %get-tuple-element.29), channel_id=1, source_target_pairs={{4,0},{8,4},{12,8},{16,12},{20,16},{24,20},{28,24},{32,28},{36,32}... | collective-permute-start | bytes 4040 | tf_op jit(solution)/shard_map/ppermute | solution.py:34
  154.7 182.3 %all-to-all-start.2 = ((f16[128,64,128]{2,1,0:T(8,128)(2,1)}), f16[128,64,128]{2,1,0:T(8,128)(2,1)S(1)}, u32[]{:S(2)}, u32[]{:S(2)}) async-start(f16[128,64,128]{2,1,0:T(8,128)(2,1)} %bitcast.24), calls=%async_computation.2 | async-start | bytes 4194304 | tf_op jit(solution)/shard_map/all_to_all | solution.py:288
  165.8 117.4 %collective-permute-start.17 = (f32[8,128]{0,1:T(8,128)S(1)}, f32[8,128]{0,1:T(8,128)S(1)}, u32[]{:S(2)}, u32[]{:S(2)}) collective-permute-start(f32[8,128]{0,1:T(8,128)S(1)} %maximum_maximum_fusion), channel_id=1, source_target_pairs={{0,60},{4,56},{8,52},{12,48},{16,44},{20,40},{24,36},{28,32},{32,2... | collective-permute-start | bytes 12296 | tf_op jit(solution)/shard_map/ppermute | solution.py:351
  170.5 114.6 %collective-permute-start.16 = (f32[8,128]{0,1:T(8,128)S(1)}, f32[8,128]{0,1:T(8,128)S(1)}, u32[]{:S(2)}, u32[]{:S(2)}) collective-permute-start(f32[8,128]{0,1:T(8,128)S(1)} %maximum_maximum_fusion), channel_id=1, source_target_pairs={{0,56},{4,60},{8,48},{12,52},{16,40},{20,44},{24,32},{28,36},{32,2... | collective-permute-start | bytes 12296 | tf_op jit(solution)/shard_map/ppermute | solution.py:351
  174.7 119.5 %collective-permute-start.15 = (f32[8,128]{0,1:T(8,128)S(1)}, f32[8,128]{0,1:T(8,128)S(1)}, u32[]{:S(2)}, u32[]{:S(2)}) collective-permute-start(f32[8,128]{0,1:T(8,128)S(1)} %maximum_maximum_fusion), channel_id=1, source_target_pairs={{0,52},{4,48},{8,60},{12,56},{16,36},{20,32},{24,44},{28,40},{32,2... | collective-permute-start | bytes 12296 | tf_op jit(solution)/shard_map/ppermute | solution.py:351
  184.8 114.5 %collective-permute-start.14 = (f32[8,128]{0,1:T(8,128)S(1)}, f32[8,128]{0,1:T(8,128)S(1)}, u32[]{:S(2)}, u32[]{:S(2)}) collective-permute-start(f32[8,128]{0,1:T(8,128)S(1)} %maximum_maximum_fusion), channel_id=1, source_target_pairs={{0,48},{4,52},{8,56},{12,60},{16,32},{20,36},{24,40},{28,44},{32,1... | collective-permute-start | bytes 12296 | tf_op jit(solution)/shard_map/ppermute | solution.py:351
  186.7 122.1 %collective-permute-start.13 = (f32[8,128]{0,1:T(8,128)S(1)}, f32[8,128]{0,1:T(8,128)S(1)}, u32[]{:S(2)}, u32[]{:S(2)}) collective-permute-start(f32[8,128]{0,1:T(8,128)S(1)} %maximum_maximum_fusion), channel_id=1, source_target_pairs={{0,44},{4,40},{8,36},{12,32},{16,60},{20,56},{24,52},{28,48},{32,1... | collective-permute-start | bytes 12296 | tf_op jit(solution)/shard_map/ppermute | solution.py:351
  283.3 27.5 %collective-permute-start.12 = (f32[8,128]{0,1:T(8,128)S(1)}, f32[8,128]{0,1:T(8,128)S(1)}, u32[]{:S(2)}, u32[]{:S(2)}) collective-permute-start(f32[8,128]{0,1:T(8,128)S(1)} %maximum_maximum_fusion), channel_id=1, source_target_pairs={{0,40},{4,44},{8,32},{12,36},{16,56},{20,60},{24,48},{28,52},{32,8... | collective-permute-start | bytes 12296 | tf_op jit(solution)/shard_map/ppermute | solution.py:351
  285.2 32.2 %collective-permute-start.11 = (f32[8,128]{0,1:T(8,128)S(1)}, f32[8,128]{0,1:T(8,128)S(1)}, u32[]{:S(2)}, u32[]{:S(2)}) collective-permute-start(f32[8,128]{0,1:T(8,128)S(1)} %maximum_maximum_fusion), channel_id=1, source_target_pairs={{0,36},{4,32},{8,44},{12,40},{16,52},{20,48},{24,60},{28,56},{32,4... | collective-permute-start | bytes 12296 | tf_op jit(solution)/shard_map/ppermute | solution.py:351
  294.2 26.4 %collective-permute-start.10 = (f32[8,128]{0,1:T(8,128)S(1)}, f32[8,128]{0,1:T(8,128)S(1)}, u32[]{:S(2)}, u32[]{:S(2)}) collective-permute-start(f32[8,128]{0,1:T(8,128)S(1)} %maximum_maximum_fusion), channel_id=1, source_target_pairs={{0,32},{4,36},{8,40},{12,44},{16,48},{20,52},{24,56},{28,60},{32,0... | collective-permute-start | bytes 12296 | tf_op jit(solution)/shard_map/ppermute | solution.py:351
  299.2 28.5 %collective-permute-start.9 = (f32[8,128]{0,1:T(8,128)S(1)}, f32[8,128]{0,1:T(8,128)S(1)}, u32[]{:S(2)}, u32[]{:S(2)}) collective-permute-start(f32[8,128]{0,1:T(8,128)S(1)} %maximum_maximum_fusion), channel_id=1, source_target_pairs={{0,28},{4,24},{8,20},{12,16},{16,12},{20,8},{24,4},{28,0},{32,60},... | collective-permute-start | bytes 12296 | tf_op jit(solution)/shard_map/ppermute | solution.py:351
  308.8 20.8 %collective-permute-start.8 = (f32[8,128]{0,1:T(8,128)S(1)}, f32[8,128]{0,1:T(8,128)S(1)}, u32[]{:S(2)}, u32[]{:S(2)}) collective-permute-start(f32[8,128]{0,1:T(8,128)S(1)} %maximum_maximum_fusion), channel_id=1, source_target_pairs={{0,24},{4,28},{8,16},{12,20},{16,8},{20,12},{24,0},{28,4},{32,56},... | collective-permute-start | bytes 12296 | tf_op jit(solution)/shard_map/ppermute | solution.py:351
  310.8 23.1 %collective-permute-start.7 = (f32[8,128]{0,1:T(8,128)S(1)}, f32[8,128]{0,1:T(8,128)S(1)}, u32[]{:S(2)}, u32[]{:S(2)}) collective-permute-start(f32[8,128]{0,1:T(8,128)S(1)} %maximum_maximum_fusion), channel_id=1, source_target_pairs={{0,20},{4,16},{8,28},{12,24},{16,4},{20,0},{24,12},{28,8},{32,52},... | collective-permute-start | bytes 12296 | tf_op jit(solution)/shard_map/ppermute | solution.py:351
  317.4 17.2 %collective-permute-start.6 = (f32[8,128]{0,1:T(8,128)S(1)}, f32[8,128]{0,1:T(8,128)S(1)}, u32[]{:S(2)}, u32[]{:S(2)}) collective-permute-start(f32[8,128]{0,1:T(8,128)S(1)} %maximum_maximum_fusion), channel_id=1, source_target_pairs={{0,16},{4,20},{8,24},{12,28},{16,0},{20,4},{24,8},{28,12},{32,48},... | collective-permute-start | bytes 12296 | tf_op jit(solution)/shard_map/ppermute | solution.py:351
  320.6 14.0 %collective-permute-start.5 = (f32[8,128]{0,1:T(8,128)S(1)}, f32[8,128]{0,1:T(8,128)S(1)}, u32[]{:S(2)}, u32[]{:S(2)}) collective-permute-start(f32[8,128]{0,1:T(8,128)S(1)} %maximum_maximum_fusion), channel_id=1, source_target_pairs={{0,12},{4,8},{8,4},{12,0},{16,28},{20,24},{24,20},{28,16},{32,44},... | collective-permute-start | bytes 12296 | tf_op jit(solution)/shard_map/ppermute | solution.py:351
  327.7 8.9 %collective-permute-start.4 = (f32[8,128]{0,1:T(8,128)S(1)}, f32[8,128]{0,1:T(8,128)S(1)}, u32[]{:S(2)}, u32[]{:S(2)}) collective-permute-start(f32[8,128]{0,1:T(8,128)S(1)} %maximum_maximum_fusion), channel_id=1, source_target_pairs={{0,8},{4,12},{8,0},{12,4},{16,24},{20,28},{24,16},{28,20},{32,40},... | collective-permute-start | bytes 12296 | tf_op jit(solution)/shard_map/ppermute | solution.py:351
  329.6 7.1 %collective-permute-start.3 = (f32[8,128]{0,1:T(8,128)S(1)}, f32[8,128]{0,1:T(8,128)S(1)}, u32[]{:S(2)}, u32[]{:S(2)}) collective-permute-start(f32[8,128]{0,1:T(8,128)S(1)} %maximum_maximum_fusion), channel_id=1, source_target_pairs={{0,4},{4,0},{8,12},{12,8},{16,20},{20,16},{24,28},{28,24},{32,36},... | collective-permute-start | bytes 12296 | tf_op jit(solution)/shard_map/ppermute | solution.py:351
  354.0 25.8 %all-to-all-start.4 = ((f32[16,16,128]{2,1,0:T(8,128)}), f32[16,16,128]{2,1,0:T(8,128)S(1)}, u32[]{:S(2)}, u32[]{:S(2)}) async-start(f32[16,16,128]{2,1,0:T(8,128)} %bitcast.11), calls=%async_computation.4 | async-start | bytes 262144 | tf_op jit(solution)/shard_map/all_to_all | solution.py:288
  361.6 14.6 %collective-permute-start.23 = (s16[1040,128]{1,0:T(8,128)(2,1)S(1)}, s16[1040,128]{1,0:T(8,128)(2,1)S(1)}, u32[]{:S(2)}, u32[]{:S(2)}) collective-permute-start(s16[1040,128]{1,0:T(8,128)(2,1)S(1)} %get-tuple-element.12), channel_id=1, source_target_pairs={{0,1},{1,2},{2,3},{3,0},{4,5},{5,6},{6,7},{7,4},{8,9},{9,10},{10,1... | collective-permute-start | bytes 798728 | tf_op jit(solution)/shard_map/ppermute | solution.py:372
  364.1 12.1 %collective-permute-start.24 = (s16[1040,128]{1,0:T(8,128)(2,1)S(1)}, s16[1040,128]{1,0:T(8,128)(2,1)S(1)}, u32[]{:S(2)}, u32[]{:S(2)}) collective-permute-start(s16[1040,128]{1,0:T(8,128)(2,1)S(1)} %get-tuple-element.13), channel_id=1, source_target_pairs={{0,2},{1,3},{2,0},{3,1},{4,6},{5,7},{6,4},{7,5},{8,10},{9,11},{10,... | collective-permute-start | bytes 798728 | tf_op jit(solution)/shard_map/ppermute | solution.py:372
  368.0 10.6 %collective-permute-start.25 = (s16[1040,128]{1,0:T(8,128)(2,1)S(1)}, s16[1040,128]{1,0:T(8,128)(2,1)S(1)}, u32[]{:S(2)}, u32[]{:S(2)}) collective-permute-start(s16[1040,128]{1,0:T(8,128)(2,1)S(1)} %get-tuple-element.14), channel_id=1, source_target_pairs={{0,3},{1,0},{2,1},{3,2},{4,7},{5,4},{6,5},{7,6},{8,11},{9,8},{10,9... | collective-permute-start | bytes 798728 | tf_op jit(solution)/shard_map/ppermute | solution.py:372
  (3 other events, 21.5 us)

commit v6 on v5

--- a/solution.py
+++ b/solution.py
@@ -196,7 +196,7 @@
 
     def add(t, carry):
         page0, page1 = pages_ref[t], pages_ref[128 + t]
-        block = blocks_ref[t] * scale_ref[8 * ((t & 15) ^ ids_ref[1])]
+        block = blocks_ref[t] * scale_ref[8 * (((t & 15) ^ ids_ref[1]) >> 2)]
         sums[page0] += block
         sums[page1] += block
         return carry
@@ -311,6 +311,11 @@
     for step in (1, 2, 4):
         other = lax.ppermute(largest, "row", [(i, i ^ step) for i in range(8)])
         largest = jnp.maximum(largest, other)
+    others = []
+    for step in (1, 2, 3):
+        others.append(lax.ppermute(largest, "col", [(i, i ^ step) for i in range(16)]))
+    for other in others:
+        largest = jnp.maximum(largest, other)
     columns = [orbitals]
     for step in range(1, 4):
         columns.append(lax.ppermute(orbitals, "gz", [(i, (i - step) % 4) for i in range(4)]))
@@ -347,7 +352,7 @@
     returning = local_ham.astype(jnp.float16).reshape(128, BS, 128)
     arrived = exchange(returning, PLANE).astype(jnp.float32)
     peaks = [largest]
-    for step in range(1, 16):
+    for step in (4, 8, 12):
         peaks.append(lax.ppermute(largest, "col", [(i, i ^ step) for i in range(16)]))
     units = jnp.square(jnp.concatenate(peaks, axis=0)[:, 0])
 

time: 382 us -> 316 us (0.83)
  the two profiles are of different devices: /device:TPU:6 before, /device:TPU:1 now
where the time goes in v6:
time: 316 us; the launch traced here: 315 us
  waiting for transfers between devices  158 us (50%)
  starting transfers between devices  107 us (34%)
  blocking collectives  21.5 us (7%)
  Pallas kernels  20.1 us (6%)
  other arithmetic  4.59 us (1%)
    ppermute x6, waiting for transfers between devices, shards(): lax.ppermute(largest, 'col', [(i, i ^ step) for i in range(16)])  136 us
    all_to_all x3, starting transfers between devices, exchange(): return lax.all_to_all(array, axes, 0, 0, tiled=True)  43.5 us
    ppermute x6, starting transfers between devices, shards(): lax.ppermute(largest, 'col', [(i, i ^ step) for i in range(16)])  25.4 us
    all_to_all x2, blocking collectives, exchange(): return lax.all_to_all(array, axes, 0, 0, tiled=True)  21.5 us
    ppermute x3, starting transfers between devices, shards(): lax.ppermute(orbitals, 'gz', [(i, (i - step) % 4) for i in range(4)])  12.4 us
    ppermute x3, starting transfers between devices, shards(): other = lax.ppermute(largest, 'row', [(i, i ^ step) for i in range(8)])  10.3 us
    ppermute x3, waiting for transfers between devices, shards(): lax.ppermute(pages[step], 'gz', [(i, (i + step) % 4) for i in range(4)])  10.2 us
    ppermute x3, starting transfers between devices, shards(): lax.ppermute(pages[step], 'gz', [(i, (i + step) % 4) for i in range(4)])  8.42 us
  transfers between devices with their start and end apart: 20, of which 12 were waited for; matrix products, arithmetic and copies ran while one was open for 1% of the time, Pallas kernels for 0%

profile of v6, /device:TPU:1, one launch (start us, length us, event | category | flops | bytes accessed | tf_op | source)
XLA Modules:
  0.0 315.1 jit_solution(13578888929683244579)
XLA Ops:
  1.2 6.4 %pack.1 = (bf16[128,64,128]{2,1,0:T(8,128)(2,1)}, s32[256]{0:T(256)}) custom-call(s32[3]{0:T(128)} %pad_add_fusion.ids_ref, s32[16,512]{1,0:T(8,128)} %bitcast.23, s32[8,16]{1,0:T(8,128)} %bitcast.20, bf16[1024,512]{1,0:T(8,128)(2,1)} %matrix_ref.1), custom_call_target="tpu_custom_call" | custom-call | tf_op jit(solution)/shard_map/pack/pallas_call | solution.py:297
  7.6 20.5 %all-to-all-start = ((bf16[128,64,128]{2,1,0:T(8,128)(2,1)}), bf16[128,64,128]{2,1,0:T(8,128)(2,1)S(1)}, u32[]{:S(2)}, u32[]{:S(2)}) async-start(bf16[128,64,128]{2,1,0:T(8,128)(2,1)} %get-tuple-element.10), calls=%async_computation | async-start | bytes 4194304 | tf_op jit(solution)/shard_map/all_to_all | solution.py:288
  29.6 2.8 collective-permute-start
  33.2 2.9 collective-permute-start.1
  37.8 4.6 %collective-permute-start.2 = (f32[8,128]{1,0:T(8,128)S(1)}, f32[8,128]{1,0:T(8,128)S(1)}, u32[]{:S(2)}, u32[]{:S(2)}) collective-permute-start(f32[8,128]{1,0:T(8,128)S(1)} %fusion.23), channel_id=1, source_target_pairs={{0,256},{64,320},{128,384},{192,448},{256,0},{320,64},{384,128},{4... | collective-permute-start | bytes 12296 | tf_op jit(solution)/shard_map/ppermute | solution.py:312
  43.9 4.7 %collective-permute-start.5 = (f32[8,128]{1,0:T(8,128)S(1)}, f32[8,128]{1,0:T(8,128)S(1)}, u32[]{:S(2)}, u32[]{:S(2)}) collective-permute-start(f32[8,128]{1,0:T(8,128)S(1)} %max.26), channel_id=1, source_target_pairs={{0,12},{4,8},{8,4},{12,0},{16,28},{20,24},{24,20},{28,16},{32,44},... | collective-permute-start | bytes 12296 | tf_op jit(solution)/shard_map/ppermute | solution.py:316
  48.7 1.9 collective-permute-start.4
  50.6 2.6 collective-permute-start.3
  53.3 3.2 %collective-permute-start.11 = (f32[128,128]{0,1:T(8,128)S(1)}, f32[128,128]{0,1:T(8,128)S(1)}, u32[]{:S(2)}, u32[]{:S(2)}) collective-permute-start(f32[128,128]{0,1:T(8,128)S(1)} %copy.19), channel_id=1, source_target_pairs={{0,1},{1,2},{2,3},{3,0},{4,5},{5,6},{6,7},{7,4},{8,9},{9,10},{10,1... | collective-permute-start | bytes 196616 | tf_op jit(solution)/shard_map/ppermute | solution.py:321
  56.5 4.5 %collective-permute-start.10 = (f32[128,128]{0,1:T(8,128)S(1)}, f32[128,128]{0,1:T(8,128)S(1)}, u32[]{:S(2)}, u32[]{:S(2)}) collective-permute-start(f32[128,128]{0,1:T(8,128)S(1)} %copy.19), channel_id=1, source_target_pairs={{0,2},{1,3},{2,0},{3,1},{4,6},{5,7},{6,4},{7,5},{8,10},{9,11},{10,... | collective-permute-start | bytes 196616 | tf_op jit(solution)/shard_map/ppermute | solution.py:321
  61.2 53.2 %collective-permute-done.5 = f32[8,128]{1,0:T(8,128)S(1)} collective-permute-done((f32[8,128]{1,0:T(8,128)S(1)}, f32[8,128]{1,0:T(8,128)S(1)}, u32[]{:S(2)}, u32[]{:S(2)}) %collective-permute-start.5) | collective-permute-done | bytes 4128 | tf_op jit(solution)/shard_map/ppermute | solution.py:316
  114.4 4.6 %collective-permute-start.9 = (f32[128,128]{0,1:T(8,128)S(1)}, f32[128,128]{0,1:T(8,128)S(1)}, u32[]{:S(2)}, u32[]{:S(2)}) collective-permute-start(f32[128,128]{0,1:T(8,128)S(1)} %copy.19), channel_id=1, source_target_pairs={{0,3},{1,0},{2,1},{3,2},{4,7},{5,4},{6,5},{7,6},{8,11},{9,8},{10,9... | collective-permute-start | bytes 196616 | tf_op jit(solution)/shard_map/ppermute | solution.py:321
  120.3 5.1 %all-to-all-done = bf16[128,64,128]{2,1,0:T(8,128)(2,1)S(1)} async-done(((bf16[128,64,128]{2,1,0:T(8,128)(2,1)}), bf16[128,64,128]{2,1,0:T(8,128)(2,1)S(1)}, u32[]{:S(2)}, u32[]{:S(2)}) %all-to-all-start) | async-done | bytes 2097184 | tf_op jit(solution)/shard_map/all_to_all | solution.py:288
  125.5 2.4 density.1
  127.9 13.5 %all_to_all.25.tiles_ref = f32[32,1,384]{2,1,0:T(1,128)S(1)} all-to-all(f32[32,1,384]{2,1,0:T(1,128)S(1)} %density.1), channel_id=1, replica_groups=mesh['row'=8,'col'=16,'gz'=4] {'row','gz'}, dimensions={0} | all-to-all | bytes 98304 | tf_op jit(solution)/shard_map/all_to_all | solution.py:288
  142.7 5.0 %collective-permute-start.12 = (f32[6,2,28]{2,1,0:T(2,128)S(1)}, f32[6,2,28]{2,1,0:T(2,128)S(1)}, u32[]{:S(2)}, u32[]{:S(2)}) collective-permute-start(f32[6,2,28]{2,1,0:T(2,128)S(1)} %get-tuple-element.30), channel_id=1, source_target_pairs={{0,4},{4,8},{8,12},{12,16},{16,20},{20,24},{24,28},{28,32},{32,36}... | collective-permute-start | bytes 4040 | tf_op jit(solution)/shard_map/ppermute | solution.py:32
  150.3 2.4 collective-permute-done.13
  156.7 15.5 %all-to-all-start.2 = ((f16[128,64,128]{2,1,0:T(8,128)(2,1)}), f16[128,64,128]{2,1,0:T(8,128)(2,1)S(1)}, u32[]{:S(2)}, u32[]{:S(2)}) async-start(f16[128,64,128]{2,1,0:T(8,128)(2,1)} %bitcast.22), calls=%async_computation.2 | async-start | bytes 4194304 | tf_op jit(solution)/shard_map/all_to_all | solution.py:288
  172.1 7.2 %collective-permute-start.8 = (f32[8,128]{1,0:T(8,128)S(1)}, f32[8,128]{1,0:T(8,128)S(1)}, u32[]{:S(2)}, u32[]{:S(2)}) collective-permute-start(f32[8,128]{1,0:T(8,128)S(1)} %get-tuple-element.21), channel_id=1, source_target_pairs={{0,48},{4,52},{8,56},{12,60},{16,32},{20,36},{24,40},{28,44},{32,1... | collective-permute-start | bytes 12296 | tf_op jit(solution)/shard_map/ppermute | solution.py:356
  179.4 6.9 %collective-permute-start.7 = (f32[8,128]{1,0:T(8,128)S(1)}, f32[8,128]{1,0:T(8,128)S(1)}, u32[]{:S(2)}, u32[]{:S(2)}) collective-permute-start(f32[8,128]{1,0:T(8,128)S(1)} %get-tuple-element.21), channel_id=1, source_target_pairs={{0,32},{4,36},{8,40},{12,44},{16,48},{20,52},{24,56},{28,60},{32,0... | collective-permute-start | bytes 12296 | tf_op jit(solution)/shard_map/ppermute | solution.py:356
  186.3 2.0 collective-permute-start.6
  188.3 73.0 %collective-permute-done.8 = f32[8,128]{1,0:T(8,128)S(1)} collective-permute-done((f32[8,128]{1,0:T(8,128)S(1)}, f32[8,128]{1,0:T(8,128)S(1)}, u32[]{:S(2)}, u32[]{:S(2)}) %collective-permute-start.8) | collective-permute-done | bytes 4128 | tf_op jit(solution)/shard_map/ppermute | solution.py:356
  261.3 10.1 %collective-permute-done.7 = f32[8,128]{1,0:T(8,128)S(1)} collective-permute-done((f32[8,128]{1,0:T(8,128)S(1)}, f32[8,128]{1,0:T(8,128)S(1)}, u32[]{:S(2)}, u32[]{:S(2)}) %collective-permute-start.7) | collective-permute-done | bytes 4128 | tf_op jit(solution)/shard_map/ppermute | solution.py:356
  272.2 6.4 %owner.1 = (s16[4,264,128]{2,1,0:T(8,128)(2,1)S(1)}, s16[1040,128]{1,0:T(8,128)(2,1)S(1)}, s16[1040,128]{1,0:T(8,128)(2,1)S(1)}, s16[1040,128]{1,0:T(8,128)(2,1)S(1)}, s16[1040,128]{1,0:T(8,128)(2,1)S(1)}) custom-call(s32[3]{0:T(128)S(1)} %copy-done.2, s32[256]{0:T(256)S(1)} %copy-done.3, s32[8,16]{1,0:T(8,128)S(1)} %bitcast.21, f32[32]{0:T(128)S(1)} %fusion.5.scale_ref, ...), custom_call_target="tpu_custom_call" | custom-call | tf_op jit(solution)/shard_map/owner/pallas_call | solution.py:360
  278.6 8.0 %all_to_all.26.coded_ref = s16[4,264,128]{2,1,0:T(8,128)(2,1)S(1)} all-to-all(s16[4,264,128]{2,1,0:T(8,128)(2,1)S(1)} %get-tuple-element.15), channel_id=1, replica_groups=mesh['row'=8,'col'=16,'gz'=4] {'gz'}, dimensions={0} | all-to-all | bytes 540672 | tf_op jit(solution)/shard_map/all_to_all | solution.py:288
  287.3 7.5 %all-to-all-start.4 = ((f32[16,16,128]{2,1,0:T(8,128)}), f32[16,16,128]{2,1,0:T(8,128)S(1)}, u32[]{:S(2)}, u32[]{:S(2)}) async-start(f32[16,16,128]{2,1,0:T(8,128)} %bitcast.10), calls=%async_computation.4 | async-start | bytes 262144 | tf_op jit(solution)/shard_map/all_to_all | solution.py:288
  294.8 2.2 collective-permute-start.14
  297.0 3.7 %collective-permute-start.15 = (s16[1040,128]{1,0:T(8,128)(2,1)S(1)}, s16[1040,128]{1,0:T(8,128)(2,1)S(1)}, u32[]{:S(2)}, u32[]{:S(2)}) collective-permute-start(s16[1040,128]{1,0:T(8,128)(2,1)S(1)} %get-tuple-element.13), channel_id=1, source_target_pairs={{0,2},{1,3},{2,0},{3,1},{4,6},{5,7},{6,4},{7,5},{8,10},{9,11},{10,... | collective-permute-start | bytes 798728 | tf_op jit(solution)/shard_map/ppermute | solution.py:377
  300.7 2.5 collective-permute-start.16
  303.2 2.5 collective-permute-done.14.coded1_ref
  305.7 4.5 %collective-permute-done.15.coded2_ref = s16[1040,128]{1,0:T(8,128)(2,1)S(1)} collective-permute-done((s16[1040,128]{1,0:T(8,128)(2,1)S(1)}, s16[1040,128]{1,0:T(8,128)(2,1)S(1)}, u32[]{:S(2)}, u32[]{:S(2)}) %collective-permute-start.15) | collective-permute-done | bytes 266272 | tf_op jit(solution)/shard_map/ppermute | solution.py:377
  310.2 3.2 %collective-permute-done.16.coded3_ref = s16[1040,128]{1,0:T(8,128)(2,1)S(1)} collective-permute-done((s16[1040,128]{1,0:T(8,128)(2,1)S(1)}, s16[1040,128]{1,0:T(8,128)(2,1)S(1)}, u32[]{:S(2)}, u32[]{:S(2)}) %collective-permute-start.16) | collective-permute-done | bytes 266272 | tf_op jit(solution)/shard_map/ppermute | solution.py:377
  (50 shorter events, 17.2 us)
Async XLA Ops:
  7.6 20.6 %copy-start = (bf16[1,1,1,1024,384]{4,3,2,1,0:T(8,128)(2,1)S(1)}, bf16[1,1,1,1024,384]{4,3,2,1,0:T(8,128)(2,1)}, u32[]{:S(2)}) copy-start(bf16[1,1,1,1024,384]{4,3,2,1,0:T(8,128)(2,1)} %param.9) | copy-start | bytes 2359300
  7.6 45.6 %copy-start.4 = (f32[128,128]{1,0:T(8,128)S(1)}, f32[128,128]{1,0:T(8,128)}, u32[]{:S(2)}) copy-start(f32[128,128]{1,0:T(8,128)} %param.11) | copy-start | bytes 196612
  7.6 53.5 %copy-start.5 = (f32[2,8,24]{2,1,0:T(8,128)S(1)}, f32[2,8,24]{2,1,0:T(8,128)}, u32[]{:S(2)}) copy-start(f32[2,8,24]{2,1,0:T(8,128)} %param.10) | copy-start | bytes 4612
  7.6 117.8 %all-to-all-start = ((bf16[128,64,128]{2,1,0:T(8,128)(2,1)}), bf16[128,64,128]{2,1,0:T(8,128)(2,1)S(1)}, u32[]{:S(2)}, u32[]{:S(2)}) async-start(bf16[128,64,128]{2,1,0:T(8,128)(2,1)} %get-tuple-element.10), calls=%async_computation | async-start | bytes 4194304 | tf_op jit(solution)/shard_map/all_to_all | solution.py:288
  28.9 112.5 %copy-start.2 = (s32[3]{0:T(128)S(1)}, s32[3]{0:T(128)}, u32[]{:S(2)}) copy-start(s32[3]{0:T(128)} %pad_add_fusion.ids_ref) | copy-start | bytes 40
  29.6 3.6 %collective-permute-start = (f32[8,128]{1,0:T(8,128)S(1)}, f32[8,128]{1,0:T(8,128)S(1)}, u32[]{:S(2)}, u32[]{:S(2)}) collective-permute-start(f32[8,128]{1,0:T(8,128)S(1)} %broadcast_in_dim.3), channel_id=1, source_target_pairs={{0,64},{64,0},{128,192},{192,128},{256,320},{320,256},{384,448},{4... | collective-permute-start | bytes 12296 | tf_op jit(solution)/shard_map/ppermute | solution.py:312
  33.2 4.6 %collective-permute-start.1 = (f32[8,128]{1,0:T(8,128)S(1)}, f32[8,128]{1,0:T(8,128)S(1)}, u32[]{:S(2)}, u32[]{:S(2)}) collective-permute-start(f32[8,128]{1,0:T(8,128)S(1)} %broadcast_maximum_fusion), channel_id=1, source_target_pairs={{0,128},{64,192},{128,0},{192,64},{256,384},{320,448},{384,256},{4... | collective-permute-start | bytes 12296 | tf_op jit(solution)/shard_map/ppermute | solution.py:312
  37.8 6.1 %collective-permute-start.2 = (f32[8,128]{1,0:T(8,128)S(1)}, f32[8,128]{1,0:T(8,128)S(1)}, u32[]{:S(2)}, u32[]{:S(2)}) collective-permute-start(f32[8,128]{1,0:T(8,128)S(1)} %fusion.23), channel_id=1, source_target_pairs={{0,256},{64,320},{128,384},{192,448},{256,0},{320,64},{384,128},{4... | collective-permute-start | bytes 12296 | tf_op jit(solution)/shard_map/ppermute | solution.py:312
  43.9 70.4 %collective-permute-start.5 = (f32[8,128]{1,0:T(8,128)S(1)}, f32[8,128]{1,0:T(8,128)S(1)}, u32[]{:S(2)}, u32[]{:S(2)}) collective-permute-start(f32[8,128]{1,0:T(8,128)S(1)} %max.26), channel_id=1, source_target_pairs={{0,12},{4,8},{8,4},{12,0},{16,28},{20,24},{24,20},{28,16},{32,44},... | collective-permute-start | bytes 12296 | tf_op jit(solution)/shard_map/ppermute | solution.py:316
  48.7 70.3 %collective-permute-start.4 = (f32[8,128]{1,0:T(8,128)S(1)}, f32[8,128]{1,0:T(8,128)S(1)}, u32[]{:S(2)}, u32[]{:S(2)}) collective-permute-start(f32[8,128]{1,0:T(8,128)S(1)} %max.26), channel_id=1, source_target_pairs={{0,8},{4,12},{8,0},{12,4},{16,24},{20,28},{24,16},{28,20},{32,40},... | collective-permute-start | bytes 12296 | tf_op jit(solution)/shard_map/ppermute | solution.py:316
  50.6 68.4 %collective-permute-start.3 = (f32[8,128]{1,0:T(8,128)S(1)}, f32[8,128]{1,0:T(8,128)S(1)}, u32[]{:S(2)}, u32[]{:S(2)}) collective-permute-start(f32[8,128]{1,0:T(8,128)S(1)} %max.26), channel_id=1, source_target_pairs={{0,4},{4,0},{8,12},{12,8},{16,20},{20,16},{24,28},{28,24},{32,36},... | collective-permute-start | bytes 12296 | tf_op jit(solution)/shard_map/ppermute | solution.py:316
  53.3 66.2 %collective-permute-start.11 = (f32[128,128]{0,1:T(8,128)S(1)}, f32[128,128]{0,1:T(8,128)S(1)}, u32[]{:S(2)}, u32[]{:S(2)}) collective-permute-start(f32[128,128]{0,1:T(8,128)S(1)} %copy.19), channel_id=1, source_target_pairs={{0,1},{1,2},{2,3},{3,0},{4,5},{5,6},{6,7},{7,4},{8,9},{9,10},{10,1... | collective-permute-start | bytes 196616 | tf_op jit(solution)/shard_map/ppermute | solution.py:321
  56.5 63.0 %collective-permute-start.10 = (f32[128,128]{0,1:T(8,128)S(1)}, f32[128,128]{0,1:T(8,128)S(1)}, u32[]{:S(2)}, u32[]{:S(2)}) collective-permute-start(f32[128,128]{0,1:T(8,128)S(1)} %copy.19), channel_id=1, source_target_pairs={{0,2},{1,3},{2,0},{3,1},{4,6},{5,7},{6,4},{7,5},{8,10},{9,11},{10,... | collective-permute-start | bytes 196616 | tf_op jit(solution)/shard_map/ppermute | solution.py:321
  114.4 5.9 %collective-permute-start.9 = (f32[128,128]{0,1:T(8,128)S(1)}, f32[128,128]{0,1:T(8,128)S(1)}, u32[]{:S(2)}, u32[]{:S(2)}) collective-permute-start(f32[128,128]{0,1:T(8,128)S(1)} %copy.19), channel_id=1, source_target_pairs={{0,3},{1,0},{2,1},{3,2},{4,7},{5,4},{6,5},{7,6},{8,11},{9,8},{10,9... | collective-permute-start | bytes 196616 | tf_op jit(solution)/shard_map/ppermute | solution.py:321
  142.7 7.6 %collective-permute-start.12 = (f32[6,2,28]{2,1,0:T(2,128)S(1)}, f32[6,2,28]{2,1,0:T(2,128)S(1)}, u32[]{:S(2)}, u32[]{:S(2)}) collective-permute-start(f32[6,2,28]{2,1,0:T(2,128)S(1)} %get-tuple-element.30), channel_id=1, source_target_pairs={{0,4},{4,8},{8,12},{12,16},{16,20},{20,24},{24,28},{28,32},{32,36}... | collective-permute-start | bytes 4040 | tf_op jit(solution)/shard_map/ppermute | solution.py:32
  147.6 5.0 %collective-permute-start.13 = (f32[6,2,28]{2,1,0:T(2,128)S(1)}, f32[6,2,28]{2,1,0:T(2,128)S(1)}, u32[]{:S(2)}, u32[]{:S(2)}) collective-permute-start(f32[6,2,28]{2,1,0:T(2,128)S(1)} %get-tuple-element.31), channel_id=1, source_target_pairs={{4,0},{8,4},{12,8},{16,12},{20,16},{24,20},{28,24},{32,28},{36,32}... | collective-permute-start | bytes 4040 | tf_op jit(solution)/shard_map/ppermute | solution.py:34
  156.7 114.8 %all-to-all-start.2 = ((f16[128,64,128]{2,1,0:T(8,128)(2,1)}), f16[128,64,128]{2,1,0:T(8,128)(2,1)S(1)}, u32[]{:S(2)}, u32[]{:S(2)}) async-start(f16[128,64,128]{2,1,0:T(8,128)(2,1)} %bitcast.22), calls=%async_computation.2 | async-start | bytes 4194304 | tf_op jit(solution)/shard_map/all_to_all | solution.py:288
  172.1 89.2 %collective-permute-start.8 = (f32[8,128]{1,0:T(8,128)S(1)}, f32[8,128]{1,0:T(8,128)S(1)}, u32[]{:S(2)}, u32[]{:S(2)}) collective-permute-start(f32[8,128]{1,0:T(8,128)S(1)} %get-tuple-element.21), channel_id=1, source_target_pairs={{0,48},{4,52},{8,56},{12,60},{16,32},{20,36},{24,40},{28,44},{32,1... | collective-permute-start | bytes 12296 | tf_op jit(solution)/shard_map/ppermute | solution.py:356
  179.4 92.0 %collective-permute-start.7 = (f32[8,128]{1,0:T(8,128)S(1)}, f32[8,128]{1,0:T(8,128)S(1)}, u32[]{:S(2)}, u32[]{:S(2)}) collective-permute-start(f32[8,128]{1,0:T(8,128)S(1)} %get-tuple-element.21), channel_id=1, source_target_pairs={{0,32},{4,36},{8,40},{12,44},{16,48},{20,52},{24,56},{28,60},{32,0... | collective-permute-start | bytes 12296 | tf_op jit(solution)/shard_map/ppermute | solution.py:356
  186.3 85.1 %collective-permute-start.6 = (f32[8,128]{1,0:T(8,128)S(1)}, f32[8,128]{1,0:T(8,128)S(1)}, u32[]{:S(2)}, u32[]{:S(2)}) collective-permute-start(f32[8,128]{1,0:T(8,128)S(1)} %get-tuple-element.21), channel_id=1, source_target_pairs={{0,16},{4,20},{8,24},{12,28},{16,0},{20,4},{24,8},{28,12},{32,48},... | collective-permute-start | bytes 12296 | tf_op jit(solution)/shard_map/ppermute | solution.py:356
  271.5 0.7 copy-start.1
  271.5 0.7 copy-start.3
  287.3 27.2 %all-to-all-start.4 = ((f32[16,16,128]{2,1,0:T(8,128)}), f32[16,16,128]{2,1,0:T(8,128)S(1)}, u32[]{:S(2)}, u32[]{:S(2)}) async-start(f32[16,16,128]{2,1,0:T(8,128)} %bitcast.10), calls=%async_computation.4 | async-start | bytes 262144 | tf_op jit(solution)/shard_map/all_to_all | solution.py:288
  294.8 10.9 %collective-permute-start.14 = (s16[1040,128]{1,0:T(8,128)(2,1)S(1)}, s16[1040,128]{1,0:T(8,128)(2,1)S(1)}, u32[]{:S(2)}, u32[]{:S(2)}) collective-permute-start(s16[1040,128]{1,0:T(8,128)(2,1)S(1)} %get-tuple-element.12), channel_id=1, source_target_pairs={{0,1},{1,2},{2,3},{3,0},{4,5},{5,6},{6,7},{7,4},{8,9},{9,10},{10,1... | collective-permute-start | bytes 798728 | tf_op jit(solution)/shard_map/ppermute | solution.py:377
  297.0 13.2 %collective-permute-start.15 = (s16[1040,128]{1,0:T(8,128)(2,1)S(1)}, s16[1040,128]{1,0:T(8,128)(2,1)S(1)}, u32[]{:S(2)}, u32[]{:S(2)}) collective-permute-start(s16[1040,128]{1,0:T(8,128)(2,1)S(1)} %get-tuple-element.13), channel_id=1, source_target_pairs={{0,2},{1,3},{2,0},{3,1},{4,6},{5,7},{6,4},{7,5},{8,10},{9,11},{10,... | collective-permute-start | bytes 798728 | tf_op jit(solution)/shard_map/ppermute | solution.py:377
  300.7 12.7 %collective-permute-start.16 = (s16[1040,128]{1,0:T(8,128)(2,1)S(1)}, s16[1040,128]{1,0:T(8,128)(2,1)S(1)}, u32[]{:S(2)}, u32[]{:S(2)}) collective-permute-start(s16[1040,128]{1,0:T(8,128)(2,1)S(1)} %get-tuple-element.14), channel_id=1, source_target_pairs={{0,3},{1,0},{2,1},{3,2},{4,7},{5,4},{6,5},{7,6},{8,11},{9,8},{10,9... | collective-permute-start | bytes 798728 | tf_op jit(solution)/shard_map/ppermute | solution.py:377

commit v7 on v6

--- a/solution.py
+++ b/solution.py
@@ -70,8 +70,8 @@
     return first[1:-1, 1:-1, 1:-1] - divergence
 
 
-def listed_pair(ids_ref, lists_ref, t):
-    row, col, depth = ids_ref[0], ids_ref[1], ids_ref[2]
+def listed_pair(place, lists_ref, t):
+    row, col, depth = place
     tile = t * 4 + depth
     a0 = lists_ref[2 * row, tile] - 16 * row
     a1 = lists_ref[2 * row + 1, tile] - 16 * row
@@ -84,8 +84,24 @@
     return jnp.where(lane < BS, low, high)
 
 
-def pack_kernel(ids_ref, lists_ref, pattern_ref, matrix_ref, out_ref, pages_ref, held):
+def pack_kernel(
+    lists_ref, pattern_ref, matrix_hbm, out_hbm, pages_ref, matrix_ref, out_ref, held, in_sems, out_sems
+):
+    place = lax.axis_index("row"), lax.axis_index("col"), lax.axis_index("gz")
+
+    def rows_in(q):
+        rows = pl.ds(pl.multiple_of(q * 128, 128), 128)
+        return pltpu.make_async_copy(matrix_hbm.at[rows], matrix_ref.at[rows], in_sems.at[q])
+
+    def chunks_out(n):
+        chunks = pl.ds(n * 16, 16)
+        return pltpu.make_async_copy(out_ref.at[chunks], out_hbm.at[chunks], out_sems.at[n])
+
+    for q in range(8):
+        rows_in(q).start()
+
     def turn(q, carry):
+        rows_in(q).wait()
         rows = pl.ds(pl.multiple_of(q * 128, 128), 128)
         first = (q < 4).astype(jnp.float32)
         for m in range(4):
@@ -104,7 +120,7 @@
     lax.fori_loop(0, 8, turn, 0)
 
     def fill(t, carry):
-        a0, a1, b = listed_pair(ids_ref, lists_ref, t)
+        a0, a1, b = listed_pair(place, lists_ref, t)
         page0 = (a0 & 1) * 64 + b * 8 + (a0 >> 1)
         page1 = (1 - (a1 & 1)) * 64 + b * 8 + (a1 >> 1)
         pages_ref[t] = page0
@@ -112,7 +128,11 @@
         out_ref[t] = held[page0] + held[page1]
         return carry
 
-    lax.fori_loop(0, 128, fill, 0, unroll=4)
+    for n in range(8):
+        lax.fori_loop(16 * n, 16 * n + 16, fill, 0, unroll=4)
+        chunks_out(n).start()
+    for n in range(8):
+        chunks_out(n).wait()
 
 
 def density_kernel(blocks_ref, phi_ref, core_ref, unit_ref, orbitals_ref, out_ref):
@@ -300,11 +320,17 @@
             jax.ShapeDtypeStruct((128, BS, 128), jnp.bfloat16),
             jax.ShapeDtypeStruct((256,), jnp.int32),
         ],
-        in_specs=[smem, smem, smem, vmem],
-        out_specs=[vmem, smem],
-        scratch_shapes=[pltpu.VMEM((128, BS, 128), jnp.bfloat16)],
+        in_specs=[smem, smem, anywhere],
+        out_specs=[anywhere, smem],
+        scratch_shapes=[
+            pltpu.VMEM((1024, 512), jnp.bfloat16),
+            pltpu.VMEM((128, BS, 128), jnp.bfloat16),
+            pltpu.VMEM((128, BS, 128), jnp.bfloat16),
+            pltpu.SemaphoreType.DMA((8,)),
+            pltpu.SemaphoreType.DMA((8,)),
+        ],
         name="pack",
-    )(ids, lists, pattern, density_matrix)
+    )(lists, pattern, density_matrix)
     incoming = exchange(outgoing, PLANE)
 
     largest = jnp.full((8, 128), jnp.max(jnp.abs(phi)).astype(jnp.float32))

time: 316 us -> 317 us (level)
  blocking collectives: 21.5 us -> 7.96 us
  waiting for transfers between devices: 158 us -> 165 us
  starting transfers between devices: 107 us -> 113 us
    all_to_all x2 -> x1, blocking collectives: 21.5 us -> 7.96 us  [exchange(): return lax.all_to_all(array, axes, 0, 0, tiled=True)]
    all_to_all x3 -> x4, waiting for transfers between devices: 5.13 us -> 12.3 us  [exchange(): return lax.all_to_all(array, axes, 0, 0, tiled=True)]
    all_to_all x3 -> x4, starting transfers between devices: 43.5 us -> 49.9 us  [exchange(): return lax.all_to_all(array, axes, 0, 0, tiled=True)]
  transfers between devices with their start and end apart: 20 -> 21, of which waited for: 12 -> 13; matrix products, arithmetic and copies ran while one was open for 1% -> 1% of each run, Pallas kernels for 0% -> 0%
where the time goes in v7:
time: 317 us; the launch traced here: 316 us
  waiting for transfers between devices  165 us (52%)
  starting transfers between devices  113 us (36%)
  Pallas kernels  21.7 us (7%)
  blocking collectives  7.96 us (3%)
  other arithmetic  4.05 us (1%)
    ppermute x6, waiting for transfers between devices, shards(): lax.ppermute(largest, 'col', [(i, i ^ step) for i in range(16)])  136 us
    all_to_all x4, starting transfers between devices, exchange(): return lax.all_to_all(array, axes, 0, 0, tiled=True)  49.9 us
    ppermute x6, starting transfers between devices, shards(): lax.ppermute(largest, 'col', [(i, i ^ step) for i in range(16)])  25.4 us
    ppermute x3, starting transfers between devices, shards(): lax.ppermute(orbitals, 'gz', [(i, (i - step) % 4) for i in range(4)])  12.4 us
    all_to_all x4, waiting for transfers between devices, exchange(): return lax.all_to_all(array, axes, 0, 0, tiled=True)  12.3 us
    ppermute x3, starting transfers between devices, shards(): other = lax.ppermute(largest, 'row', [(i, i ^ step) for i in range(8)])  10.3 us
    ppermute x3, waiting for transfers between devices, shards(): lax.ppermute(pages[step], 'gz', [(i, (i + step) % 4) for i in range(4)])  10.2 us
    ppermute x3, starting transfers between devices, shards(): lax.ppermute(pages[step], 'gz', [(i, (i + step) % 4) for i in range(4)])  8.42 us
  transfers between devices with their start and end apart: 21, of which 13 were waited for; matrix products, arithmetic and copies ran while one was open for 1% of the time, Pallas kernels for 0%

profile of v7, /device:TPU:1, one launch (start us, length us, event | category | flops | bytes accessed | tf_op | source)
XLA Modules:
  0.0 316.3 jit_solution(5569615347008069207)
XLA Ops:
  0.6 7.2 %pack.1 = (bf16[128,64,128]{2,1,0:T(8,128)(2,1)}, s32[256]{0:T(256)}) custom-call(s32[16,512]{1,0:T(8,128)} %bitcast.23, s32[8,16]{1,0:T(8,128)} %bitcast.20, bf16[1024,512]{1,0:T(8,128)(2,1)} %matrix_hbm.1), custom_call_target="tpu_custom_call" | custom-call | tf_op jit(solution)/shard_map/pack/pallas_call | solution.py:317
  7.9 20.5 %all-to-all-start = ((bf16[128,64,128]{2,1,0:T(8,128)(2,1)}), bf16[128,64,128]{2,1,0:T(8,128)(2,1)S(1)}, u32[]{:S(2)}, u32[]{:S(2)}) async-start(bf16[128,64,128]{2,1,0:T(8,128)(2,1)} %get-tuple-element.10), calls=%async_computation | async-start | bytes 4194304 | tf_op jit(solution)/shard_map/all_to_all | solution.py:308
  29.8 2.8 collective-permute-start
  33.4 2.9 collective-permute-start.1
  38.1 4.6 %collective-permute-start.2 = (f32[8,128]{1,0:T(8,128)S(1)}, f32[8,128]{1,0:T(8,128)S(1)}, u32[]{:S(2)}, u32[]{:S(2)}) collective-permute-start(f32[8,128]{1,0:T(8,128)S(1)} %fusion.23), channel_id=1, source_target_pairs={{0,256},{64,320},{128,384},{192,448},{256,0},{320,64},{384,128},{4... | collective-permute-start | bytes 12296 | tf_op jit(solution)/shard_map/ppermute | solution.py:338
  44.2 4.7 %collective-permute-start.5 = (f32[8,128]{1,0:T(8,128)S(1)}, f32[8,128]{1,0:T(8,128)S(1)}, u32[]{:S(2)}, u32[]{:S(2)}) collective-permute-start(f32[8,128]{1,0:T(8,128)S(1)} %max.26), channel_id=1, source_target_pairs={{0,12},{4,8},{8,4},{12,0},{16,28},{20,24},{24,20},{28,16},{32,44},... | collective-permute-start | bytes 12296 | tf_op jit(solution)/shard_map/ppermute | solution.py:342
  50.9 2.6 collective-permute-start.3
  53.6 3.2 %collective-permute-start.11 = (f32[128,128]{0,1:T(8,128)S(1)}, f32[128,128]{0,1:T(8,128)S(1)}, u32[]{:S(2)}, u32[]{:S(2)}) collective-permute-start(f32[128,128]{0,1:T(8,128)S(1)} %copy.19), channel_id=1, source_target_pairs={{0,1},{1,2},{2,3},{3,0},{4,5},{5,6},{6,7},{7,4},{8,9},{9,10},{10,1... | collective-permute-start | bytes 196616 | tf_op jit(solution)/shard_map/ppermute | solution.py:347
  56.8 4.5 %collective-permute-start.10 = (f32[128,128]{0,1:T(8,128)S(1)}, f32[128,128]{0,1:T(8,128)S(1)}, u32[]{:S(2)}, u32[]{:S(2)}) collective-permute-start(f32[128,128]{0,1:T(8,128)S(1)} %copy.19), channel_id=1, source_target_pairs={{0,2},{1,3},{2,0},{3,1},{4,6},{5,7},{6,4},{7,5},{8,10},{9,11},{10,... | collective-permute-start | bytes 196616 | tf_op jit(solution)/shard_map/ppermute | solution.py:347
  61.5 53.2 %collective-permute-done.5 = f32[8,128]{1,0:T(8,128)S(1)} collective-permute-done((f32[8,128]{1,0:T(8,128)S(1)}, f32[8,128]{1,0:T(8,128)S(1)}, u32[]{:S(2)}, u32[]{:S(2)}) %collective-permute-start.5) | collective-permute-done | bytes 4128 | tf_op jit(solution)/shard_map/ppermute | solution.py:342
  114.6 4.6 %collective-permute-start.9 = (f32[128,128]{0,1:T(8,128)S(1)}, f32[128,128]{0,1:T(8,128)S(1)}, u32[]{:S(2)}, u32[]{:S(2)}) collective-permute-start(f32[128,128]{0,1:T(8,128)S(1)} %copy.19), channel_id=1, source_target_pairs={{0,3},{1,0},{2,1},{3,2},{4,7},{5,4},{6,5},{7,6},{8,11},{9,8},{10,9... | collective-permute-start | bytes 196616 | tf_op jit(solution)/shard_map/ppermute | solution.py:347
  120.6 5.1 %all-to-all-done = bf16[128,64,128]{2,1,0:T(8,128)(2,1)S(1)} async-done(((bf16[128,64,128]{2,1,0:T(8,128)(2,1)}), bf16[128,64,128]{2,1,0:T(8,128)(2,1)S(1)}, u32[]{:S(2)}, u32[]{:S(2)}) %all-to-all-start) | async-done | bytes 2097184 | tf_op jit(solution)/shard_map/all_to_all | solution.py:308
  125.7 3.1 density.1
  128.8 6.5 %all-to-all-start.1 = ((f32[32,1,384]{2,1,0:T(1,128)}), f32[32,1,384]{2,1,0:T(1,128)S(1)}, u32[]{:S(2)}, u32[]{:S(2)}) async-start(f32[32,1,384]{2,1,0:T(1,128)} %density.1), calls=%async_computation.1 | async-start | bytes 98304 | tf_op jit(solution)/shard_map/all_to_all | solution.py:308
  135.4 7.2 %all-to-all-done.1.tiles_ref = f32[32,1,384]{2,1,0:T(1,128)S(1)} async-done(((f32[32,1,384]{2,1,0:T(1,128)}), f32[32,1,384]{2,1,0:T(1,128)S(1)}, u32[]{:S(2)}, u32[]{:S(2)}) %all-to-all-start.1) | async-done | bytes 49184 | tf_op jit(solution)/shard_map/all_to_all | solution.py:308
  143.8 5.0 %collective-permute-start.12 = (f32[6,2,28]{2,1,0:T(2,128)S(1)}, f32[6,2,28]{2,1,0:T(2,128)S(1)}, u32[]{:S(2)}, u32[]{:S(2)}) collective-permute-start(f32[6,2,28]{2,1,0:T(2,128)S(1)} %get-tuple-element.30), channel_id=1, source_target_pairs={{0,4},{4,8},{8,12},{12,16},{16,20},{20,24},{24,28},{28,32},{32,36}... | collective-permute-start | bytes 4040 | tf_op jit(solution)/shard_map/ppermute | solution.py:32
  151.4 2.4 collective-permute-done.13
  157.8 15.4 %all-to-all-start.2 = ((f16[128,64,128]{2,1,0:T(8,128)(2,1)}), f16[128,64,128]{2,1,0:T(8,128)(2,1)S(1)}, u32[]{:S(2)}, u32[]{:S(2)}) async-start(f16[128,64,128]{2,1,0:T(8,128)(2,1)} %bitcast.22), calls=%async_computation.2 | async-start | bytes 4194304 | tf_op jit(solution)/shard_map/all_to_all | solution.py:308
  173.3 7.2 %collective-permute-start.8 = (f32[8,128]{1,0:T(8,128)S(1)}, f32[8,128]{1,0:T(8,128)S(1)}, u32[]{:S(2)}, u32[]{:S(2)}) collective-permute-start(f32[8,128]{1,0:T(8,128)S(1)} %get-tuple-element.21), channel_id=1, source_target_pairs={{0,48},{4,52},{8,56},{12,60},{16,32},{20,36},{24,40},{28,44},{32,1... | collective-permute-start | bytes 12296 | tf_op jit(solution)/shard_map/ppermute | solution.py:382
  180.5 6.9 %collective-permute-start.7 = (f32[8,128]{1,0:T(8,128)S(1)}, f32[8,128]{1,0:T(8,128)S(1)}, u32[]{:S(2)}, u32[]{:S(2)}) collective-permute-start(f32[8,128]{1,0:T(8,128)S(1)} %get-tuple-element.21), channel_id=1, source_target_pairs={{0,32},{4,36},{8,40},{12,44},{16,48},{20,52},{24,56},{28,60},{32,0... | collective-permute-start | bytes 12296 | tf_op jit(solution)/shard_map/ppermute | solution.py:382
  187.5 2.0 collective-permute-start.6
  189.5 73.0 %collective-permute-done.8 = f32[8,128]{1,0:T(8,128)S(1)} collective-permute-done((f32[8,128]{1,0:T(8,128)S(1)}, f32[8,128]{1,0:T(8,128)S(1)}, u32[]{:S(2)}, u32[]{:S(2)}) %collective-permute-start.8) | collective-permute-done | bytes 4128 | tf_op jit(solution)/shard_map/ppermute | solution.py:382
  262.4 10.1 %collective-permute-done.7 = f32[8,128]{1,0:T(8,128)S(1)} collective-permute-done((f32[8,128]{1,0:T(8,128)S(1)}, f32[8,128]{1,0:T(8,128)S(1)}, u32[]{:S(2)}, u32[]{:S(2)}) %collective-permute-start.7) | collective-permute-done | bytes 4128 | tf_op jit(solution)/shard_map/ppermute | solution.py:382
  273.3 6.4 %owner.1 = (s16[4,264,128]{2,1,0:T(8,128)(2,1)S(1)}, s16[1040,128]{1,0:T(8,128)(2,1)S(1)}, s16[1040,128]{1,0:T(8,128)(2,1)S(1)}, s16[1040,128]{1,0:T(8,128)(2,1)S(1)}, s16[1040,128]{1,0:T(8,128)(2,1)S(1)}) custom-call(s32[3]{0:T(128)S(1)} %pad_add_fusion.ids_ref, s32[256]{0:T(256)S(1)} %copy-done.2, s32[8,16]{1,0:T(8,128)S(1)} %bitcast.21, ...), custom_call_target="tpu_custom_call" | custom-call | tf_op jit(solution)/shard_map/owner/pallas_call | solution.py:386
  279.7 8.0 %all_to_all.25.coded_ref = s16[4,264,128]{2,1,0:T(8,128)(2,1)S(1)} all-to-all(s16[4,264,128]{2,1,0:T(8,128)(2,1)S(1)} %get-tuple-element.15), channel_id=1, replica_groups=mesh['row'=8,'col'=16,'gz'=4] {'gz'}, dimensions={0} | all-to-all | bytes 540672 | tf_op jit(solution)/shard_map/all_to_all | solution.py:308
  288.4 7.5 %all-to-all-start.4 = ((f32[16,16,128]{2,1,0:T(8,128)}), f32[16,16,128]{2,1,0:T(8,128)S(1)}, u32[]{:S(2)}, u32[]{:S(2)}) async-start(f32[16,16,128]{2,1,0:T(8,128)} %bitcast.10), calls=%async_computation.4 | async-start | bytes 262144 | tf_op jit(solution)/shard_map/all_to_all | solution.py:308
  295.9 2.2 collective-permute-start.14
  298.1 3.7 %collective-permute-start.15 = (s16[1040,128]{1,0:T(8,128)(2,1)S(1)}, s16[1040,128]{1,0:T(8,128)(2,1)S(1)}, u32[]{:S(2)}, u32[]{:S(2)}) collective-permute-start(s16[1040,128]{1,0:T(8,128)(2,1)S(1)} %get-tuple-element.13), channel_id=1, source_target_pairs={{0,2},{1,3},{2,0},{3,1},{4,6},{5,7},{6,4},{7,5},{8,10},{9,11},{10,... | collective-permute-start | bytes 798728 | tf_op jit(solution)/shard_map/ppermute | solution.py:403
  301.8 2.5 collective-permute-start.16
  304.3 2.5 collective-permute-done.14.coded1_ref
  306.8 4.5 %collective-permute-done.15.coded2_ref = s16[1040,128]{1,0:T(8,128)(2,1)S(1)} collective-permute-done((s16[1040,128]{1,0:T(8,128)(2,1)S(1)}, s16[1040,128]{1,0:T(8,128)(2,1)S(1)}, u32[]{:S(2)}, u32[]{:S(2)}) %collective-permute-start.15) | collective-permute-done | bytes 266272 | tf_op jit(solution)/shard_map/ppermute | solution.py:403
  311.3 3.2 collective-permute-done.16.coded3_ref
  (49 shorter events, 18.6 us)
Async XLA Ops:
  7.9 20.6 %copy-start = (bf16[1,1,1,1024,384]{4,3,2,1,0:T(8,128)(2,1)S(1)}, bf16[1,1,1,1024,384]{4,3,2,1,0:T(8,128)(2,1)}, u32[]{:S(2)}) copy-start(bf16[1,1,1,1024,384]{4,3,2,1,0:T(8,128)(2,1)} %param.9) | copy-start | bytes 2359300
  7.9 45.6 %copy-start.3 = (f32[128,128]{1,0:T(8,128)S(1)}, f32[128,128]{1,0:T(8,128)}, u32[]{:S(2)}) copy-start(f32[128,128]{1,0:T(8,128)} %param.11) | copy-start | bytes 196612
  7.9 53.5 %copy-start.4 = (f32[2,8,24]{2,1,0:T(8,128)S(1)}, f32[2,8,24]{2,1,0:T(8,128)}, u32[]{:S(2)}) copy-start(f32[2,8,24]{2,1,0:T(8,128)} %param.10) | copy-start | bytes 4612
  7.9 117.8 %all-to-all-start = ((bf16[128,64,128]{2,1,0:T(8,128)(2,1)}), bf16[128,64,128]{2,1,0:T(8,128)(2,1)S(1)}, u32[]{:S(2)}, u32[]{:S(2)}) async-start(bf16[128,64,128]{2,1,0:T(8,128)(2,1)} %get-tuple-element.10), calls=%async_computation | async-start | bytes 4194304 | tf_op jit(solution)/shard_map/all_to_all | solution.py:308
  29.8 3.6 %collective-permute-start = (f32[8,128]{1,0:T(8,128)S(1)}, f32[8,128]{1,0:T(8,128)S(1)}, u32[]{:S(2)}, u32[]{:S(2)}) collective-permute-start(f32[8,128]{1,0:T(8,128)S(1)} %broadcast_in_dim.3), channel_id=1, source_target_pairs={{0,64},{64,0},{128,192},{192,128},{256,320},{320,256},{384,448},{4... | collective-permute-start | bytes 12296 | tf_op jit(solution)/shard_map/ppermute | solution.py:338
  33.4 4.6 %collective-permute-start.1 = (f32[8,128]{1,0:T(8,128)S(1)}, f32[8,128]{1,0:T(8,128)S(1)}, u32[]{:S(2)}, u32[]{:S(2)}) collective-permute-start(f32[8,128]{1,0:T(8,128)S(1)} %broadcast_maximum_fusion), channel_id=1, source_target_pairs={{0,128},{64,192},{128,0},{192,64},{256,384},{320,448},{384,256},{4... | collective-permute-start | bytes 12296 | tf_op jit(solution)/shard_map/ppermute | solution.py:338
  38.1 6.1 %collective-permute-start.2 = (f32[8,128]{1,0:T(8,128)S(1)}, f32[8,128]{1,0:T(8,128)S(1)}, u32[]{:S(2)}, u32[]{:S(2)}) collective-permute-start(f32[8,128]{1,0:T(8,128)S(1)} %fusion.23), channel_id=1, source_target_pairs={{0,256},{64,320},{128,384},{192,448},{256,0},{320,64},{384,128},{4... | collective-permute-start | bytes 12296 | tf_op jit(solution)/shard_map/ppermute | solution.py:338
  44.2 70.4 %collective-permute-start.5 = (f32[8,128]{1,0:T(8,128)S(1)}, f32[8,128]{1,0:T(8,128)S(1)}, u32[]{:S(2)}, u32[]{:S(2)}) collective-permute-start(f32[8,128]{1,0:T(8,128)S(1)} %max.26), channel_id=1, source_target_pairs={{0,12},{4,8},{8,4},{12,0},{16,28},{20,24},{24,20},{28,16},{32,44},... | collective-permute-start | bytes 12296 | tf_op jit(solution)/shard_map/ppermute | solution.py:342
  48.9 70.3 %collective-permute-start.4 = (f32[8,128]{1,0:T(8,128)S(1)}, f32[8,128]{1,0:T(8,128)S(1)}, u32[]{:S(2)}, u32[]{:S(2)}) collective-permute-start(f32[8,128]{1,0:T(8,128)S(1)} %max.26), channel_id=1, source_target_pairs={{0,8},{4,12},{8,0},{12,4},{16,24},{20,28},{24,16},{28,20},{32,40},... | collective-permute-start | bytes 12296 | tf_op jit(solution)/shard_map/ppermute | solution.py:342
  50.9 68.4 %collective-permute-start.3 = (f32[8,128]{1,0:T(8,128)S(1)}, f32[8,128]{1,0:T(8,128)S(1)}, u32[]{:S(2)}, u32[]{:S(2)}) collective-permute-start(f32[8,128]{1,0:T(8,128)S(1)} %max.26), channel_id=1, source_target_pairs={{0,4},{4,0},{8,12},{12,8},{16,20},{20,16},{24,28},{28,24},{32,36},... | collective-permute-start | bytes 12296 | tf_op jit(solution)/shard_map/ppermute | solution.py:342
  53.6 66.3 %collective-permute-start.11 = (f32[128,128]{0,1:T(8,128)S(1)}, f32[128,128]{0,1:T(8,128)S(1)}, u32[]{:S(2)}, u32[]{:S(2)}) collective-permute-start(f32[128,128]{0,1:T(8,128)S(1)} %copy.19), channel_id=1, source_target_pairs={{0,1},{1,2},{2,3},{3,0},{4,5},{5,6},{6,7},{7,4},{8,9},{9,10},{10,1... | collective-permute-start | bytes 196616 | tf_op jit(solution)/shard_map/ppermute | solution.py:347
  56.8 63.1 %collective-permute-start.10 = (f32[128,128]{0,1:T(8,128)S(1)}, f32[128,128]{0,1:T(8,128)S(1)}, u32[]{:S(2)}, u32[]{:S(2)}) collective-permute-start(f32[128,128]{0,1:T(8,128)S(1)} %copy.19), channel_id=1, source_target_pairs={{0,2},{1,3},{2,0},{3,1},{4,6},{5,7},{6,4},{7,5},{8,10},{9,11},{10,... | collective-permute-start | bytes 196616 | tf_op jit(solution)/shard_map/ppermute | solution.py:347
  114.6 5.9 %collective-permute-start.9 = (f32[128,128]{0,1:T(8,128)S(1)}, f32[128,128]{0,1:T(8,128)S(1)}, u32[]{:S(2)}, u32[]{:S(2)}) collective-permute-start(f32[128,128]{0,1:T(8,128)S(1)} %copy.19), channel_id=1, source_target_pairs={{0,3},{1,0},{2,1},{3,2},{4,7},{5,4},{6,5},{7,6},{8,11},{9,8},{10,9... | collective-permute-start | bytes 196616 | tf_op jit(solution)/shard_map/ppermute | solution.py:347
  128.8 13.7 %all-to-all-start.1 = ((f32[32,1,384]{2,1,0:T(1,128)}), f32[32,1,384]{2,1,0:T(1,128)S(1)}, u32[]{:S(2)}, u32[]{:S(2)}) async-start(f32[32,1,384]{2,1,0:T(1,128)} %density.1), calls=%async_computation.1 | async-start | bytes 98304 | tf_op jit(solution)/shard_map/all_to_all | solution.py:308
  143.8 7.6 %collective-permute-start.12 = (f32[6,2,28]{2,1,0:T(2,128)S(1)}, f32[6,2,28]{2,1,0:T(2,128)S(1)}, u32[]{:S(2)}, u32[]{:S(2)}) collective-permute-start(f32[6,2,28]{2,1,0:T(2,128)S(1)} %get-tuple-element.30), channel_id=1, source_target_pairs={{0,4},{4,8},{8,12},{12,16},{16,20},{20,24},{24,28},{28,32},{32,36}... | collective-permute-start | bytes 4040 | tf_op jit(solution)/shard_map/ppermute | solution.py:32
  148.8 5.0 %collective-permute-start.13 = (f32[6,2,28]{2,1,0:T(2,128)S(1)}, f32[6,2,28]{2,1,0:T(2,128)S(1)}, u32[]{:S(2)}, u32[]{:S(2)}) collective-permute-start(f32[6,2,28]{2,1,0:T(2,128)S(1)} %get-tuple-element.31), channel_id=1, source_target_pairs={{4,0},{8,4},{12,8},{16,12},{20,16},{24,20},{28,24},{32,28},{36,32}... | collective-permute-start | bytes 4040 | tf_op jit(solution)/shard_map/ppermute | solution.py:34
  157.8 114.8 %all-to-all-start.2 = ((f16[128,64,128]{2,1,0:T(8,128)(2,1)}), f16[128,64,128]{2,1,0:T(8,128)(2,1)S(1)}, u32[]{:S(2)}, u32[]{:S(2)}) async-start(f16[128,64,128]{2,1,0:T(8,128)(2,1)} %bitcast.22), calls=%async_computation.2 | async-start | bytes 4194304 | tf_op jit(solution)/shard_map/all_to_all | solution.py:308
  173.3 89.2 %collective-permute-start.8 = (f32[8,128]{1,0:T(8,128)S(1)}, f32[8,128]{1,0:T(8,128)S(1)}, u32[]{:S(2)}, u32[]{:S(2)}) collective-permute-start(f32[8,128]{1,0:T(8,128)S(1)} %get-tuple-element.21), channel_id=1, source_target_pairs={{0,48},{4,52},{8,56},{12,60},{16,32},{20,36},{24,40},{28,44},{32,1... | collective-permute-start | bytes 12296 | tf_op jit(solution)/shard_map/ppermute | solution.py:382
  180.5 92.0 %collective-permute-start.7 = (f32[8,128]{1,0:T(8,128)S(1)}, f32[8,128]{1,0:T(8,128)S(1)}, u32[]{:S(2)}, u32[]{:S(2)}) collective-permute-start(f32[8,128]{1,0:T(8,128)S(1)} %get-tuple-element.21), channel_id=1, source_target_pairs={{0,32},{4,36},{8,40},{12,44},{16,48},{20,52},{24,56},{28,60},{32,0... | collective-permute-start | bytes 12296 | tf_op jit(solution)/shard_map/ppermute | solution.py:382
  187.5 85.1 %collective-permute-start.6 = (f32[8,128]{1,0:T(8,128)S(1)}, f32[8,128]{1,0:T(8,128)S(1)}, u32[]{:S(2)}, u32[]{:S(2)}) collective-permute-start(f32[8,128]{1,0:T(8,128)S(1)} %get-tuple-element.21), channel_id=1, source_target_pairs={{0,16},{4,20},{8,24},{12,28},{16,0},{20,4},{24,8},{28,12},{32,48},... | collective-permute-start | bytes 12296 | tf_op jit(solution)/shard_map/ppermute | solution.py:382
  272.6 0.7 copy-start.1
  272.6 0.7 copy-start.2
  288.4 27.2 %all-to-all-start.4 = ((f32[16,16,128]{2,1,0:T(8,128)}), f32[16,16,128]{2,1,0:T(8,128)S(1)}, u32[]{:S(2)}, u32[]{:S(2)}) async-start(f32[16,16,128]{2,1,0:T(8,128)} %bitcast.10), calls=%async_computation.4 | async-start | bytes 262144 | tf_op jit(solution)/shard_map/all_to_all | solution.py:308
  295.9 10.9 %collective-permute-start.14 = (s16[1040,128]{1,0:T(8,128)(2,1)S(1)}, s16[1040,128]{1,0:T(8,128)(2,1)S(1)}, u32[]{:S(2)}, u32[]{:S(2)}) collective-permute-start(s16[1040,128]{1,0:T(8,128)(2,1)S(1)} %get-tuple-element.12), channel_id=1, source_target_pairs={{0,1},{1,2},{2,3},{3,0},{4,5},{5,6},{6,7},{7,4},{8,9},{9,10},{10,1... | collective-permute-start | bytes 798728 | tf_op jit(solution)/shard_map/ppermute | solution.py:403
  298.1 13.2 %collective-permute-start.15 = (s16[1040,128]{1,0:T(8,128)(2,1)S(1)}, s16[1040,128]{1,0:T(8,128)(2,1)S(1)}, u32[]{:S(2)}, u32[]{:S(2)}) collective-permute-start(s16[1040,128]{1,0:T(8,128)(2,1)S(1)} %get-tuple-element.13), channel_id=1, source_target_pairs={{0,2},{1,3},{2,0},{3,1},{4,6},{5,7},{6,4},{7,5},{8,10},{9,11},{10,... | collective-permute-start | bytes 798728 | tf_op jit(solution)/shard_map/ppermute | solution.py:403
  301.8 12.7 %collective-permute-start.16 = (s16[1040,128]{1,0:T(8,128)(2,1)S(1)}, s16[1040,128]{1,0:T(8,128)(2,1)S(1)}, u32[]{:S(2)}, u32[]{:S(2)}) collective-permute-start(s16[1040,128]{1,0:T(8,128)(2,1)S(1)} %get-tuple-element.14), channel_id=1, source_target_pairs={{0,3},{1,0},{2,1},{3,2},{4,7},{5,4},{6,5},{7,6},{8,11},{9,8},{10,9... | collective-permute-start | bytes 798728 | tf_op jit(solution)/shard_map/ppermute | solution.py:403
